TPU v7x, 128 devices: a whole 4x4x4 slice. The times are simulated.
128 devices in a mesh: dp: 8 (over x, core), seq: 16 (over z, y).
Axes of the slice: x: 4, y: 4, z: 4, core: 2. Of those that a mesh axis runs over, the one named last changes fastest.
Arguments:
- text_rows: bfloat16 [16384, 8192], P(('dp', 'seq')), may hold values from -6 to 6
- image_rows: bfloat16 [32, 256, 8192], P('dp', 'seq'), may hold values from -6 to 6
- tile_group: int32 [32], replicated, may hold values from 0 to 7, as said below
- tile_offset: int32 [32], replicated, may hold values from 0 to 1792, as said below
- seq_len: int32 [8], P('dp'), may hold values from 1024 to 2048, as said below
- doc_ids: int32 [8, 2048], P('dp'), may hold values from 0 to 7, never falling along the last dimension, each value on 1 to 512 neighbouring positions
- norm_gain: float32 [8192], replicated, may hold values from 0.1 to 1.9
- q_weight: bfloat16 [8192, 8192], P(None, 'seq'), may hold values from -0.0625 to 0.0625
- k_weight: bfloat16 [8192, 1024], P(None, 'seq'), may hold values from -0.0625 to 0.0625
- v_weight: bfloat16 [8192, 1024], P(None, 'seq'), may hold values from -0.0625 to 0.0625
- q_bias: float32 [8192], P('seq'), may hold values from -3 to 3
- k_bias: float32 [1024], P('seq'), may hold values from -40 to 40
- v_bias: float32 [1024], P('seq'), may hold values from -3 to 3
Outputs:
- attention: bfloat16 [16384, 8192], P('dp', 'seq')
Inputs may be any that keep to these rules, and one draw needn't show every extreme that they name: `tile_group`: the 4 tiles r * 4 to r * 4 + 3 of each r < 8 go to distinct packed sequences; one packed sequence takes exactly 7 tiles and none takes more. `tile_offset`: the tiles of one packed sequence lie back to back in increasing tile order and end at or before its seq_len. `seq_len`: some packed sequence uses all 2048 positions. `doc_ids`: document ids never fall along a sequence and no document is longer than 512 positions.
All inputs are finite; a program needn't handle non-finite values.
Results may differ from a plain program's by a relative error of at most 0.003.
The roundings to bfloat16 on the way count: a program that leaves them out, or rounds other values in their place, can miss the bound.
Values may be sent and summed in bfloat16 or wider, within the bound.
No kernel may reach another device: no remote copies, remote signals or barrier semaphores. Data moves between devices by JAX's collectives and lax.ppermute only.
A program may use at most 128 MiB of HBM per device.

v0:
```python
import math

import jax
import jax.numpy as jnp
from jax import lax
from jax.experimental import pallas as pl
from jax.experimental.pallas import tpu as pltpu
from jax.sharding import Mesh, PartitionSpec as P

TR = 256
UNIT = 16
HD = 128
LENGTH = 2048
CAPACITY = 36
ROWS = CAPACITY * UNIT
WINDOW = 512
THETA = 1000000.0
NEGATIVE = -1e30
EPSILON = 1e-06


def shifted(block, axis, step):
    count = lax.axis_size(axis)
    return lax.ppermute(block, axis, [(low, (low + step) % count) for low in range(count)])


def rms_norm(row_block, gain):
    float_rows = row_block.astype(jnp.float32)
    inv_rms = lax.rsqrt(jnp.mean(float_rows * float_rows, axis=-1, keepdims=True) + EPSILON)
    return (float_rows * inv_rms * gain).astype(jnp.bfloat16)


def norm_text_kernel(rows_ref, gain_ref, out_ref):
    out_ref[...] = rms_norm(rows_ref[...], gain_ref[...])


def norm_text(rows, gain):
    count, features = rows.shape
    step = 2 * UNIT
    return pl.pallas_call(
        norm_text_kernel,
        grid=(count // step,),
        in_specs=[
            pl.BlockSpec((step, features), lambda i: (i, 0)),
            pl.BlockSpec((1, features), lambda i: (0, 0)),
        ],
        out_specs=pl.BlockSpec((step, features), lambda i: (i, 0)),
        out_shape=jax.ShapeDtypeStruct(rows.shape, jnp.bfloat16),
        name="norm_text",
    )(rows, gain)


def norm_image_kernel(chosen_ref, rows_ref, gain_ref, out_ref):
    out_ref[0] = rms_norm(rows_ref[0], gain_ref[...])


def norm_image(pieces, gain, chosen):
    _, piece_rows, features = pieces.shape
    groups = chosen.shape[0]
    return pl.pallas_call(
        norm_image_kernel,
        grid_spec=pltpu.PrefetchScalarGridSpec(
            num_scalar_prefetch=1,
            grid=(groups,),
            in_specs=[
                pl.BlockSpec((1, piece_rows, features), lambda i, chosen: (chosen[i], 0, 0)),
                pl.BlockSpec((1, features), lambda i, chosen: (0, 0)),
            ],
            out_specs=pl.BlockSpec((1, piece_rows, features), lambda i, chosen: (i, 0, 0)),
        ),
        out_shape=jax.ShapeDtypeStruct((groups, piece_rows, features), jnp.bfloat16),
        name="norm_image",
    )(chosen, pieces, gain)


def pick_kernel(chosen_ref, rows_ref, out_ref):
    out_ref[...] = rows_ref[...]


def pick_slots(pieces, chosen):
    _, piece_rows, features = pieces.shape
    count = chosen.shape[0]
    return pl.pallas_call(
        pick_kernel,
        grid_spec=pltpu.PrefetchScalarGridSpec(
            num_scalar_prefetch=1,
            grid=(count,),
            in_specs=[pl.BlockSpec((1, piece_rows, features), lambda i, chosen: (chosen[i], 0, 0))],
            out_specs=pl.BlockSpec((1, piece_rows, features), lambda i, chosen: (i, 0, 0)),
        ),
        out_shape=jax.ShapeDtypeStruct((count, piece_rows, features), jnp.bfloat16),
        name="pick_slots",
    )(chosen, pieces)


def rotated(values, cosine, sine):
    return values * cosine + pltpu.roll(values, HD // 2, 1) * sine


def project_first_kernel(
    place_ref,
    t0, t1, t2a, t2b, t3,
    i0, i1, i2a, i2b, i3,
    weight_ref, kv_bias_ref, q_bias_ref, cos_ref, sin_ref,
    out_ref, kv_ref, compact_ref,
    rows_ref, weight_buf, sum_ref, sems, weight_sems, copy_sem,
):
    slots = weight_buf.shape[0]
    chunks = 8
    depth = weight_buf.shape[1]
    width = weight_buf.shape[2]
    target = place_ref[65]

    def weight_copies(step, slot):
        kv = [
            pltpu.make_async_copy(
                weight_ref.at[pl.ds((step * 4 + y) * depth, depth), pl.ds(width, HD)],
                weight_buf.at[slot, :, pl.ds(y * HD, HD)],
                weight_sems.at[slot, y],
            )
            for y in range(4)
        ]
        query = pltpu.make_async_copy(
            weight_ref.at[pl.ds(((step - chunks) * 4 + target) * depth, depth), pl.ds(0, width)],
            weight_buf.at[slot],
            weight_sems.at[slot, 0],
        )
        return kv, query

    def start(step):
        slot = step % slots

        @pl.when(step < chunks)
        def _():
            for copy in weight_copies(step, slot)[0]:
                copy.start()

        @pl.when((step >= chunks) & (step < 2 * chunks))
        def _():
            weight_copies(step, slot)[1].start()

    for step in range(slots - 1):
        start(jnp.int32(step))

    total = place_ref[64]
    for unit in range(24, CAPACITY):
        @pl.when(unit >= total)
        def _(unit=unit):
            rows_ref[pl.ds(UNIT * unit, UNIT), :] = jnp.zeros(
                (UNIT, rows_ref.shape[1]), jnp.bfloat16
            )

    def unit_copy(index):
        delta, slot = index % 32 // 8, index % 8
        if index < 32:
            source = (t0, t1, t2a if slot < 4 else t2b, t3)[delta]
            slot = slot % 4 if delta == 2 else slot
            source = source.at[pl.ds(UNIT * slot, UNIT), :]
        else:
            source = (i0, i1, i2a if slot < 4 else i2b, i3)[delta]
            slot = slot % 4 if delta == 2 else slot
            source = source.at[slot]
        row = pl.multiple_of(UNIT * jnp.maximum(place_ref[index], 0), UNIT)
        return pltpu.make_async_copy(source, rows_ref.at[pl.ds(row, UNIT), :], sems.at[index])

    used = [index for index in range(64) if index < 32 or index % 8 < 7]
    for index in used:
        @pl.when(place_ref[index] >= 0)
        def _(index=index):
            unit_copy(index).start()
    for index in used:
        @pl.when(place_ref[index] >= 0)
        def _(index=index):
            unit_copy(index).wait()
    copy_out = pltpu.make_async_copy(rows_ref, compact_ref, copy_sem)
    copy_out.start()

    def product(step, part):
        slot = step % slots
        lanes = pl.ds(pl.multiple_of(part * depth, depth), depth)
        value = jnp.dot(
            rows_ref[:, lanes], weight_buf[slot], preferred_element_type=jnp.float32
        )

        @pl.when(part == 0)
        def _():
            sum_ref[...] = value

        @pl.when(part > 0)
        def _():
            sum_ref[...] += value

    def kv_step(step, carry):
        start(step + slots - 1)
        for copy in weight_copies(step, step % slots)[0]:
            copy.wait()
        product(step, step)
        return carry

    lax.fori_loop(0, chunks, kv_step, 0)
    cosine = cos_ref[...]
    sine = sin_ref[...]
    in_low = lax.broadcasted_iota(jnp.int32, cosine.shape, 1) < HD // 2
    half = HD // 2
    for head in range(2):
        low_lanes = slice(2 * head * HD, (2 * head + 1) * HD)
        high_lanes = slice((2 * head + 1) * HD, (2 * head + 2) * HD)
        low = sum_ref[:, low_lanes] + kv_bias_ref[:, low_lanes]
        high = sum_ref[:, high_lanes] + kv_bias_ref[:, high_lanes]
        key = jnp.where(in_low, low, pltpu.roll(high, half, 1))
        value = jnp.where(in_low, pltpu.roll(low, half, 1), high)
        kv_ref[head, :, :HD] = rotated(key, cosine, sine).astype(jnp.bfloat16)
        kv_ref[head, :, HD:] = value.astype(jnp.bfloat16)

    def query_step(step, carry):
        start(step + slots - 1)
        weight_copies(step, step % slots)[1].wait()
        product(step, step - chunks)
        return carry

    lax.fori_loop(chunks, 2 * chunks, query_step, 0)
    for head in range(width // HD):
        lanes = slice(head * HD, (head + 1) * HD)
        out_ref[:, lanes] = rotated(
            sum_ref[:, lanes] + q_bias_ref[:, lanes], cos_ref[...], sin_ref[...]
        ).astype(jnp.bfloat16)
    out_ref[:, width:] = kv_ref[target // 2]
    copy_out.wait()


def cost(width, features):
    return pl.CostEstimate(
        flops=2 * ROWS * features * width,
        transcendentals=0,
        bytes_accessed=2 * features * (width + ROWS),
    )


def project_first(place, texts, images, weights, kv_bias, q_bias, cosine, sine):
    width = q_bias.shape[1]
    features = texts[0].shape[1]
    depth = features // 8
    any_spec = pl.BlockSpec(memory_space=pltpu.HBM)
    whole = lambda shape: pl.BlockSpec(shape, lambda i, place: (0,) * len(shape))
    return pl.pallas_call(
        project_first_kernel,
        grid_spec=pltpu.PrefetchScalarGridSpec(
            num_scalar_prefetch=1,
            grid=(1,),
            in_specs=[any_spec] * 11
            + [whole((1, width)), whole((1, width)), whole((ROWS, HD)), whole((ROWS, HD))],
            out_specs=(
                whole((ROWS, width + 2 * HD)),
                whole((2, ROWS, 2 * HD)),
                any_spec,
            ),
            scratch_shapes=[
                pltpu.VMEM((ROWS, features), jnp.bfloat16),
                pltpu.VMEM((4, depth, width), jnp.bfloat16),
                pltpu.VMEM((ROWS, width), jnp.float32),
                pltpu.SemaphoreType.DMA((64,)),
                pltpu.SemaphoreType.DMA((4, 4)),
                pltpu.SemaphoreType.DMA,
            ],
        ),
        out_shape=(
            jax.ShapeDtypeStruct((ROWS, width + 2 * HD), jnp.bfloat16),
            jax.ShapeDtypeStruct((2, ROWS, 2 * HD), jnp.bfloat16),
            jax.ShapeDtypeStruct((ROWS, features), jnp.bfloat16),
        ),
        compiler_params=pltpu.CompilerParams(vmem_limit_bytes=40 << 20),
        cost_estimate=cost(2 * width, features),
        name="project_first",
    )(place, *texts, *images, weights, kv_bias, q_bias, cosine, sine)


def project_next_kernel(
    target_ref, rows_ref, weight_ref, kv_ref, bias_ref, cos_ref, sin_ref, out_ref, sum_ref
):
    part = pl.program_id(0)
    width = weight_ref.shape[1]
    value = jnp.dot(rows_ref[...], weight_ref[...], preferred_element_type=jnp.float32)

    @pl.when(part == 0)
    def _():
        sum_ref[...] = value

    @pl.when(part > 0)
    def _():
        sum_ref[...] += value

    @pl.when(part == pl.num_programs(0) - 1)
    def _():
        for head in range(width // HD):
            lanes = slice(head * HD, (head + 1) * HD)
            out_ref[:, lanes] = rotated(
                sum_ref[:, lanes] + bias_ref[:, lanes], cos_ref[...], sin_ref[...]
            ).astype(jnp.bfloat16)
        out_ref[:, width:] = kv_ref[0]


def project_next(target, compact, weights, kv, q_bias, cosine, sine):
    width = q_bias.shape[1]
    features = compact.shape[1]
    parts = 8
    depth = features // parts
    whole = lambda shape: pl.BlockSpec(shape, lambda k, target: (0,) * len(shape))
    return pl.pallas_call(
        project_next_kernel,
        grid_spec=pltpu.PrefetchScalarGridSpec(
            num_scalar_prefetch=1,
            grid=(parts,),
            in_specs=[
                pl.BlockSpec((ROWS, depth), lambda k, target: (0, k)),
                pl.BlockSpec((depth, width), lambda k, target: (k * 4 + target[0], 0)),
                pl.BlockSpec((1, ROWS, 2 * HD), lambda k, target: (target[0] // 2, 0, 0)),
                whole((1, width)),
                whole((ROWS, HD)),
                whole((ROWS, HD)),
            ],
            out_specs=whole((ROWS, width + 2 * HD)),
            scratch_shapes=[pltpu.VMEM((ROWS, width), jnp.float32)],
        ),
        out_shape=jax.ShapeDtypeStruct((ROWS, width + 2 * HD), jnp.bfloat16),
        compiler_params=pltpu.CompilerParams(vmem_limit_bytes=32 << 20),
        cost_estimate=cost(width, features),
        name="project_next",
    )(
        target, pltpu.with_memory_space_constraint(compact, pltpu.HBM), weights, kv, q_bias,
        cosine, sine,
    )


def attend_kernel(
    info_ref, text_ref, part0, part1, part2, part3, out_ref, merged_ref, run_ref, mask_ref
):
    parts = (part0, part1, part2, part3)
    step = pl.program_id(0)
    block = out_ref.shape[0]
    width = part0.shape[1]
    mine = info_ref[11]
    run_start = info_ref[8]
    run_end = info_ref[9]
    used = info_ref[10]
    first_unit = (run_start + UNIT - 1) // UNIT
    lag = first_unit * UNIT - run_start

    @pl.when(step == 0)
    def _():
        merged_ref[0:WINDOW, :] = jnp.zeros((WINDOW, width), jnp.bfloat16)
        run_ref[0:128, :] = jnp.zeros((128, width), jnp.bfloat16)
        run_ref[128 + 7 * TR:, :] = jnp.zeros((run_ref.shape[0] - 128 - 7 * TR, width), jnp.bfloat16)

        def tile_step(tile, carry):
            for piece in range(16):
                level, delta = piece // 4, piece % 4
                member = (mine + delta) % 4
                source = pl.multiple_of(tile * 64 + level * UNIT, UNIT)
                target = pl.multiple_of(128 + tile * TR + (4 * level + member) * UNIT, UNIT)
                run_ref[pl.ds(target, UNIT), :] = parts[delta][pl.ds(source, UNIT), :]
            return carry

        lax.fori_loop(0, (run_end - run_start) // TR, tile_step, 0)

        def clear_step(tile, carry):
            target = pl.multiple_of(128 + tile * TR, TR // 2)
            run_ref[pl.ds(target, TR), :] = jnp.zeros((TR, width), jnp.bfloat16)
            return carry

        lax.fori_loop((run_end - run_start) // TR, 7, clear_step, 0)

        def block_step(row, carry):
            for delta in range(4):
                number = row * 4 + (mine + delta) % 4
                begin = number * 128
                for unit in range(8):
                    source = pl.multiple_of(text_ref[number * 8 + unit] * UNIT, UNIT)
                    target = pl.multiple_of(WINDOW + begin + unit * UNIT, UNIT)
                    merged_ref[pl.ds(target, UNIT), :] = parts[delta][pl.ds(source, UNIT), :]

                @pl.when((begin < run_end) & (begin + 128 > run_start))
                def _():
                    origin = pl.multiple_of(128 + UNIT * (8 * number - first_unit), UNIT)
                    window = run_ref[pl.ds(origin, 256), :]
                    place = lax.broadcasted_iota(jnp.int32, (128, 256), 0)
                    taken = lax.broadcasted_iota(jnp.int32, (128, 256), 1)
                    pick = jnp.where(taken == place + lag, 1.0, 0.0).astype(jnp.bfloat16)
                    moved = jnp.dot(pick, window, preferred_element_type=jnp.float32)
                    here = pl.ds(pl.multiple_of(WINDOW + begin, 128), 128)
                    old = merged_ref[here, :].astype(jnp.float32)
                    position = begin + lax.broadcasted_iota(jnp.int32, old.shape, 0)
                    covered = (position >= run_start) & (position < run_end)
                    merged_ref[here, :] = jnp.where(covered, moved, old).astype(jnp.bfloat16)
            return carry

        lax.fori_loop(0, 4, block_step, 0)

    base = pl.multiple_of(step * block, block)
    span = block + WINDOW
    position = base + lax.broadcasted_iota(jnp.int32, (block, 1), 0)
    doc_start = jnp.zeros((block, 1), jnp.int32)
    for doc in range(1, 8):
        doc_start = jnp.where(position >= info_ref[doc], info_ref[doc], doc_start)
    other = base - WINDOW + lax.broadcasted_iota(jnp.int32, (block, span), 1)
    allowed = (other >= doc_start) & (other <= position) & (other < used)
    mask_ref[...] = jnp.where(allowed, 0.0, NEGATIVE)
    queries = pl.ds(pl.multiple_of(WINDOW + base, block), block)
    keys = merged_ref[pl.ds(base, span), 4 * HD:5 * HD]
    values = merged_ref[pl.ds(base, span), 5 * HD:6 * HD]
    factor = HD ** (-0.5) * math.log2(math.e)
    for head in range(4):
        lanes = slice(head * HD, (head + 1) * HD)
        scores = lax.dot_general(
            merged_ref[queries, lanes], keys, (((1,), (1,)), ((), ())),
            preferred_element_type=jnp.float32,
        ) + mask_ref[...]
        peak = jnp.max(scores, axis=-1, keepdims=True)
        exponent = jnp.exp2((scores - peak) * factor)
        inverse = 1.0 / jnp.sum(exponent, axis=-1, keepdims=True)
        probs = (exponent * inverse).astype(jnp.bfloat16)
        mixed = jnp.dot(probs, values, preferred_element_type=jnp.float32)
        out_ref[:, lanes] = jnp.where(position < used, mixed, 0.0).astype(jnp.bfloat16)


def attend(info, text_index, parts):
    block = 256
    shape = parts[0].shape
    width = shape[1]
    return pl.pallas_call(
        attend_kernel,
        grid_spec=pltpu.PrefetchScalarGridSpec(
            num_scalar_prefetch=2,
            grid=(LENGTH // block,),
            in_specs=[pl.BlockSpec(shape, lambda i, a, b: (0, 0))] * 4,
            out_specs=pl.BlockSpec((block, 4 * HD), lambda i, a, b: (i, 0)),
            scratch_shapes=[
                pltpu.VMEM((WINDOW + LENGTH, width), jnp.bfloat16),
                pltpu.VMEM((128 + 7 * TR + 384, width), jnp.bfloat16),
                pltpu.VMEM((block, block + WINDOW), jnp.float32),
            ],
        ),
        out_shape=jax.ShapeDtypeStruct((LENGTH, 4 * HD), jnp.bfloat16),
        compiler_params=pltpu.CompilerParams(vmem_limit_bytes=48 << 20),
        name="attend",
    )(info, text_index, *parts)


def tables(tile_group, tile_offset, seq_len, doc_ids, group, z, y):
    mine = tile_group == group
    present = jnp.any(mine.reshape(8, 4), axis=1)
    count = jnp.sum(mine.astype(jnp.int32))
    run_start = jnp.where(count > 0, jnp.min(jnp.where(mine, tile_offset, LENGTH)), 0)
    run_end = run_start + TR * count
    low_unit = (run_start + UNIT - 1) // UNIT
    high_unit = run_end // UNIT
    eight = jnp.arange(8, dtype=jnp.int32)
    rank = jnp.sum((present[None, :] & (eight[None, :] < eight[:, None])).astype(jnp.int32), axis=1)
    order = jnp.arange(32, dtype=jnp.int32)
    four = jnp.arange(4, dtype=jnp.int32)
    unit_of = 8 * (4 * (order[None, :] // 8) + four[:, None]) + order[None, :] % 8
    before = jnp.sum((unit_of < low_unit).astype(jnp.int32), axis=1)
    hidden = jnp.sum((unit_of < high_unit).astype(jnp.int32), axis=1) - before
    held = (unit_of < low_unit) | (unit_of >= high_unit)
    compact = 4 * count + order[None, :] - jnp.where(unit_of >= high_unit, hidden[:, None], 0)
    compact = jnp.where(held, compact, -1)
    text_index = jnp.maximum(compact, 0).reshape(4, 4, 8).transpose(1, 0, 2).reshape(-1)
    my_before = lax.dynamic_index_in_dim(before, y, 0, keepdims=False)
    my_hidden = lax.dynamic_index_in_dim(hidden, y, 0, keepdims=False)
    member = (z + four) % 4
    my_compact = lax.dynamic_index_in_dim(compact, y, 0, keepdims=False).reshape(4, 8)
    text_place = jnp.take(my_compact, member, axis=0).reshape(-1)
    image_place = jnp.where(eight[None, :] < count, 4 * eight[None, :] + member[:, None], -1)
    image_place = image_place.reshape(-1)
    total = 4 * count + 32 - my_hidden
    place = jnp.concatenate([text_place, image_place, total[None], (y[None] + 2) % 4])
    place = place.astype(jnp.int32)
    is_slot = present[None, :] & (rank[None, :] == eight[:7, None])
    slots = jnp.sum(jnp.where(is_slot, eight[None, :], 0), axis=1).astype(jnp.int32)
    number = jnp.arange(ROWS, dtype=jnp.int32) // UNIT
    inner = jnp.arange(ROWS, dtype=jnp.int32) % UNIT
    image_at = run_start + TR * (number // 4) + UNIT * (4 * (number % 4) + y)
    text_number = number - 4 * count
    text_number = jnp.clip(text_number + jnp.where(text_number >= my_before, my_hidden, 0), 0, 31)
    text_at = 128 * (4 * (text_number // 8) + y) + UNIT * (text_number % 8)
    position = jnp.where(number < 4 * count, image_at, text_at) + inner
    starts = jnp.sum((doc_ids[0][None, :] < eight[:, None]).astype(jnp.int32), axis=1)
    doc_start = jnp.max(
        jnp.where(starts[None, :] <= position[:, None], starts[None, :], 0), axis=1
    )
    in_doc = position - doc_start
    info = jnp.concatenate([starts, run_start[None], run_end[None], seq_len, y[None]])
    return place, slots, text_index, info.astype(jnp.int32), in_doc


def one_device(
    text_rows, image_rows, tile_group, tile_offset, seq_len, doc_ids, norm_gain,
    q_weight, k_weight, v_weight, q_bias, k_bias, v_bias,
):
    group = lax.axis_index("x") * 2 + lax.axis_index("c")
    z = lax.axis_index("z")
    y = lax.axis_index("y")
    depth = q_weight.shape[0] // 8
    gain = norm_gain.reshape(1, -1)

    def own_part(weight):
        return lax.dynamic_slice_in_dim(weight, group * depth, depth, 0)

    weight_part = jnp.concatenate(
        [own_part(q_weight), own_part(k_weight), own_part(v_weight)], axis=1
    )
    weights = lax.all_gather(weight_part, ("x", "c", "y"), axis=0, tiled=True)

    t0 = norm_text(text_rows, gain)
    t3 = shifted(t0, "z", 1)
    t1 = shifted(t0, "z", -1)

    place, slots, text_index, info, in_doc = tables(
        tile_group, tile_offset, seq_len, doc_ids, group, z, y
    )
    row_groups = lax.dynamic_slice_in_dim(tile_group, group * 4, 4)
    matches = row_groups[None, :] == jnp.arange(8, dtype=jnp.int32)[:, None]
    chosen = jnp.sum(jnp.where(matches, jnp.arange(4, dtype=jnp.int32)[None, :], 0), axis=1)
    image_rows, t0 = lax.optimization_barrier((image_rows, t0))
    outgoing = norm_image(image_rows, gain, chosen.astype(jnp.int32))
    arrived = lax.all_to_all(outgoing, ("x", "c"), split_axis=0, concat_axis=0, tiled=True)
    i0 = pick_slots(arrived, slots)
    i3 = shifted(i0, "z", 1)
    i1 = shifted(i0, "z", -1)
    t2a = shifted(t3[:64], "z", 1)
    t2b = shifted(t1[64:], "z", -1)
    i2a = shifted(i3[:4], "z", 1)
    i2b = shifted(i1[4:], "z", -1)

    bias = jnp.concatenate([q_bias, k_bias, v_bias])
    biases = [bias, shifted(bias, "y", -1), shifted(bias, "y", 2), shifted(bias, "y", 1)]
    q_biases = [value[None, :4 * HD] for value in biases]
    kv_bias = jnp.stack([value[4 * HD:] for value in biases])
    member = jnp.arange(4, dtype=jnp.int32)[:, None, None]
    delta = jnp.arange(4, dtype=jnp.int32)[None, :, None]
    kv_bias = jnp.sum(jnp.where((y + delta) % 4 == member, kv_bias[None], 0.0), axis=1)
    kv_bias = kv_bias.reshape(1, -1)
    frequency = THETA ** (-(jnp.arange(HD // 2, dtype=jnp.float32) * 2.0) / HD)
    angles = in_doc.astype(jnp.float32)[:, None] * frequency[None, :]
    cosine = jnp.concatenate([jnp.cos(angles), jnp.cos(angles)], axis=-1)
    sine = jnp.concatenate([-jnp.sin(angles), jnp.sin(angles)], axis=-1)

    out2, kv, compact = project_first(
        place, (t0, t1, t2a, t2b, t3), (i0, i1, i2a, i2b, i3),
        weights, kv_bias, q_biases[2], cosine, sine,
    )
    part2 = shifted(out2, "y", 2)
    outs = {}
    after = kv
    for step in (1, 3, 0):
        target = (y[None] + step) % 4
        outs[step] = project_next(
            target.astype(jnp.int32), compact, weights, after, q_biases[step], cosine, sine
        )
        after, outs[step] = lax.optimization_barrier((after, outs[step]))
    part3 = shifted(outs[1], "y", 1)
    part1 = shifted(outs[3], "y", -1)
    return attend(info, text_index, (outs[0], part1, part2, part3))


def solution(mesh):
    fine = Mesh(mesh.devices.reshape(4, 2, 4, 4), ("x", "c", "z", "y"))
    dp, seq = ("x", "c"), ("z", "y")
    return jax.shard_map(
        one_device,
        mesh=fine,
        in_specs=(
            P(dp + seq, None),
            P(dp, seq, None),
            P(),
            P(),
            P(dp),
            P(dp, None),
            P(),
            P(None, seq),
            P(None, seq),
            P(None, seq),
            P(seq),
            P(seq),
            P(seq),
        ),
        out_specs=P(dp, seq),
        check_vma=False,
    )
```

profile of v0, /device:TPU:1, one launch (start us, length us, event | category | flops | bytes accessed | tf_op | source)
XLA Modules:
  0.0 292.2 jit_solution(5847312883458439636)
XLA Ops:
  6.5 1.0 constant_dynamic-slice_fusion
  7.9 1.3 constant_dynamic-slice_fusion.2
  9.2 1.3 pad_maximum_fusion
  10.5 4.4 %norm_text.1.t0 = bf16[128,8192]{1,0:T(8,128)(2,1)} custom-call(bf16[128,8192]{1,0:T(8,128)(2,1)} %rows_ref.1, f32[1,8192]{1,0:T(1,128)} %bitcast.29), custom_call_target="tpu_custom_call" | custom-call | tf_op jit(solution)/shard_map/norm_text/pallas_call | solution.py:40
  14.9 0.6 select_reduce_fusion.3.chosen_ref
  15.6 6.8 %norm_image.1 = bf16[8,16,8192]{2,1,0:T(8,128)(2,1)} custom-call(s32[8]{0:T(128)} %select_reduce_fusion.3.chosen_ref, bf16[4,16,8192]{2,1,0:T(8,128)(2,1)} %rows_ref.2, f32[1,8192]{1,0:T(1,128)} %bitcast.30), custom_call_target="tpu_custom_call" | custom-call | tf_op jit(solution)/shard_map/norm_image/pallas_call | solution.py:60
  22.4 6.1 %all-to-all-start = ((bf16[8,16,8192]{2,1,0:T(8,128)(2,1)}), bf16[8,16,8192]{2,1,0:T(8,128)(2,1)}, u32[]{:S(2)}, u32[]{:S(2)}) async-start(bf16[8,16,8192]{2,1,0:T(8,128)(2,1)} %norm_image.1), calls=%async_computation | async-start | bytes 4194304 | tf_op jit(solution)/shard_map/all_to_all | solution.py:525
  28.4 1.7 collective-permute-start.1
  30.1 2.2 collective-permute-start
  32.4 1.3 collective-permute-start.10
  33.8 0.7 select_reduce_fusion.4
  37.7 0.7 select_reduce_fusion.2.chosen_ref
  38.4 34.0 %all-to-all-done.rows_ref = bf16[8,16,8192]{2,1,0:T(8,128)(2,1)} async-done(((bf16[8,16,8192]{2,1,0:T(8,128)(2,1)}), bf16[8,16,8192]{2,1,0:T(8,128)(2,1)}, u32[]{:S(2)}, u32[]{:S(2)}) %all-to-all-start) | async-done | bytes 2097184 | tf_op jit(solution)/shard_map/all_to_all | solution.py:525
  72.4 5.0 %pick_slots.1.i0 = bf16[7,16,8192]{2,1,0:T(8,128)(2,1)} custom-call(s32[7]{0:T(128)} %select_reduce_fusion.2.chosen_ref, bf16[8,16,8192]{2,1,0:T(8,128)(2,1)} %all-to-all-done.rows_ref), custom_call_target="tpu_custom_call" | custom-call | tf_op jit(solution)/shard_map/pick_slots/pallas_call | solution.py:83
  77.4 1.3 collective-permute-start.5
  78.7 0.7 dynamic_slice.29
  79.3 0.6 dynamic_slice.24
  80.6 1.3 fusion.14
  82.1 1.5 collective-permute-start.4
  83.6 0.6 iota_compare_fusion.4
  84.3 1.3 subtract_convert_fusion
  85.6 1.1 fusion
  87.2 2.8 collective-permute-start.9
  90.0 2.3 slice.48
  92.4 2.3 slice.49
  94.7 24.8 %collective-permute-done.5.i3 = bf16[7,16,8192]{2,1,0:T(8,128)(2,1)} collective-permute-done((bf16[7,16,8192]{2,1,0:T(8,128)(2,1)}, bf16[7,16,8192]{2,1,0:T(8,128)(2,1)}, u32[]{:S(2)}, u32[]{:S(2)}) %collective-permute-start.5) | collective-permute-done | bytes 1835040 | tf_op jit(solution)/shard_map/ppermute | solution.py:24
  119.5 1.5 collective-permute-start.3
  121.0 2.3 slice.50
  124.2 2.5 collective-permute-start.8
  127.6 1.2 slice.51
  128.8 2.7 collective-permute-start.7
  131.6 10.4 %collective-permute-done.2.t2a = bf16[64,8192]{1,0:T(8,128)(2,1)} collective-permute-done((bf16[64,8192]{1,0:T(8,128)(2,1)}, bf16[64,8192]{1,0:T(8,128)(2,1)}, u32[]{:S(2)}, u32[]{:S(2)}) %collective-permute-start.2) | collective-permute-done | bytes 1048608 | tf_op jit(solution)/shard_map/ppermute | solution.py:24
  142.0 3.3 %collective-permute-done.3.t2b = bf16[64,8192]{1,0:T(8,128)(2,1)} collective-permute-done((bf16[64,8192]{1,0:T(8,128)(2,1)}, bf16[64,8192]{1,0:T(8,128)(2,1)}, u32[]{:S(2)}, u32[]{:S(2)}) %collective-permute-start.3) | collective-permute-done | bytes 1048608 | tf_op jit(solution)/shard_map/ppermute | solution.py:24
  145.3 16.9 %collective-permute-done.7.i2b = bf16[3,16,8192]{2,1,0:T(8,128)(2,1)S(1)} collective-permute-done((bf16[3,16,8192]{2,1,0:T(8,128)(2,1)S(1)}, bf16[3,16,8192]{2,1,0:T(8,128)(2,1)S(1)}, u32[]{:S(2)}, u32[]{:S(2)}) %collective-permute-start.7) | collective-permute-done | bytes 786464 | tf_op jit(solution)/shard_map/ppermute | solution.py:24
  162.2 0.9 copy-done.2
  163.1 1.4 collective-permute-done.6.i2a
  164.5 3.3 %all-gather.2.cloned.1.call-done.weight_ref = bf16[32768,640]{1,0:T(8,128)(2,1)} async-done(((bf16[1024,640]{1,0:T(8,128)(2,1)}), bf16[32768,640]{1,0:T(8,128)(2,1)}) %all-gather.2.cloned.1.call-update) | async-done | bytes 41943056 | tf_op jit(solution)/shard_map/all_gather | solution.py:511
  167.8 1.5 copy-done.1
  169.3 1.1 copy-done.3
  170.4 21.8 %project_first.1 = (bf16[576,768]{1,0:T(8,128)(2,1)}, bf16[2,576,256]{2,1,0:T(8,128)(2,1)S(1)}, bf16[576,8192]{1,0:T(8,128)(2,1)}) custom-call(s32[66]{0:T(128)S(1)} %pad_add_fusion.place_ref, bf16[128,8192]{1,0:T(8,128)(2,1)S(1)} %copy-done, bf16[128,8192]{1,0:T(8,128)(2,1)} %collective-permute-done.t1, bf16[64,8192]{1,0:T(8,128)(2,1)} %collective-permute-done.2.t2a, ...), custom_call_target="tpu_custom_call" | custom-call | flops 9663676416 | bytes 26214400 | tf_op jit(solution)/shard_map/project_first/pallas_call | solution.py:245
  192.2 12.6 %project_next.3 = bf16[576,768]{1,0:T(8,128)(2,1)} custom-call(s32[1]{0:T(128)S(6)} %select_n.316.target_ref, bf16[576,8192]{1,0:T(8,128)(2,1)} %get-tuple-element.18.rows_ref, bf16[32768,640]{1,0:T(8,128)(2,1)} %all-gather.2.cloned.1.call-done.weight_ref, bf16[2,576,256]{2,1,0:T(8,128)(2,1)S(1)} %get-tuple-element.20.kv_ref, f32[1,512]{1,0:T(1,128)S(1)} %bitcast.27, ...), custom_call_target="tpu_custom_call" | custom-call | flops 4831838208 | bytes 17825792 | tf_op jit(solution)/shard_map/project_next/pallas_call | solution.py:308
  204.8 12.6 %project_next.4 = bf16[576,768]{1,0:T(8,128)(2,1)} custom-call(s32[1]{0:T(128)S(6)} %select_n.317.target_ref, bf16[576,8192]{1,0:T(8,128)(2,1)} %get-tuple-element.18.rows_ref, bf16[32768,640]{1,0:T(8,128)(2,1)} %all-gather.2.cloned.1.call-done.weight_ref, bf16[2,576,256]{2,1,0:T(8,128)(2,1)S(1)} %get-tuple-element.20.kv_ref, f32[1,512]{1,0:T(1,128)S(1)} %bitcast.25, ...), custom_call_target="tpu_custom_call" | custom-call | flops 4831838208 | bytes 17825792 | tf_op jit(solution)/shard_map/project_next/pallas_call | solution.py:308
  217.4 2.0 collective-permute-start.11
  219.3 1.4 collective-permute-start.12
  221.0 11.7 %project_next.5.part0 = bf16[576,768]{1,0:T(8,128)(2,1)S(1)} custom-call(s32[1]{0:T(128)S(6)} %select_n.318.target_ref, bf16[576,8192]{1,0:T(8,128)(2,1)} %get-tuple-element.18.rows_ref, bf16[32768,640]{1,0:T(8,128)(2,1)} %all-gather.2.cloned.1.call-done.weight_ref, bf16[2,576,256]{2,1,0:T(8,128)(2,1)S(1)} %get-tuple-element.20.kv_ref, ...), custom_call_target="tpu_custom_call" | custom-call | flops 4831838208 | bytes 17825792 | tf_op jit(solution)/shard_map/project_next/pallas_call | solution.py:308
  232.7 6.3 %collective-permute-done.11.part1 = bf16[576,768]{1,0:T(8,128)(2,1)} collective-permute-done((bf16[576,768]{1,0:T(8,128)(2,1)}, bf16[576,768]{1,0:T(8,128)(2,1)}, u32[]{:S(2)}, u32[]{:S(2)}) %collective-permute-start.11) | collective-permute-done | bytes 884768 | tf_op jit(solution)/shard_map/ppermute | solution.py:24
  239.0 21.8 %collective-permute-done.13.part3 = bf16[576,768]{1,0:T(8,128)(2,1)} collective-permute-done((bf16[576,768]{1,0:T(8,128)(2,1)}, bf16[576,768]{1,0:T(8,128)(2,1)}, u32[]{:S(2)}, u32[]{:S(2)}) %collective-permute-start.13) | collective-permute-done | bytes 884768 | tf_op jit(solution)/shard_map/ppermute | solution.py:24
  260.8 24.5 %attend.1 = bf16[2048,512]{1,0:T(8,128)(2,1)} custom-call(s32[12]{0:T(128)S(1)} %concatenate.21.info_ref, s32[128]{0:T(128)S(1)} %reshape.376.text_ref, bf16[576,768]{1,0:T(8,128)(2,1)S(1)} %project_next.5.part0, bf16[576,768]{1,0:T(8,128)(2,1)} %collective-permute-done.11.part1, bf16[576,768]{1,0:T(8,128)(2,1)} %collective-permute-done.12.part2, ...), custom_call_target="tpu_custom_call" | custom-call | tf_op jit(solution)/shard_map/attend/pallas_call | solution.py:429
  (76 shorter events, 3.4 us)
Async XLA Ops:
  6.5 161.3 %all-gather.2.cloned.1.call-start = ((), (), s32[]{:S(2)}) async-start(), calls=%async_computation.1 | async-start | bytes 43253760 | tf_op jit(solution)/shard_map/all_gather | solution.py:511
  10.5 4.4 %copy-start.9 = (s32[32]{0:T(128)S(1)}, s32[32]{0:T(128)}, u32[]{:S(2)}) copy-start(s32[32]{0:T(128)} %param.15) | copy-start | bytes 388
  22.3 6.1 %copy-start = (bf16[128,8192]{1,0:T(8,128)(2,1)S(1)}, bf16[128,8192]{1,0:T(8,128)(2,1)}, u32[]{:S(2)}) copy-start(bf16[128,8192]{1,0:T(8,128)(2,1)} %norm_text.1.t0) | copy-start | bytes 6291460
  22.3 10.0 %copy-start.4 = (f32[512]{0:T(512)S(1)}, f32[512]{0:T(512)}, u32[]{:S(2)}) copy-start(f32[512]{0:T(512)} %param.23) | copy-start | bytes 6148
  22.3 10.0 %copy-start.6 = (f32[64]{0:T(128)S(1)}, f32[64]{0:T(128)}, u32[]{:S(2)}) copy-start(f32[64]{0:T(128)} %param.25) | copy-start | bytes 772
  22.3 10.0 %copy-start.7 = (f32[64]{0:T(128)S(1)}, f32[64]{0:T(128)}, u32[]{:S(2)}) copy-start(f32[64]{0:T(128)} %param.24) | copy-start | bytes 772
  22.4 11.4 %copy-start.8 = (s32[32]{0:T(128)S(1)}, s32[32]{0:T(128)}, u32[]{:S(2)}) copy-start(s32[32]{0:T(128)} %param.16) | copy-start | bytes 388
  22.4 50.0 %all-to-all-start = ((bf16[8,16,8192]{2,1,0:T(8,128)(2,1)}), bf16[8,16,8192]{2,1,0:T(8,128)(2,1)}, u32[]{:S(2)}, u32[]{:S(2)}) async-start(bf16[8,16,8192]{2,1,0:T(8,128)(2,1)} %norm_image.1), calls=%async_computation | async-start | bytes 4194304 | tf_op jit(solution)/shard_map/all_to_all | solution.py:525
  28.4 53.5 %copy-start.5 = (s32[1,2048]{1,0:T(1,128)S(1)}, s32[1,2048]{1,0:T(1,128)}, u32[]{:S(2)}) copy-start(s32[1,2048]{1,0:T(1,128)} %param.18) | copy-start | bytes 24580
  28.4 58.8 %collective-permute-start.1 = (bf16[128,8192]{1,0:T(8,128)(2,1)S(1)}, bf16[128,8192]{1,0:T(8,128)(2,1)}, u32[]{:S(2)}, u32[]{:S(2)}) collective-permute-start(bf16[128,8192]{1,0:T(8,128)(2,1)S(1)} %copy-done), channel_id=1, source_target_pairs={{0,4},{4,8},{8,12},{12,0},{1,5},{5,9},{9,13},{13,1},{2,6},{6,10},{... | collective-permute-start | bytes 6291464 | tf_op jit(solution)/shard_map/ppermute | solution.py:24
  30.1 62.2 %collective-permute-start = (bf16[128,8192]{1,0:T(8,128)(2,1)S(1)}, bf16[128,8192]{1,0:T(8,128)(2,1)}, u32[]{:S(2)}, u32[]{:S(2)}) collective-permute-start(bf16[128,8192]{1,0:T(8,128)(2,1)S(1)} %copy-done), channel_id=1, source_target_pairs={{0,12},{4,0},{8,4},{12,8},{1,13},{5,1},{9,5},{13,9},{2,14},{6,2},{... | collective-permute-start | bytes 6291464 | tf_op jit(solution)/shard_map/ppermute | solution.py:24
  32.4 90.8 %collective-permute-start.10 = (f32[640]{0:T(1024)S(1)}, f32[640]{0:T(1024)S(1)}, u32[]{:S(2)}, u32[]{:S(2)}) collective-permute-start(f32[640]{0:T(1024)S(1)} %pad_maximum_fusion.3), channel_id=1, source_target_pairs={{0,1},{1,2},{2,3},{3,0},{4,5},{5,6},{6,7},{7,4},{8,9},{9,10},{10,1... | collective-permute-start | bytes 7688 | tf_op jit(solution)/shard_map/ppermute | solution.py:24
  77.4 42.2 %collective-permute-start.5 = (bf16[7,16,8192]{2,1,0:T(8,128)(2,1)}, bf16[7,16,8192]{2,1,0:T(8,128)(2,1)}, u32[]{:S(2)}, u32[]{:S(2)}) collective-permute-start(bf16[7,16,8192]{2,1,0:T(8,128)(2,1)} %pick_slots.1.i0), channel_id=1, source_target_pairs={{0,4},{4,8},{8,12},{12,0},{1,5},{5,9},{9,13},{13,1},{2,6},{6,10},{... | collective-permute-start | bytes 5505032 | tf_op jit(solution)/shard_map/ppermute | solution.py:24
  82.1 45.5 %collective-permute-start.4 = (bf16[7,16,8192]{2,1,0:T(8,128)(2,1)}, bf16[7,16,8192]{2,1,0:T(8,128)(2,1)}, u32[]{:S(2)}, u32[]{:S(2)}) collective-permute-start(bf16[7,16,8192]{2,1,0:T(8,128)(2,1)} %pick_slots.1.i0), channel_id=1, source_target_pairs={{0,12},{4,0},{8,4},{12,8},{1,13},{5,1},{9,5},{13,9},{2,14},{6,2},{... | collective-permute-start | bytes 5505032 | tf_op jit(solution)/shard_map/ppermute | solution.py:24
  87.2 37.0 %collective-permute-start.9 = (f32[640]{0:T(1024)S(1)}, f32[640]{0:T(1024)S(1)}, u32[]{:S(2)}, u32[]{:S(2)}) collective-permute-start(f32[640]{0:T(1024)S(1)} %pad_maximum_fusion.3), channel_id=1, source_target_pairs={{0,2},{1,3},{2,0},{3,1},{4,6},{5,7},{6,4},{7,5},{8,10},{9,11},{10,... | collective-permute-start | bytes 7688 | tf_op jit(solution)/shard_map/ppermute | solution.py:24
  92.4 49.6 %collective-permute-start.2 = (bf16[64,8192]{1,0:T(8,128)(2,1)}, bf16[64,8192]{1,0:T(8,128)(2,1)}, u32[]{:S(2)}, u32[]{:S(2)}) collective-permute-start(bf16[64,8192]{1,0:T(8,128)(2,1)} %slice.48), channel_id=1, source_target_pairs={{0,4},{4,8},{8,12},{12,0},{1,5},{5,9},{9,13},{13,1},{2,6},{6,10},{... | collective-permute-start | bytes 3145736 | tf_op jit(solution)/shard_map/ppermute | solution.py:24
  119.5 25.8 %collective-permute-start.3 = (bf16[64,8192]{1,0:T(8,128)(2,1)}, bf16[64,8192]{1,0:T(8,128)(2,1)}, u32[]{:S(2)}, u32[]{:S(2)}) collective-permute-start(bf16[64,8192]{1,0:T(8,128)(2,1)} %slice.49), channel_id=1, source_target_pairs={{0,12},{4,0},{8,4},{12,8},{1,13},{5,1},{9,5},{13,9},{2,14},{6,2},{... | collective-permute-start | bytes 3145736 | tf_op jit(solution)/shard_map/ppermute | solution.py:24
  123.3 41.2 %collective-permute-start.6 = (bf16[4,16,8192]{2,1,0:T(8,128)(2,1)}, bf16[4,16,8192]{2,1,0:T(8,128)(2,1)}, u32[]{:S(2)}, u32[]{:S(2)}) collective-permute-start(bf16[4,16,8192]{2,1,0:T(8,128)(2,1)} %slice.50), channel_id=1, source_target_pairs={{0,4},{4,8},{8,12},{12,0},{1,5},{5,9},{9,13},{13,1},{2,6},{6,10},{... | collective-permute-start | bytes 3145736 | tf_op jit(solution)/shard_map/ppermute | solution.py:24
  124.2 3.4 %collective-permute-start.8 = (f32[640]{0:T(1024)S(1)}, f32[640]{0:T(1024)S(1)}, u32[]{:S(2)}, u32[]{:S(2)}) collective-permute-start(f32[640]{0:T(1024)S(1)} %pad_maximum_fusion.3), channel_id=1, source_target_pairs={{0,3},{1,0},{2,1},{3,2},{4,7},{5,4},{6,5},{7,6},{8,11},{9,8},{10,9... | collective-permute-start | bytes 7688 | tf_op jit(solution)/shard_map/ppermute | solution.py:24
  128.8 33.4 %collective-permute-start.7 = (bf16[3,16,8192]{2,1,0:T(8,128)(2,1)S(1)}, bf16[3,16,8192]{2,1,0:T(8,128)(2,1)S(1)}, u32[]{:S(2)}, u32[]{:S(2)}) collective-permute-start(bf16[3,16,8192]{2,1,0:T(8,128)(2,1)S(1)} %slice.51), channel_id=1, source_target_pairs={{0,12},{4,0},{8,4},{12,8},{1,13},{5,1},{9,5},{13,9},{2,14},{6,2},{... | collective-permute-start | bytes 2359304 | tf_op jit(solution)/shard_map/ppermute | solution.py:24
  162.2 0.9 copy-start.2
  167.8 1.5 copy-start.1
  169.3 1.1 copy-start.3
  217.4 21.6 %collective-permute-start.11 = (bf16[576,768]{1,0:T(8,128)(2,1)}, bf16[576,768]{1,0:T(8,128)(2,1)}, u32[]{:S(2)}, u32[]{:S(2)}) collective-permute-start(bf16[576,768]{1,0:T(8,128)(2,1)} %project_next.4), channel_id=1, source_target_pairs={{0,3},{1,0},{2,1},{3,2},{4,7},{5,4},{6,5},{7,6},{8,11},{9,8},{10,9... | collective-permute-start | bytes 2654216 | tf_op jit(solution)/shard_map/ppermute | solution.py:24
  219.3 41.5 %collective-permute-start.13 = (bf16[576,768]{1,0:T(8,128)(2,1)}, bf16[576,768]{1,0:T(8,128)(2,1)}, u32[]{:S(2)}, u32[]{:S(2)}) collective-permute-start(bf16[576,768]{1,0:T(8,128)(2,1)} %project_next.3), channel_id=1, source_target_pairs={{0,1},{1,2},{2,3},{3,0},{4,5},{5,6},{6,7},{7,4},{8,9},{9,10},{10,1... | collective-permute-start | bytes 2654216 | tf_op jit(solution)/shard_map/ppermute | solution.py:24
  219.3 41.5 %collective-permute-start.12 = (bf16[576,768]{1,0:T(8,128)(2,1)}, bf16[576,768]{1,0:T(8,128)(2,1)}, u32[]{:S(2)}, u32[]{:S(2)}) collective-permute-start(bf16[576,768]{1,0:T(8,128)(2,1)} %get-tuple-element.23), channel_id=1, source_target_pairs={{0,2},{1,3},{2,0},{3,1},{4,6},{5,7},{6,4},{7,5},{8,10},{9,11},{10,... | collective-permute-start | bytes 2654216 | tf_op jit(solution)/shard_map/ppermute | solution.py:24
Sparse Core Ops, SparseCore 0:
  10.6 157.1 all-gather.1
where the time goes:
time: 294 us; the launch traced here: 292 us
  waiting for transfers between devices  122 us (41%)
  Pallas kernels  99.2 us (34%)
  starting transfers between devices  27 us (9%)
  between operations  17.5 us (6%)
  local copies, waits for them, and re-layouts  16.8 us (6%)
  other arithmetic  9.26 us (3%)
    ppermute x14, waiting for transfers between devices, shifted(): lax.ppermute(block, axis, [(low, (low + step) % count) for low in range(c...  85.1 us
    pallas_call x3, Pallas kernels, project_next(): pl.pallas_call(project_next_kernel, grid_spec=pltpu.PrefetchScalarGridSpe...  36.8 us
    all_to_all x1, waiting for transfers between devices, one_device(): lax.all_to_all(outgoing, ('x', 'c'), split_axis=0, concat_axis=0, tiled=T...  34 us
    pallas_call x1, Pallas kernels, attend(): pl.pallas_call(attend_kernel, grid_spec=pltpu.PrefetchScalarGridSpec(num_...  24.5 us
    pallas_call x1, Pallas kernels, project_first(): pl.pallas_call(project_first_kernel, grid_spec=pltpu.PrefetchScalarGridSp...  21.8 us
    ppermute x14, starting transfers between devices, shifted(): lax.ppermute(block, axis, [(low, (low + step) % count) for low in range(c...  20.9 us
    pallas_call x1, Pallas kernels, norm_image(): pl.pallas_call(norm_image_kernel, grid_spec=pltpu.PrefetchScalarGridSpec(...  6.77 us
    all_to_all x1, starting transfers between devices, one_device(): lax.all_to_all(outgoing, ('x', 'c'), split_axis=0, concat_axis=0, tiled=T...  6.06 us
  transfers between devices with their start and end apart: 16, of which 10 were waited for; matrix products, arithmetic and copies ran while one was open for 6% of the time, Pallas kernels for 10%

commit v1 on v0

--- a/solution.py
+++ b/solution.py
@@ -97,58 +97,78 @@
     return values * cosine + pltpu.roll(values, HD // 2, 1) * sine
 
 
-def project_first_kernel(
-    place_ref,
-    t0, t1, t2a, t2b, t3,
-    i0, i1, i2a, i2b, i3,
-    weight_ref, kv_bias_ref, q_bias_ref, cos_ref, sin_ref,
-    out_ref, kv_ref, compact_ref,
-    rows_ref, weight_buf, sum_ref, sems, weight_sems, copy_sem,
-):
+COLUMNS = 256
+PIECE = 1024
+
+
+def weight_tile(own_q, own_kv, pieces, place_ref, weight_buf, sems):
+    def copies(tile, slot):
+        found = []
+        lane = 0
+        for delta, first, count in tile:
+            lanes = pl.ds(lane, count)
+            lane += count
+            if delta == 0:
+                source = own_kv if first == 512 else own_q.at[:, pl.ds(first, count)]
+                found.append((source, weight_buf.at[slot, :, lanes]))
+            else:
+                for index, piece in enumerate(pieces[delta]):
+                    row = pl.multiple_of(place_ref[66 + index // 2] + index % 2 * PIECE, PIECE)
+                    found.append(
+                        (
+                            piece.at[:, pl.ds(first, count)],
+                            weight_buf.at[slot, pl.ds(row, PIECE), lanes],
+                        )
+                    )
+        return [
+            pltpu.make_async_copy(source, target, sems.at[slot, index])
+            for index, (source, target) in enumerate(found)
+        ]
+
+    return copies
+
+
+def run_tiles(tiles, copies, rows_ref, weight_buf, sum_ref, finish, before):
     slots = weight_buf.shape[0]
-    chunks = 8
-    depth = weight_buf.shape[1]
-    width = weight_buf.shape[2]
-    target = place_ref[65]
-
-    def weight_copies(step, slot):
-        kv = [
-            pltpu.make_async_copy(
-                weight_ref.at[pl.ds((step * 4 + y) * depth, depth), pl.ds(width, HD)],
-                weight_buf.at[slot, :, pl.ds(y * HD, HD)],
-                weight_sems.at[slot, y],
-            )
-            for y in range(4)
-        ]
-        query = pltpu.make_async_copy(
-            weight_ref.at[pl.ds(((step - chunks) * 4 + target) * depth, depth), pl.ds(0, width)],
-            weight_buf.at[slot],
-            weight_sems.at[slot, 0],
+    for index in range(min(slots, len(tiles))):
+        for copy in copies(tiles[index], index):
+            copy.start()
+    before()
+
+    def step(number, carry):
+        slot = number % slots
+        for index, tile in enumerate(tiles):
+            @pl.when(number == index)
+            def _(index=index, tile=tile):
+                for copy in copies(tile, index % slots):
+                    copy.wait()
+
+        sum_ref[slot] = jnp.dot(
+            rows_ref[...], weight_buf[slot], preferred_element_type=jnp.float32
         )
-        return kv, query
-
-    def start(step):
-        slot = step % slots
-
-        @pl.when(step < chunks)
-        def _():
-            for copy in weight_copies(step, slot)[0]:
-                copy.start()
-
-        @pl.when((step >= chunks) & (step < 2 * chunks))
-        def _():
-            weight_copies(step, slot)[1].start()
-
-    for step in range(slots - 1):
-        start(jnp.int32(step))
-
-    total = place_ref[64]
-    for unit in range(24, CAPACITY):
-        @pl.when(unit >= total)
-        def _(unit=unit):
-            rows_ref[pl.ds(UNIT * unit, UNIT), :] = jnp.zeros(
-                (UNIT, rows_ref.shape[1]), jnp.bfloat16
-            )
+        for index in range(len(tiles)):
+            @pl.when(number == index)
+            def _(index=index):
+                if index + slots < len(tiles):
+                    for copy in copies(tiles[index + slots], index % slots):
+                        copy.start()
+                finish(index, sum_ref.at[index % slots])
+
+        return carry
+
+    lax.fori_loop(0, len(tiles), step, 0)
+
+
+def project_first_kernel(*refs):
+    place_ref = refs[0]
+    t0, t1, t2a, t2b, t3, i0, i1, i2a, i2b, i3 = refs[1:11]
+    own_q, own_kv = refs[11:13]
+    pieces = {1: refs[13:21], 2: refs[21:29], 3: refs[29:37]}
+    kv_bias_ref, q_bias_ref, cos_ref, sin_ref, out_ref, kv_ref, compact_ref = refs[37:44]
+    rows_ref, weight_buf, sum_ref, sems, weight_sems, copy_sem = refs[44:]
+    copies = weight_tile(own_q, own_kv, pieces, place_ref, weight_buf, weight_sems)
+    width = q_bias_ref.shape[1]
+    copy_out = pltpu.make_async_copy(rows_ref, compact_ref, copy_sem)
 
     def unit_copy(index):
         delta, slot = index % 32 // 8, index % 8
@@ -163,69 +183,63 @@
         row = pl.multiple_of(UNIT * jnp.maximum(place_ref[index], 0), UNIT)
         return pltpu.make_async_copy(source, rows_ref.at[pl.ds(row, UNIT), :], sems.at[index])
 
-    used = [index for index in range(64) if index < 32 or index % 8 < 7]
-    for index in used:
-        @pl.when(place_ref[index] >= 0)
-        def _(index=index):
-            unit_copy(index).start()
-    for index in used:
-        @pl.when(place_ref[index] >= 0)
-        def _(index=index):
-            unit_copy(index).wait()
-    copy_out = pltpu.make_async_copy(rows_ref, compact_ref, copy_sem)
-    copy_out.start()
-
-    def product(step, part):
-        slot = step % slots
-        lanes = pl.ds(pl.multiple_of(part * depth, depth), depth)
-        value = jnp.dot(
-            rows_ref[:, lanes], weight_buf[slot], preferred_element_type=jnp.float32
-        )
-
-        @pl.when(part == 0)
-        def _():
-            sum_ref[...] = value
-
-        @pl.when(part > 0)
-        def _():
-            sum_ref[...] += value
-
-    def kv_step(step, carry):
-        start(step + slots - 1)
-        for copy in weight_copies(step, step % slots)[0]:
-            copy.wait()
-        product(step, step)
-        return carry
-
-    lax.fori_loop(0, chunks, kv_step, 0)
-    cosine = cos_ref[...]
-    sine = sin_ref[...]
-    in_low = lax.broadcasted_iota(jnp.int32, cosine.shape, 1) < HD // 2
-    half = HD // 2
-    for head in range(2):
-        low_lanes = slice(2 * head * HD, (2 * head + 1) * HD)
-        high_lanes = slice((2 * head + 1) * HD, (2 * head + 2) * HD)
-        low = sum_ref[:, low_lanes] + kv_bias_ref[:, low_lanes]
-        high = sum_ref[:, high_lanes] + kv_bias_ref[:, high_lanes]
-        key = jnp.where(in_low, low, pltpu.roll(high, half, 1))
-        value = jnp.where(in_low, pltpu.roll(low, half, 1), high)
-        kv_ref[head, :, :HD] = rotated(key, cosine, sine).astype(jnp.bfloat16)
-        kv_ref[head, :, HD:] = value.astype(jnp.bfloat16)
-
-    def query_step(step, carry):
-        start(step + slots - 1)
-        weight_copies(step, step % slots)[1].wait()
-        product(step, step - chunks)
-        return carry
-
-    lax.fori_loop(chunks, 2 * chunks, query_step, 0)
-    for head in range(width // HD):
-        lanes = slice(head * HD, (head + 1) * HD)
-        out_ref[:, lanes] = rotated(
-            sum_ref[:, lanes] + q_bias_ref[:, lanes], cos_ref[...], sin_ref[...]
-        ).astype(jnp.bfloat16)
-    out_ref[:, width:] = kv_ref[target // 2]
+    def assemble():
+        total = place_ref[64]
+        for unit in range(24, CAPACITY):
+            @pl.when(unit >= total)
+            def _(unit=unit):
+                rows_ref[pl.ds(UNIT * unit, UNIT), :] = jnp.zeros(
+                    (UNIT, rows_ref.shape[1]), jnp.bfloat16
+                )
+
+        used = [index for index in range(64) if index < 32 or index % 8 < 7]
+        for index in used:
+            @pl.when(place_ref[index] >= 0)
+            def _(index=index):
+                unit_copy(index).start()
+        for index in used:
+            @pl.when(place_ref[index] >= 0)
+            def _(index=index):
+                unit_copy(index).wait()
+        copy_out.start()
+
+    def finish(index, product):
+        if index == 1:
+            odd = place_ref[65] == 1
+            halves = [
+                sum_ref[delta // 2, :, pl.ds(delta % 2 * HD, HD)]
+                + kv_bias_ref[:, pl.ds(delta * HD, HD)]
+                for delta in range(4)
+            ]
+            in_low = lax.broadcasted_iota(jnp.int32, halves[0].shape, 1) < HD // 2
+            ends = (
+                (jnp.where(odd, halves[3], halves[0]), jnp.where(odd, halves[0], halves[1])),
+                (jnp.where(odd, halves[1], halves[2]), jnp.where(odd, halves[2], halves[3])),
+            )
+            for head, (low, high) in enumerate(ends):
+                key = jnp.where(in_low, low, pltpu.roll(high, HD // 2, 1))
+                value = jnp.where(in_low, pltpu.roll(low, HD // 2, 1), high)
+                kv_ref[head, :, :HD] = rotated(key, cos_ref[...], sin_ref[...]).astype(
+                    jnp.bfloat16
+                )
+                kv_ref[head, :, HD:] = value.astype(jnp.bfloat16)
+            out_ref[:, width:] = kv_ref[1]
+        if index >= 2:
+            store_heads(out_ref, index - 2, product, q_bias_ref, cos_ref, sin_ref)
+
+    tiles = [
+        [(0, 512, HD), (1, 512, HD)], [(2, 512, HD), (3, 512, HD)],
+        [(2, 0, COLUMNS)], [(2, COLUMNS, COLUMNS)],
+    ]
+    run_tiles(tiles, copies, rows_ref, weight_buf, sum_ref, finish, assemble)
     copy_out.wait()
+
+
+def store_heads(out_ref, part, product, bias_ref, cos_ref, sin_ref):
+    for head in range(COLUMNS // HD):
+        lanes = slice(part * COLUMNS + head * HD, part * COLUMNS + (head + 1) * HD)
+        values = product[:, head * HD:(head + 1) * HD] + bias_ref[:, lanes]
+        out_ref[:, lanes] = rotated(values, cos_ref[...], sin_ref[...]).astype(jnp.bfloat16)
 
 
 def cost(width, features):
@@ -236,99 +250,144 @@
     )
 
 
-def project_first(place, texts, images, weights, kv_bias, q_bias, cosine, sine):
+def far(values):
+    return [pltpu.with_memory_space_constraint(value, pltpu.HBM) for value in values]
+
+
+def whole(shape):
+    return pl.BlockSpec(shape, lambda i, place: (0,) * len(shape))
+
+
+def project_first(place, texts, images, own, pieces, kv_bias, q_bias, cosine, sine):
     width = q_bias.shape[1]
     features = texts[0].shape[1]
-    depth = features // 8
-    any_spec = pl.BlockSpec(memory_space=pltpu.HBM)
-    whole = lambda shape: pl.BlockSpec(shape, lambda i, place: (0,) * len(shape))
+    far_spec = pl.BlockSpec(memory_space=pltpu.HBM)
+    flat = [piece for delta in (1, 2, 3) for piece in pieces[delta]]
     return pl.pallas_call(
         project_first_kernel,
         grid_spec=pltpu.PrefetchScalarGridSpec(
             num_scalar_prefetch=1,
             grid=(1,),
-            in_specs=[any_spec] * 11
+            in_specs=[far_spec] * (12 + len(flat))
             + [whole((1, width)), whole((1, width)), whole((ROWS, HD)), whole((ROWS, HD))],
-            out_specs=(
-                whole((ROWS, width + 2 * HD)),
-                whole((2, ROWS, 2 * HD)),
-                any_spec,
-            ),
+            out_specs=(whole((ROWS, width + 2 * HD)), whole((2, ROWS, 2 * HD)), far_spec),
             scratch_shapes=[
                 pltpu.VMEM((ROWS, features), jnp.bfloat16),
-                pltpu.VMEM((4, depth, width), jnp.bfloat16),
-                pltpu.VMEM((ROWS, width), jnp.float32),
+                pltpu.VMEM((2, features, COLUMNS), jnp.bfloat16),
+                pltpu.VMEM((2, ROWS, COLUMNS), jnp.float32),
                 pltpu.SemaphoreType.DMA((64,)),
-                pltpu.SemaphoreType.DMA((4, 4)),
+                pltpu.SemaphoreType.DMA((2, 16)),
                 pltpu.SemaphoreType.DMA,
             ],
         ),
         out_shape=(
             jax.ShapeDtypeStruct((ROWS, width + 2 * HD), jnp.bfloat16),
             jax.ShapeDtypeStruct((2, ROWS, 2 * HD), jnp.bfloat16),
-            jax.ShapeDtypeStruct((ROWS, features), jnp.bfloat16),
+            pltpu.HBM((ROWS, features), jnp.bfloat16),
         ),
         compiler_params=pltpu.CompilerParams(vmem_limit_bytes=40 << 20),
         cost_estimate=cost(2 * width, features),
         name="project_first",
-    )(place, *texts, *images, weights, kv_bias, q_bias, cosine, sine)
-
-
-def project_next_kernel(
-    target_ref, rows_ref, weight_ref, kv_ref, bias_ref, cos_ref, sin_ref, out_ref, sum_ref
-):
-    part = pl.program_id(0)
-    width = weight_ref.shape[1]
-    value = jnp.dot(rows_ref[...], weight_ref[...], preferred_element_type=jnp.float32)
-
-    @pl.when(part == 0)
-    def _():
-        sum_ref[...] = value
-
-    @pl.when(part > 0)
-    def _():
-        sum_ref[...] += value
-
-    @pl.when(part == pl.num_programs(0) - 1)
-    def _():
-        for head in range(width // HD):
-            lanes = slice(head * HD, (head + 1) * HD)
-            out_ref[:, lanes] = rotated(
-                sum_ref[:, lanes] + bias_ref[:, lanes], cos_ref[...], sin_ref[...]
-            ).astype(jnp.bfloat16)
-        out_ref[:, width:] = kv_ref[0]
-
-
-def project_next(target, compact, weights, kv, q_bias, cosine, sine):
-    width = q_bias.shape[1]
+    )(place, *far([*texts, *images, *own, *flat]), kv_bias, q_bias, cosine, sine)
+
+
+def project_near_kernel(*refs):
+    place_ref, compact_ref = refs[:2]
+    pieces = {1: refs[2:10], 3: refs[10:18]}
+    kv_ref, bias1_ref, bias3_ref, cos_ref, sin_ref, out1_ref, out3_ref = refs[18:25]
+    rows_ref, weight_buf, sum_ref, row_sem, weight_sems = refs[25:]
+    copies = weight_tile(None, None, pieces, place_ref, weight_buf, weight_sems)
+    copy_in = pltpu.make_async_copy(compact_ref, rows_ref, row_sem)
+    copy_in.start()
+    width = bias1_ref.shape[1]
+    odd = place_ref[65]
+    out1_ref[:, width:] = kv_ref[odd]
+    out3_ref[:, width:] = kv_ref[1 - odd]
+
+    def finish(index, product):
+        out_ref, bias_ref = ((out1_ref, bias1_ref), (out3_ref, bias3_ref))[index // 2]
+        store_heads(out_ref, index % 2, product, bias_ref, cos_ref, sin_ref)
+
+    tiles = [[(delta, first, COLUMNS)] for delta in (1, 3) for first in (0, COLUMNS)]
+    run_tiles(tiles, copies, rows_ref, weight_buf, sum_ref, finish, copy_in.wait)
+
+
+def project_near(place, compact, pieces, kv, bias1, bias3, cosine, sine):
+    width = bias1.shape[1]
     features = compact.shape[1]
-    parts = 8
-    depth = features // parts
-    whole = lambda shape: pl.BlockSpec(shape, lambda k, target: (0,) * len(shape))
+    far_spec = pl.BlockSpec(memory_space=pltpu.HBM)
+    flat = [piece for delta in (1, 3) for piece in pieces[delta]]
+    shape = (ROWS, width + 2 * HD)
     return pl.pallas_call(
-        project_next_kernel,
+        project_near_kernel,
         grid_spec=pltpu.PrefetchScalarGridSpec(
             num_scalar_prefetch=1,
-            grid=(parts,),
-            in_specs=[
-                pl.BlockSpec((ROWS, depth), lambda k, target: (0, k)),
-                pl.BlockSpec((depth, width), lambda k, target: (k * 4 + target[0], 0)),
-                pl.BlockSpec((1, ROWS, 2 * HD), lambda k, target: (target[0] // 2, 0, 0)),
-                whole((1, width)),
-                whole((ROWS, HD)),
-                whole((ROWS, HD)),
-            ],
-            out_specs=whole((ROWS, width + 2 * HD)),
-            scratch_shapes=[pltpu.VMEM((ROWS, width), jnp.float32)],
-        ),
-        out_shape=jax.ShapeDtypeStruct((ROWS, width + 2 * HD), jnp.bfloat16),
-        compiler_params=pltpu.CompilerParams(vmem_limit_bytes=32 << 20),
+            grid=(1,),
+            in_specs=[far_spec] * (1 + len(flat))
+            + [
+                whole((2, ROWS, 2 * HD)), whole((1, width)), whole((1, width)),
+                whole((ROWS, HD)), whole((ROWS, HD)),
+            ],
+            out_specs=(whole(shape), whole(shape)),
+            scratch_shapes=[
+                pltpu.VMEM((ROWS, features), jnp.bfloat16),
+                pltpu.VMEM((2, features, COLUMNS), jnp.bfloat16),
+                pltpu.VMEM((2, ROWS, COLUMNS), jnp.float32),
+                pltpu.SemaphoreType.DMA,
+                pltpu.SemaphoreType.DMA((2, 16)),
+            ],
+        ),
+        out_shape=(jax.ShapeDtypeStruct(shape, jnp.bfloat16),) * 2,
+        compiler_params=pltpu.CompilerParams(vmem_limit_bytes=40 << 20),
+        cost_estimate=cost(2 * width, features),
+        name="project_near",
+    )(place, *far([compact, *flat]), kv, bias1, bias3, cosine, sine)
+
+
+def project_own_kernel(
+    place_ref, compact_ref, own_q, kv_ref, bias_ref, cos_ref, sin_ref, out_ref,
+    rows_ref, weight_buf, sum_ref, row_sem, weight_sems,
+):
+    copies = weight_tile(own_q, None, {}, place_ref, weight_buf, weight_sems)
+    copy_in = pltpu.make_async_copy(compact_ref, rows_ref, row_sem)
+    copy_in.start()
+    out_ref[:, bias_ref.shape[1]:] = kv_ref[0]
+
+    def finish(index, product):
+        store_heads(out_ref, index, product, bias_ref, cos_ref, sin_ref)
+
+    tiles = [[(0, 0, COLUMNS)], [(0, COLUMNS, COLUMNS)]]
+    run_tiles(tiles, copies, rows_ref, weight_buf, sum_ref, finish, copy_in.wait)
+
+
+def project_own(place, compact, own_q, kv, bias, cosine, sine):
+    width = bias.shape[1]
+    features = compact.shape[1]
+    far_spec = pl.BlockSpec(memory_space=pltpu.HBM)
+    shape = (ROWS, width + 2 * HD)
+    return pl.pallas_call(
+        project_own_kernel,
+        grid_spec=pltpu.PrefetchScalarGridSpec(
+            num_scalar_prefetch=1,
+            grid=(1,),
+            in_specs=[far_spec] * 2
+            + [
+                whole((2, ROWS, 2 * HD)), whole((1, width)), whole((ROWS, HD)), whole((ROWS, HD)),
+            ],
+            out_specs=whole(shape),
+            scratch_shapes=[
+                pltpu.VMEM((ROWS, features), jnp.bfloat16),
+                pltpu.VMEM((2, features, COLUMNS), jnp.bfloat16),
+                pltpu.VMEM((2, ROWS, COLUMNS), jnp.float32),
+                pltpu.SemaphoreType.DMA,
+                pltpu.SemaphoreType.DMA((2, 16)),
+            ],
+        ),
+        out_shape=jax.ShapeDtypeStruct(shape, jnp.bfloat16),
+        compiler_params=pltpu.CompilerParams(vmem_limit_bytes=40 << 20),
         cost_estimate=cost(width, features),
-        name="project_next",
-    )(
-        target, pltpu.with_memory_space_constraint(compact, pltpu.HBM), weights, kv, q_bias,
-        cosine, sine,
-    )
+        name="project_own",
+    )(place, *far([compact, own_q]), kv, bias, cosine, sine)
 
 
 def attend_kernel(
@@ -396,34 +455,51 @@
         lax.fori_loop(0, 4, block_step, 0)
 
     base = pl.multiple_of(step * block, block)
-    span = block + WINDOW
-    position = base + lax.broadcasted_iota(jnp.int32, (block, 1), 0)
-    doc_start = jnp.zeros((block, 1), jnp.int32)
+    first_doc = jnp.int32(0)
     for doc in range(1, 8):
-        doc_start = jnp.where(position >= info_ref[doc], info_ref[doc], doc_start)
-    other = base - WINDOW + lax.broadcasted_iota(jnp.int32, (block, span), 1)
-    allowed = (other >= doc_start) & (other <= position) & (other < used)
-    mask_ref[...] = jnp.where(allowed, 0.0, NEGATIVE)
-    queries = pl.ds(pl.multiple_of(WINDOW + base, block), block)
-    keys = merged_ref[pl.ds(base, span), 4 * HD:5 * HD]
-    values = merged_ref[pl.ds(base, span), 5 * HD:6 * HD]
-    factor = HD ** (-0.5) * math.log2(math.e)
-    for head in range(4):
-        lanes = slice(head * HD, (head + 1) * HD)
-        scores = lax.dot_general(
-            merged_ref[queries, lanes], keys, (((1,), (1,)), ((), ())),
-            preferred_element_type=jnp.float32,
-        ) + mask_ref[...]
-        peak = jnp.max(scores, axis=-1, keepdims=True)
-        exponent = jnp.exp2((scores - peak) * factor)
-        inverse = 1.0 / jnp.sum(exponent, axis=-1, keepdims=True)
-        probs = (exponent * inverse).astype(jnp.bfloat16)
-        mixed = jnp.dot(probs, values, preferred_element_type=jnp.float32)
-        out_ref[:, lanes] = jnp.where(position < used, mixed, 0.0).astype(jnp.bfloat16)
+        first_doc = jnp.where(base >= info_ref[doc], info_ref[doc], first_doc)
+    reach = (base - first_doc + 127) // 128
+
+    def attend_span(span):
+        position = base + lax.broadcasted_iota(jnp.int32, (block, 1), 0)
+        doc_start = jnp.zeros((block, 1), jnp.int32)
+        for doc in range(1, 8):
+            doc_start = jnp.where(position >= info_ref[doc], info_ref[doc], doc_start)
+        other = base + block - span + lax.broadcasted_iota(jnp.int32, (block, span), 1)
+        allowed = (other >= doc_start) & (other <= position) & (other < used)
+        mask_ref[:, :span] = jnp.where(allowed, 0.0, NEGATIVE)
+        queries = pl.ds(pl.multiple_of(WINDOW + base, block), block)
+        window = pl.ds(pl.multiple_of(WINDOW + base + block - span, 128), span)
+        keys = merged_ref[window, 4 * HD:5 * HD]
+        values = merged_ref[window, 5 * HD:6 * HD]
+        factor = HD ** (-0.5) * math.log2(math.e)
+        for head in range(4):
+            lanes = slice(head * HD, (head + 1) * HD)
+            scores = lax.dot_general(
+                merged_ref[queries, lanes], keys, (((1,), (1,)), ((), ())),
+                preferred_element_type=jnp.float32,
+            ) + mask_ref[:, :span]
+            peak = jnp.max(scores, axis=-1, keepdims=True)
+            exponent = jnp.exp2((scores - peak) * factor)
+            inverse = 1.0 / jnp.sum(exponent, axis=-1, keepdims=True)
+            probs = (exponent * inverse).astype(jnp.bfloat16)
+            mixed = jnp.dot(probs, values, preferred_element_type=jnp.float32)
+            out_ref[:, lanes] = jnp.where(position < used, mixed, 0.0).astype(jnp.bfloat16)
+
+    for extra in (1, 2, 3, 4):
+        within = reach <= 1 if extra == 1 else reach == extra
+
+        @pl.when(within & (base < used))
+        def _(extra=extra):
+            attend_span(block + 128 * extra)
+
+    @pl.when(base >= used)
+    def _():
+        out_ref[...] = jnp.zeros(out_ref.shape, jnp.bfloat16)
 
 
 def attend(info, text_index, parts):
-    block = 256
+    block = 128
     shape = parts[0].shape
     width = shape[1]
     return pl.pallas_call(
@@ -445,7 +521,7 @@
     )(info, text_index, *parts)
 
 
-def tables(tile_group, tile_offset, seq_len, doc_ids, group, z, y):
+def tables(tile_group, tile_offset, seq_len, doc_ids, group, z, y, quarters):
     mine = tile_group == group
     present = jnp.any(mine.reshape(8, 4), axis=1)
     count = jnp.sum(mine.astype(jnp.int32))
@@ -472,7 +548,7 @@
     image_place = jnp.where(eight[None, :] < count, 4 * eight[None, :] + member[:, None], -1)
     image_place = image_place.reshape(-1)
     total = 4 * count + 32 - my_hidden
-    place = jnp.concatenate([text_place, image_place, total[None], (y[None] + 2) % 4])
+    place = jnp.concatenate([text_place, image_place, total[None], y[None] % 2, quarters])
     place = place.astype(jnp.int32)
     is_slot = present[None, :] & (rank[None, :] == eight[:7, None])
     slots = jnp.sum(jnp.where(is_slot, eight[None, :], 0), axis=1).astype(jnp.int32)
@@ -496,26 +572,52 @@
     text_rows, image_rows, tile_group, tile_offset, seq_len, doc_ids, norm_gain,
     q_weight, k_weight, v_weight, q_bias, k_bias, v_bias,
 ):
-    group = lax.axis_index("x") * 2 + lax.axis_index("c")
+    x = lax.axis_index("x")
+    core = lax.axis_index("c")
+    group = x * 2 + core
     z = lax.axis_index("z")
     y = lax.axis_index("y")
-    depth = q_weight.shape[0] // 8
     gain = norm_gain.reshape(1, -1)
-
-    def own_part(weight):
-        return lax.dynamic_slice_in_dim(weight, group * depth, depth, 0)
-
-    weight_part = jnp.concatenate(
-        [own_part(q_weight), own_part(k_weight), own_part(v_weight)], axis=1
-    )
-    weights = lax.all_gather(weight_part, ("x", "c", "y"), axis=0, tiled=True)
 
     t0 = norm_text(text_rows, gain)
     t3 = shifted(t0, "z", 1)
     t1 = shifted(t0, "z", -1)
 
+    quarter = 2 * core + x % 2
+    begin, t0 = lax.optimization_barrier((quarter * 2 * PIECE, t0))
+    own_kv = jnp.concatenate([k_weight, v_weight], axis=1)
+
+    def own_part(half):
+        first = begin + half * PIECE
+        return jnp.concatenate(
+            [
+                lax.dynamic_slice_in_dim(weight, first, PIECE, 0)
+                for weight in (q_weight, own_kv)
+            ],
+            axis=1,
+        )
+
+    low, high = own_part(0), own_part(1)
+    direct = {}
+    direct[1, 0] = shifted(low, "y", -1)
+    direct[3, 1] = shifted(high, "y", 1)
+    direct[1, 1] = shifted(high, "y", -1)
+    direct[3, 0] = shifted(low, "y", 1)
+    direct[2, 0] = shifted(direct[1, 0], "y", -1)
+    direct[2, 1] = shifted(direct[3, 1], "y", 1)
+    across = {key: shifted(value, "x", -1 if key[1] else 1) for key, value in direct.items()}
+    pieces = {
+        delta: [direct[delta, 0], direct[delta, 1], across[delta, 0], across[delta, 1]]
+        for delta in (1, 2, 3)
+    }
+    pieces = {
+        delta: found + [shifted(value, "c", 1) for value in found]
+        for delta, found in pieces.items()
+    }
+    quarters = jnp.stack([quarter ^ 0, quarter ^ 1, quarter ^ 2, quarter ^ 3]) * 2 * PIECE
+
     place, slots, text_index, info, in_doc = tables(
-        tile_group, tile_offset, seq_len, doc_ids, group, z, y
+        tile_group, tile_offset, seq_len, doc_ids, group, z, y, quarters
     )
     row_groups = lax.dynamic_slice_in_dim(tile_group, group * 4, 4)
     matches = row_groups[None, :] == jnp.arange(8, dtype=jnp.int32)[:, None]
@@ -534,32 +636,23 @@
     bias = jnp.concatenate([q_bias, k_bias, v_bias])
     biases = [bias, shifted(bias, "y", -1), shifted(bias, "y", 2), shifted(bias, "y", 1)]
     q_biases = [value[None, :4 * HD] for value in biases]
-    kv_bias = jnp.stack([value[4 * HD:] for value in biases])
-    member = jnp.arange(4, dtype=jnp.int32)[:, None, None]
-    delta = jnp.arange(4, dtype=jnp.int32)[None, :, None]
-    kv_bias = jnp.sum(jnp.where((y + delta) % 4 == member, kv_bias[None], 0.0), axis=1)
-    kv_bias = kv_bias.reshape(1, -1)
+    kv_bias = jnp.concatenate([value[None, 4 * HD:] for value in biases], axis=1)
     frequency = THETA ** (-(jnp.arange(HD // 2, dtype=jnp.float32) * 2.0) / HD)
     angles = in_doc.astype(jnp.float32)[:, None] * frequency[None, :]
     cosine = jnp.concatenate([jnp.cos(angles), jnp.cos(angles)], axis=-1)
     sine = jnp.concatenate([-jnp.sin(angles), jnp.sin(angles)], axis=-1)
 
     out2, kv, compact = project_first(
-        place, (t0, t1, t2a, t2b, t3), (i0, i1, i2a, i2b, i3),
-        weights, kv_bias, q_biases[2], cosine, sine,
+        place, (t0, t1, t2a, t2b, t3), (i0, i1, i2a, i2b, i3), (q_weight, own_kv),
+        pieces, kv_bias, q_biases[2], cosine, sine,
     )
     part2 = shifted(out2, "y", 2)
-    outs = {}
-    after = kv
-    for step in (1, 3, 0):
-        target = (y[None] + step) % 4
-        outs[step] = project_next(
-            target.astype(jnp.int32), compact, weights, after, q_biases[step], cosine, sine
-        )
-        after, outs[step] = lax.optimization_barrier((after, outs[step]))
-    part3 = shifted(outs[1], "y", 1)
-    part1 = shifted(outs[3], "y", -1)
-    return attend(info, text_index, (outs[0], part1, part2, part3))
+    out1, out3 = project_near(place, compact, pieces, kv, q_biases[1], q_biases[3], cosine, sine)
+    part3 = shifted(out1, "y", 1)
+    part1 = shifted(out3, "y", -1)
+    kv, out1 = lax.optimization_barrier((kv, out1))
+    part0 = project_own(place, compact, q_weight, kv, q_biases[0], cosine, sine)
+    return attend(info, text_index, (part0, part1, part2, part3))
 
 
 def solution(mesh):

time: 294 us -> 398 us (1.35)
  waiting for transfers between devices: 122 us -> 207 us
  starting transfers between devices: 27 us -> 60.3 us
  between operations: 17.5 us -> 4.18 us
  Pallas kernels: 99.2 us -> 92.4 us
  other arithmetic: 9.26 us -> 13.3 us
    ppermute x14 -> x38, waiting for transfers between devices: 85.1 us -> 190 us  [shifted(): lax.ppermute(block, axis, [(low, (low + step) % count) for low in range(c...]
    ppermute x14 -> x38, starting transfers between devices: 20.9 us -> 55.6 us  [shifted(): lax.ppermute(block, axis, [(low, (low + step) % count) for low in range(c...]
    all_to_all x1, waiting for transfers between devices: 34 us -> 16.5 us  [one_device(): lax.all_to_all(outgoing, ('x', 'c'), split_axis=0, concat_axis=0, tiled=T...]
    pallas_call x3 -> x2, Pallas kernels: 36.8 us -> 31.5 us  [the longest x1 20 us: project_near(): pl.pallas_call(project_near_kernel, grid_spec=pltpu.PrefetchScalarGridSpe...]
  transfers between devices with their start and end apart: 16 -> 39, of which waited for: 10 -> 13; matrix products, arithmetic and copies ran while one was open for 6% -> 6% of each run, Pallas kernels for 10% -> 6%
where the time goes in v1:
time: 398 us; the launch traced here: 397 us
  waiting for transfers between devices  207 us (52%)
  Pallas kernels  92.4 us (23%)
  starting transfers between devices  60.3 us (15%)
  local copies, waits for them, and re-layouts  19.6 us (5%)
  other arithmetic  13.3 us (3%)
  between operations  4.18 us (1%)
    ppermute x38, waiting for transfers between devices, shifted(): lax.ppermute(block, axis, [(low, (low + step) % count) for low in range(c...  190 us
    ppermute x38, starting transfers between devices, shifted(): lax.ppermute(block, axis, [(low, (low + step) % count) for low in range(c...  55.6 us
    pallas_call x1, Pallas kernels, attend(): pl.pallas_call(attend_kernel, grid_spec=pltpu.PrefetchScalarGridSpec(num_...  24.4 us
    pallas_call x1, Pallas kernels, project_first(): pl.pallas_call(project_first_kernel, grid_spec=pltpu.PrefetchScalarGridSp...  20.3 us
    pallas_call x1, Pallas kernels, project_near(): pl.pallas_call(project_near_kernel, grid_spec=pltpu.PrefetchScalarGridSpe...  20 us
    all_to_all x1, waiting for transfers between devices, one_device(): lax.all_to_all(outgoing, ('x', 'c'), split_axis=0, concat_axis=0, tiled=T...  16.5 us
    pallas_call x1, Pallas kernels, project_own(): pl.pallas_call(project_own_kernel, grid_spec=pltpu.PrefetchScalarGridSpec...  11.5 us
  transfers between devices with their start and end apart: 39, of which 13 were waited for; matrix products, arithmetic and copies ran while one was open for 6% of the time, Pallas kernels for 6%

profile of v1, /device:TPU:1, one launch (start us, length us, event | category | flops | bytes accessed | tf_op | source)
XLA Modules:
  0.0 396.6 jit_solution(4311055267026270039)
XLA Ops:
  0.0 4.5 %norm_text.1.refs_1_ = bf16[128,8192]{1,0:T(8,128)(2,1)} custom-call(bf16[128,8192]{1,0:T(8,128)(2,1)} %rows_ref.1, f32[1,8192]{1,0:T(1,128)} %bitcast.31), custom_call_target="tpu_custom_call" | custom-call | tf_op jit(solution)/shard_map/norm_text/pallas_call | solution.py:40
  5.5 2.7 copy.19
  8.3 2.2 constant_dynamic-slice_fusion
  11.1 2.2 collective-permute-start.25
  13.4 1.3 collective-permute-start.34
  14.7 1.8 collective-permute-start.33
  16.4 1.6 collective-permute-start.32
  18.1 25.1 %collective-permute-done.34 = f32[640]{0:T(1024)S(1)} collective-permute-done((f32[640]{0:T(1024)S(1)}, f32[640]{0:T(1024)S(1)}, u32[]{:S(2)}, u32[]{:S(2)}) %collective-permute-start.34) | collective-permute-done | bytes 2592 | tf_op jit(solution)/shard_map/ppermute | solution.py:24
  43.2 1.5 collective-permute-start.1
  44.7 3.0 collective-permute-start
  48.0 2.6 collective-permute-start.9
  50.6 2.7 collective-permute-start.28
  53.3 24.2 %collective-permute-done.17.refs_30_.refs_11_ = bf16[1024,640]{1,0:T(8,128)(2,1)S(1)} collective-permute-done((bf16[1024,640]{1,0:T(8,128)(2,1)S(1)}, bf16[1024,640]{1,0:T(8,128)(2,1)S(1)}, u32[]{:S(2)}, u32[]{:S(2)}) %collective-permute-start.17) | collective-permute-done | bytes 1310752 | tf_op jit(solution)/shard_map/ppermute | solution.py:24
  81.0 10.6 %collective-permute-done.1.refs_5_ = bf16[128,8192]{1,0:T(8,128)(2,1)} collective-permute-done((bf16[128,8192]{1,0:T(8,128)(2,1)}, bf16[128,8192]{1,0:T(8,128)(2,1)}, u32[]{:S(2)}, u32[]{:S(2)}) %collective-permute-start.1) | collective-permute-done | bytes 2097184 | tf_op jit(solution)/shard_map/ppermute | solution.py:24
  91.7 2.0 collective-permute-start.12
  95.6 6.8 %norm_image.1 = bf16[8,16,8192]{2,1,0:T(8,128)(2,1)} custom-call(s32[8]{0:T(128)} %select_reduce_fusion.2.chosen_ref, bf16[4,16,8192]{2,1,0:T(8,128)(2,1)} %rows_ref.2, f32[1,8192]{1,0:T(1,128)} %bitcast.32), custom_call_target="tpu_custom_call" | custom-call | tf_op jit(solution)/shard_map/norm_image/pallas_call | solution.py:60
  102.4 4.8 %all-to-all-start = ((bf16[8,16,8192]{2,1,0:T(8,128)(2,1)}), bf16[8,16,8192]{2,1,0:T(8,128)(2,1)}, u32[]{:S(2)}, u32[]{:S(2)}) async-start(bf16[8,16,8192]{2,1,0:T(8,128)(2,1)} %norm_image.1), calls=%async_computation | async-start | bytes 4194304 | tf_op jit(solution)/shard_map/all_to_all | solution.py:627
  107.4 2.8 collective-permute-start.27
  110.2 4.8 %collective-permute-start.13 = (bf16[1024,640]{1,0:T(8,128)(2,1)}, bf16[1024,640]{1,0:T(8,128)(2,1)S(1)}, u32[]{:S(2)}, u32[]{:S(2)}) collective-permute-start(bf16[1024,640]{1,0:T(8,128)(2,1)} %copy-done.6), channel_id=1, source_target_pairs={{0,16},{16,0},{1,17},{17,1},{2,18},{18,2},{3,19},{19,3},{4,20},{20... | collective-permute-start | bytes 3932168 | tf_op jit(solution)/shard_map/ppermute | solution.py:24
  114.9 19.4 %collective-permute-done.10.refs_15_.refs_4_ = bf16[1024,640]{1,0:T(8,128)(2,1)} collective-permute-done((bf16[1024,640]{1,0:T(8,128)(2,1)}, bf16[1024,640]{1,0:T(8,128)(2,1)}, u32[]{:S(2)}, u32[]{:S(2)}) %collective-permute-start.10) | collective-permute-done | bytes 1310752 | tf_op jit(solution)/shard_map/ppermute | solution.py:24
  134.4 1.2 collective-permute-start.11
  137.4 2.3 slice.48
  141.5 16.5 %all-to-all-done.rows_ref = bf16[8,16,8192]{2,1,0:T(8,128)(2,1)} async-done(((bf16[8,16,8192]{2,1,0:T(8,128)(2,1)}), bf16[8,16,8192]{2,1,0:T(8,128)(2,1)}, u32[]{:S(2)}, u32[]{:S(2)}) %all-to-all-start) | async-done | bytes 2097184 | tf_op jit(solution)/shard_map/all_to_all | solution.py:627
  158.0 5.0 %pick_slots.1.refs_6_ = bf16[7,16,8192]{2,1,0:T(8,128)(2,1)} custom-call(s32[7]{0:T(128)} %select_reduce_fusion.1.chosen_ref, bf16[8,16,8192]{2,1,0:T(8,128)(2,1)} %all-to-all-done.rows_ref), custom_call_target="tpu_custom_call" | custom-call | tf_op jit(solution)/shard_map/pick_slots/pallas_call | solution.py:83
  163.0 2.7 collective-permute-start.4
  169.0 2.3 slice.49
  171.3 16.9 %collective-permute-done.11.refs_16_.refs_5_ = bf16[1024,640]{1,0:T(8,128)(2,1)} collective-permute-done((bf16[1024,640]{1,0:T(8,128)(2,1)}, bf16[1024,640]{1,0:T(8,128)(2,1)}, u32[]{:S(2)}, u32[]{:S(2)}) %collective-permute-start.11) | collective-permute-done | bytes 1310752 | tf_op jit(solution)/shard_map/ppermute | solution.py:24
  191.5 1.9 fusion.2
  193.4 30.2 %collective-permute-done.3.refs_4_ = bf16[64,8192]{1,0:T(8,128)(2,1)} collective-permute-done((bf16[64,8192]{1,0:T(8,128)(2,1)}, bf16[64,8192]{1,0:T(8,128)(2,1)}, u32[]{:S(2)}, u32[]{:S(2)}) %collective-permute-start.3) | collective-permute-done | bytes 1048608 | tf_op jit(solution)/shard_map/ppermute | solution.py:24
  223.7 1.6 collective-permute-start.19
  225.3 3.4 collective-permute-start.14
  228.7 3.0 collective-permute-start.20
  233.1 4.1 %pad_maximum_fusion.refs_12_ = bf16[8192,128]{1,0:T(8,128)(2,1)} fusion(bf16[8192,64]{1,0:T(8,128)(2,1)} %copy.19, bf16[8192,64]{1,0:T(8,128)(2,1)S(1)} %copy.18), kind=kLoop, calls=%fused_computation.3 | loop fusion | flops 4194304 | bytes 4194304 | tf_op jit(solution)/shard_map/concatenate | solution.py:588
  237.2 13.5 %collective-permute-done.19.refs_23_ = bf16[1024,640]{1,0:T(8,128)(2,1)} collective-permute-done((bf16[1024,640]{1,0:T(8,128)(2,1)}, bf16[1024,640]{1,0:T(8,128)(2,1)}, u32[]{:S(2)}, u32[]{:S(2)}) %collective-permute-start.19) | collective-permute-done | bytes 1310752 | tf_op jit(solution)/shard_map/ppermute | solution.py:24
  250.7 5.8 %collective-permute-start.15 = (bf16[1024,640]{1,0:T(8,128)(2,1)}, bf16[1024,640]{1,0:T(8,128)(2,1)S(1)}, u32[]{:S(2)}, u32[]{:S(2)}) collective-permute-start(bf16[1024,640]{1,0:T(8,128)(2,1)} %collective-permute-done.11.refs_16_.refs_5_), channel_id=1, source_target_pairs={{0,16},{16,0},{1,17},{17,1},{2,18},{18,2},{3,19},{19,3},{4,20},{20... | collective-permute-start | bytes 3932168 | tf_op jit(solution)/shard_map/ppermute | solution.py:24
  256.5 3.6 collective-permute-done.20.refs_24_
  261.0 2.3 slice.50
  263.7 2.1 slice.51
  265.8 3.3 collective-permute-start.7
  270.7 15.5 %collective-permute-done.7.refs_9_ = bf16[3,16,8192]{2,1,0:T(8,128)(2,1)S(1)} collective-permute-done((bf16[3,16,8192]{2,1,0:T(8,128)(2,1)}, bf16[3,16,8192]{2,1,0:T(8,128)(2,1)S(1)}, u32[]{:S(2)}, u32[]{:S(2)}) %collective-permute-start.7) | collective-permute-done | bytes 786464 | tf_op jit(solution)/shard_map/ppermute | solution.py:24
  286.3 4.3 %collective-permute-done.6.refs_8_ = bf16[4,16,8192]{2,1,0:T(8,128)(2,1)} collective-permute-done((bf16[4,16,8192]{2,1,0:T(8,128)(2,1)}, bf16[4,16,8192]{2,1,0:T(8,128)(2,1)}, u32[]{:S(2)}, u32[]{:S(2)}) %collective-permute-start.6) | collective-permute-done | bytes 1048608 | tf_op jit(solution)/shard_map/ppermute | solution.py:24
  290.6 20.3 %project_first.1 = (bf16[576,768]{1,0:T(8,128)(2,1)}, bf16[2,576,256]{2,1,0:T(8,128)(2,1)S(1)}, bf16[576,8192]{1,0:T(8,128)(2,1)}) custom-call(s32[70]{0:T(128)S(1)} %concatenate.31.refs_0_.place_ref, bf16[128,8192]{1,0:T(8,128)(2,1)} %norm_text.1.refs_1_, bf16[128,8192]{1,0:T(8,128)(2,1)} %collective-permute-done.refs_2_, ...), custom_call_target="tpu_custom_call" | custom-call | flops 9663676416 | bytes 26214400 | tf_op jit(solution)/shard_map/project_first/pallas_call | solution.py:266
  310.9 20.0 %project_near.1 = (bf16[576,768]{1,0:T(8,128)(2,1)}, bf16[576,768]{1,0:T(8,128)(2,1)}) custom-call(s32[70]{0:T(128)S(1)} %concatenate.31.refs_0_.place_ref, bf16[576,8192]{1,0:T(8,128)(2,1)} %get-tuple-element.19.refs_1_.compact_ref, bf16[1024,640]{1,0:T(8,128)(2,1)} %collective-permute-done.8.refs_13_.refs_2_, bf16[1024,640]{1,0:T(8,128)(2,1)} %copy-done.6, ...), custom_call_target="tpu_custom_call" | custom-call | flops 9663676416 | bytes 26214400 | tf_op jit(solution)/shard_map/project_near/pallas_call | solution.py:321
  331.0 1.5 collective-permute-start.37
  333.8 11.5 %project_own.1.part0 = bf16[576,768]{1,0:T(8,128)(2,1)S(1)} custom-call(s32[70]{0:T(128)S(1)} %concatenate.31.refs_0_.place_ref, bf16[576,8192]{1,0:T(8,128)(2,1)} %get-tuple-element.19.refs_1_.compact_ref, bf16[8192,512]{1,0:T(8,128)(2,1)} %own_q.1, bf16[2,576,256]{2,1,0:T(8,128)(2,1)S(1)} %copy-done.1, f32[1,512]{1,0:T(1,128)S(1)} %bitcast.27, ...), custom_call_target="tpu_custom_call" | custom-call | flops 4831838208 | bytes 17825792 | tf_op jit(solution)/shard_map/project_own/pallas_call | solution.py:368
  345.3 6.6 %collective-permute-done.35.part1 = bf16[576,768]{1,0:T(8,128)(2,1)S(1)} collective-permute-done((bf16[576,768]{1,0:T(8,128)(2,1)}, bf16[576,768]{1,0:T(8,128)(2,1)S(1)}, u32[]{:S(2)}, u32[]{:S(2)}) %collective-permute-start.35) | collective-permute-done | bytes 884768 | tf_op jit(solution)/shard_map/ppermute | solution.py:24
  352.0 20.3 %collective-permute-done.37.part3 = bf16[576,768]{1,0:T(8,128)(2,1)S(1)} collective-permute-done((bf16[576,768]{1,0:T(8,128)(2,1)}, bf16[576,768]{1,0:T(8,128)(2,1)S(1)}, u32[]{:S(2)}, u32[]{:S(2)}) %collective-permute-start.37) | collective-permute-done | bytes 884768 | tf_op jit(solution)/shard_map/ppermute | solution.py:24
  372.2 24.4 %attend.1 = bf16[2048,512]{1,0:T(8,128)(2,1)} custom-call(s32[12]{0:T(128)S(1)} %concatenate.30.info_ref, s32[128]{0:T(128)S(1)} %reshape.320.text_ref, bf16[576,768]{1,0:T(8,128)(2,1)S(1)} %project_own.1.part0, bf16[576,768]{1,0:T(8,128)(2,1)S(1)} %collective-permute-done.35.part1, bf16[576,768]{1,0:T(8,128)(2,1)S(1)} %collective-permute-done.36.part2, ...), custom_call_target="tpu_custom_call" | custom-call | tf_op jit(solution)/shard_map/attend/pallas_call | solution.py:505
  (136 shorter events, 20.0 us)
Async XLA Ops:
  11.1 69.9 %copy-start.17 = (s32[32]{0:T(128)S(1)}, s32[32]{0:T(128)}, u32[]{:S(2)}) copy-start(s32[32]{0:T(128)} %param.15) | copy-start | bytes 388
  11.1 36.9 %collective-permute-start.25 = (bf16[1024,640]{1,0:T(8,128)(2,1)S(1)}, bf16[1024,640]{1,0:T(8,128)(2,1)S(1)}, u32[]{:S(2)}, u32[]{:S(2)}) collective-permute-start(bf16[1024,640]{1,0:T(8,128)(2,1)S(1)} %pad_maximum_fusion.1), channel_id=1, source_target_pairs={{0,1},{1,2},{2,3},{3,0},{4,5},{5,6},{6,7},{7,4},{8,9},{9,10},{10,1... | collective-permute-start | bytes 3932168 | tf_op jit(solution)/shard_map/ppermute | solution.py:24
  13.4 29.8 %collective-permute-start.34 = (f32[640]{0:T(1024)S(1)}, f32[640]{0:T(1024)S(1)}, u32[]{:S(2)}, u32[]{:S(2)}) collective-permute-start(f32[640]{0:T(1024)S(1)} %pad_maximum_fusion.5), channel_id=1, source_target_pairs={{0,1},{1,2},{2,3},{3,0},{4,5},{5,6},{6,7},{7,4},{8,9},{9,10},{10,1... | collective-permute-start | bytes 7688 | tf_op jit(solution)/shard_map/ppermute | solution.py:24
  14.7 30.0 %collective-permute-start.33 = (f32[640]{0:T(1024)S(1)}, f32[640]{0:T(1024)S(1)}, u32[]{:S(2)}, u32[]{:S(2)}) collective-permute-start(f32[640]{0:T(1024)S(1)} %pad_maximum_fusion.5), channel_id=1, source_target_pairs={{0,2},{1,3},{2,0},{3,1},{4,6},{5,7},{6,4},{7,5},{8,10},{9,11},{10,... | collective-permute-start | bytes 7688 | tf_op jit(solution)/shard_map/ppermute | solution.py:24
  16.4 31.4 %collective-permute-start.32 = (f32[640]{0:T(1024)S(1)}, f32[640]{0:T(1024)S(1)}, u32[]{:S(2)}, u32[]{:S(2)}) collective-permute-start(f32[640]{0:T(1024)S(1)} %pad_maximum_fusion.5), channel_id=1, source_target_pairs={{0,3},{1,0},{2,1},{3,2},{4,7},{5,4},{6,5},{7,6},{8,11},{9,8},{10,9... | collective-permute-start | bytes 7688 | tf_op jit(solution)/shard_map/ppermute | solution.py:24
  18.1 32.6 %collective-permute-start.8 = (bf16[1024,640]{1,0:T(8,128)(2,1)S(1)}, bf16[1024,640]{1,0:T(8,128)(2,1)}, u32[]{:S(2)}, u32[]{:S(2)}) collective-permute-start(bf16[1024,640]{1,0:T(8,128)(2,1)S(1)} %pad_maximum_fusion.1), channel_id=1, source_target_pairs={{0,3},{1,0},{2,1},{3,2},{4,7},{5,4},{6,5},{7,6},{8,11},{9,8},{10,9... | collective-permute-start | bytes 3932168 | tf_op jit(solution)/shard_map/ppermute | solution.py:24
  43.2 48.5 %collective-permute-start.1 = (bf16[128,8192]{1,0:T(8,128)(2,1)}, bf16[128,8192]{1,0:T(8,128)(2,1)}, u32[]{:S(2)}, u32[]{:S(2)}) collective-permute-start(bf16[128,8192]{1,0:T(8,128)(2,1)} %norm_text.1.refs_1_), channel_id=1, source_target_pairs={{0,4},{4,8},{8,12},{12,0},{1,5},{5,9},{9,13},{13,1},{2,6},{6,10},{... | collective-permute-start | bytes 6291464 | tf_op jit(solution)/shard_map/ppermute | solution.py:24
  44.7 49.0 %collective-permute-start = (bf16[128,8192]{1,0:T(8,128)(2,1)}, bf16[128,8192]{1,0:T(8,128)(2,1)}, u32[]{:S(2)}, u32[]{:S(2)}) collective-permute-start(bf16[128,8192]{1,0:T(8,128)(2,1)} %norm_text.1.refs_1_), channel_id=1, source_target_pairs={{0,12},{4,0},{8,4},{12,8},{1,13},{5,1},{9,5},{13,9},{2,14},{6,2},{... | collective-permute-start | bytes 6291464 | tf_op jit(solution)/shard_map/ppermute | solution.py:24
  47.9 29.6 %collective-permute-start.17 = (bf16[1024,640]{1,0:T(8,128)(2,1)S(1)}, bf16[1024,640]{1,0:T(8,128)(2,1)S(1)}, u32[]{:S(2)}, u32[]{:S(2)}) collective-permute-start(bf16[1024,640]{1,0:T(8,128)(2,1)S(1)} %pad_maximum_fusion.2), channel_id=1, source_target_pairs={{0,1},{1,2},{2,3},{3,0},{4,5},{5,6},{6,7},{7,4},{8,9},{9,10},{10,1... | collective-permute-start | bytes 3932168 | tf_op jit(solution)/shard_map/ppermute | solution.py:24
  48.0 54.4 %copy-start.4 = (bf16[1024,640]{1,0:T(8,128)(2,1)}, bf16[1024,640]{1,0:T(8,128)(2,1)S(1)}, u32[]{:S(2)}) copy-start(bf16[1024,640]{1,0:T(8,128)(2,1)S(1)} %collective-permute-done.25.refs_29_.refs_10_) | copy-start | bytes 3932164
  48.0 30.7 %collective-permute-start.9 = (bf16[1024,640]{1,0:T(8,128)(2,1)S(1)}, bf16[1024,640]{1,0:T(8,128)(2,1)S(1)}, u32[]{:S(2)}, u32[]{:S(2)}) collective-permute-start(bf16[1024,640]{1,0:T(8,128)(2,1)S(1)} %pad_maximum_fusion.2), channel_id=1, source_target_pairs={{0,3},{1,0},{2,1},{3,2},{4,7},{5,4},{6,5},{7,6},{8,11},{9,8},{10,9... | collective-permute-start | bytes 3932168 | tf_op jit(solution)/shard_map/ppermute | solution.py:24
  50.6 56.5 %collective-permute-start.28 = (bf16[1024,640]{1,0:T(8,128)(2,1)S(1)}, bf16[1024,640]{1,0:T(8,128)(2,1)}, u32[]{:S(2)}, u32[]{:S(2)}) collective-permute-start(bf16[1024,640]{1,0:T(8,128)(2,1)S(1)} %collective-permute-done.25.refs_29_.refs_10_), channel_id=1, source_target_pairs={{0,16},{16,0},{1,17},{17,1},{2,18},{18,2},{3,19},{19,3},{4,20},{20... | collective-permute-start | bytes 3932168 | tf_op jit(solution)/shard_map/ppermute | solution.py:24
  77.5 29.9 %collective-permute-start.26 = (bf16[1024,640]{1,0:T(8,128)(2,1)S(1)}, bf16[1024,640]{1,0:T(8,128)(2,1)}, u32[]{:S(2)}, u32[]{:S(2)}) collective-permute-start(bf16[1024,640]{1,0:T(8,128)(2,1)S(1)} %collective-permute-done.25.refs_29_.refs_10_), channel_id=1, source_target_pairs={{0,32},{32,64},{64,96},{96,0},{1,33},{33,65},{65,97},{97,1},{2,34}... | collective-permute-start | bytes 3932168 | tf_op jit(solution)/shard_map/ppermute | solution.py:24
  79.8 30.4 %collective-permute-start.16 = (bf16[1024,640]{1,0:T(8,128)(2,1)}, bf16[1024,640]{1,0:T(8,128)(2,1)}, u32[]{:S(2)}, u32[]{:S(2)}) collective-permute-start(bf16[1024,640]{1,0:T(8,128)(2,1)} %collective-permute-done.8.refs_13_.refs_2_), channel_id=1, source_target_pairs={{0,3},{1,0},{2,1},{3,2},{4,7},{5,4},{6,5},{7,6},{8,11},{9,8},{10,9... | collective-permute-start | bytes 3932168 | tf_op jit(solution)/shard_map/ppermute | solution.py:24
  91.7 18.5 %collective-permute-start.12 = (bf16[1024,640]{1,0:T(8,128)(2,1)}, bf16[1024,640]{1,0:T(8,128)(2,1)}, u32[]{:S(2)}, u32[]{:S(2)}) collective-permute-start(bf16[1024,640]{1,0:T(8,128)(2,1)} %collective-permute-done.8.refs_13_.refs_2_), channel_id=1, source_target_pairs={{0,16},{16,0},{1,17},{17,1},{2,18},{18,2},{3,19},{19,3},{4,20},{20... | collective-permute-start | bytes 3932168 | tf_op jit(solution)/shard_map/ppermute | solution.py:24
  93.7 40.6 %collective-permute-start.10 = (bf16[1024,640]{1,0:T(8,128)(2,1)}, bf16[1024,640]{1,0:T(8,128)(2,1)}, u32[]{:S(2)}, u32[]{:S(2)}) collective-permute-start(bf16[1024,640]{1,0:T(8,128)(2,1)} %collective-permute-done.8.refs_13_.refs_2_), channel_id=1, source_target_pairs={{0,32},{32,64},{64,96},{96,0},{1,33},{33,65},{65,97},{97,1},{2,34}... | collective-permute-start | bytes 3932168 | tf_op jit(solution)/shard_map/ppermute | solution.py:24
  102.4 33.3 %copy-start.16 = (s32[32]{0:T(128)S(1)}, s32[32]{0:T(128)}, u32[]{:S(2)}) copy-start(s32[32]{0:T(128)} %param.16) | copy-start | bytes 388
  102.4 55.7 %all-to-all-start = ((bf16[8,16,8192]{2,1,0:T(8,128)(2,1)}), bf16[8,16,8192]{2,1,0:T(8,128)(2,1)}, u32[]{:S(2)}, u32[]{:S(2)}) async-start(bf16[8,16,8192]{2,1,0:T(8,128)(2,1)} %norm_image.1), calls=%async_computation | async-start | bytes 4194304 | tf_op jit(solution)/shard_map/all_to_all | solution.py:627
  107.1 32.5 %collective-permute-start.29 = (bf16[1024,640]{1,0:T(8,128)(2,1)}, bf16[1024,640]{1,0:T(8,128)(2,1)}, u32[]{:S(2)}, u32[]{:S(2)}) collective-permute-start(bf16[1024,640]{1,0:T(8,128)(2,1)} %copy-done.5), channel_id=1, source_target_pairs={{0,16},{16,0},{1,17},{17,1},{2,18},{18,2},{3,19},{19,3},{4,20},{20... | collective-permute-start | bytes 3932168 | tf_op jit(solution)/shard_map/ppermute | solution.py:24
  107.4 55.6 %collective-permute-start.27 = (bf16[1024,640]{1,0:T(8,128)(2,1)}, bf16[1024,640]{1,0:T(8,128)(2,1)}, u32[]{:S(2)}, u32[]{:S(2)}) collective-permute-start(bf16[1024,640]{1,0:T(8,128)(2,1)} %copy-done.5), channel_id=1, source_target_pairs={{0,96},{32,0},{64,32},{96,64},{1,97},{33,1},{65,33},{97,65},{2,98}... | collective-permute-start | bytes 3932168 | tf_op jit(solution)/shard_map/ppermute | solution.py:24
  110.1 52.9 %collective-permute-start.18 = (bf16[1024,640]{1,0:T(8,128)(2,1)}, bf16[1024,640]{1,0:T(8,128)(2,1)}, u32[]{:S(2)}, u32[]{:S(2)}) collective-permute-start(bf16[1024,640]{1,0:T(8,128)(2,1)} %copy-done.5), channel_id=1, source_target_pairs={{0,1},{1,2},{2,3},{3,0},{4,5},{5,6},{6,7},{7,4},{8,9},{9,10},{10,1... | collective-permute-start | bytes 3932168 | tf_op jit(solution)/shard_map/ppermute | solution.py:24
  110.2 61.1 %collective-permute-start.13 = (bf16[1024,640]{1,0:T(8,128)(2,1)}, bf16[1024,640]{1,0:T(8,128)(2,1)S(1)}, u32[]{:S(2)}, u32[]{:S(2)}) collective-permute-start(bf16[1024,640]{1,0:T(8,128)(2,1)} %copy-done.6), channel_id=1, source_target_pairs={{0,16},{16,0},{1,17},{17,1},{2,18},{18,2},{3,19},{19,3},{4,20},{20... | collective-permute-start | bytes 3932168 | tf_op jit(solution)/shard_map/ppermute | solution.py:24
  134.4 53.8 %collective-permute-start.11 = (bf16[1024,640]{1,0:T(8,128)(2,1)}, bf16[1024,640]{1,0:T(8,128)(2,1)}, u32[]{:S(2)}, u32[]{:S(2)}) collective-permute-start(bf16[1024,640]{1,0:T(8,128)(2,1)} %copy-done.6), channel_id=1, source_target_pairs={{0,96},{32,0},{64,32},{96,64},{1,97},{33,1},{65,33},{97,65},{2,98}... | collective-permute-start | bytes 3932168 | tf_op jit(solution)/shard_map/ppermute | solution.py:24
  139.7 49.6 %collective-permute-start.2 = (bf16[64,8192]{1,0:T(8,128)(2,1)}, bf16[64,8192]{1,0:T(8,128)(2,1)}, u32[]{:S(2)}, u32[]{:S(2)}) collective-permute-start(bf16[64,8192]{1,0:T(8,128)(2,1)} %slice.48), channel_id=1, source_target_pairs={{0,4},{4,8},{8,12},{12,0},{1,5},{5,9},{9,13},{13,1},{2,6},{6,10},{... | collective-permute-start | bytes 3145736 | tf_op jit(solution)/shard_map/ppermute | solution.py:24
  163.0 26.2 %copy-start.13 = (s32[1,2048]{1,0:T(1,128)S(1)}, s32[1,2048]{1,0:T(1,128)}, u32[]{:S(2)}) copy-start(s32[1,2048]{1,0:T(1,128)} %param.18) | copy-start | bytes 24580
  163.0 62.3 %collective-permute-start.5 = (bf16[7,16,8192]{2,1,0:T(8,128)(2,1)}, bf16[7,16,8192]{2,1,0:T(8,128)(2,1)}, u32[]{:S(2)}, u32[]{:S(2)}) collective-permute-start(bf16[7,16,8192]{2,1,0:T(8,128)(2,1)} %pick_slots.1.refs_6_), channel_id=1, source_target_pairs={{0,4},{4,8},{8,12},{12,0},{1,5},{5,9},{9,13},{13,1},{2,6},{6,10},{... | collective-permute-start | bytes 5505032 | tf_op jit(solution)/shard_map/ppermute | solution.py:24
  163.0 65.7 %collective-permute-start.4 = (bf16[7,16,8192]{2,1,0:T(8,128)(2,1)}, bf16[7,16,8192]{2,1,0:T(8,128)(2,1)}, u32[]{:S(2)}, u32[]{:S(2)}) collective-permute-start(bf16[7,16,8192]{2,1,0:T(8,128)(2,1)} %pick_slots.1.refs_6_), channel_id=1, source_target_pairs={{0,12},{4,0},{8,4},{12,8},{1,13},{5,1},{9,5},{13,9},{2,14},{6,2},{... | collective-permute-start | bytes 5505032 | tf_op jit(solution)/shard_map/ppermute | solution.py:24
  171.3 61.4 %copy-start.7 = (bf16[1024,640]{1,0:T(8,128)(2,1)}, bf16[1024,640]{1,0:T(8,128)(2,1)S(1)}, u32[]{:S(2)}) copy-start(bf16[1024,640]{1,0:T(8,128)(2,1)S(1)} %collective-permute-done.13.refs_18_.refs_7_) | copy-start | bytes 3932164
  171.3 52.4 %collective-permute-start.3 = (bf16[64,8192]{1,0:T(8,128)(2,1)}, bf16[64,8192]{1,0:T(8,128)(2,1)}, u32[]{:S(2)}, u32[]{:S(2)}) collective-permute-start(bf16[64,8192]{1,0:T(8,128)(2,1)} %slice.49), channel_id=1, source_target_pairs={{0,12},{4,0},{8,4},{12,8},{1,13},{5,1},{9,5},{13,9},{2,14},{6,2},{... | collective-permute-start | bytes 3145736 | tf_op jit(solution)/shard_map/ppermute | solution.py:24
  188.2 43.5 %collective-permute-start.30 = (bf16[1024,640]{1,0:T(8,128)(2,1)}, bf16[1024,640]{1,0:T(8,128)(2,1)}, u32[]{:S(2)}, u32[]{:S(2)}) collective-permute-start(bf16[1024,640]{1,0:T(8,128)(2,1)} %collective-permute-done.26.refs_31_.refs_12_), channel_id=1, source_target_pairs={{0,16},{16,0},{1,17},{17,1},{2,18},{18,2},{3,19},{19,3},{4,20},{20... | collective-permute-start | bytes 3932168 | tf_op jit(solution)/shard_map/ppermute | solution.py:24
  189.3 43.6 %collective-permute-start.21 = (bf16[1024,640]{1,0:T(8,128)(2,1)}, bf16[1024,640]{1,0:T(8,128)(2,1)}, u32[]{:S(2)}, u32[]{:S(2)}) collective-permute-start(bf16[1024,640]{1,0:T(8,128)(2,1)} %collective-permute-done.16.refs_21_), channel_id=1, source_target_pairs={{0,16},{16,0},{1,17},{17,1},{2,18},{18,2},{3,19},{19,3},{4,20},{20... | collective-permute-start | bytes 3932168 | tf_op jit(solution)/shard_map/ppermute | solution.py:24
  223.7 27.0 %collective-permute-start.19 = (bf16[1024,640]{1,0:T(8,128)(2,1)}, bf16[1024,640]{1,0:T(8,128)(2,1)}, u32[]{:S(2)}, u32[]{:S(2)}) collective-permute-start(bf16[1024,640]{1,0:T(8,128)(2,1)} %collective-permute-done.16.refs_21_), channel_id=1, source_target_pairs={{0,32},{32,64},{64,96},{96,0},{1,33},{33,65},{65,97},{97,1},{2,34}... | collective-permute-start | bytes 3932168 | tf_op jit(solution)/shard_map/ppermute | solution.py:24
  225.3 31.2 %collective-permute-start.14 = (bf16[1024,640]{1,0:T(8,128)(2,1)}, bf16[1024,640]{1,0:T(8,128)(2,1)}, u32[]{:S(2)}, u32[]{:S(2)}) collective-permute-start(bf16[1024,640]{1,0:T(8,128)(2,1)} %collective-permute-done.10.refs_15_.refs_4_), channel_id=1, source_target_pairs={{0,16},{16,0},{1,17},{17,1},{2,18},{18,2},{3,19},{19,3},{4,20},{20... | collective-permute-start | bytes 3932168 | tf_op jit(solution)/shard_map/ppermute | solution.py:24
  228.7 31.3 %collective-permute-start.20 = (bf16[1024,640]{1,0:T(8,128)(2,1)}, bf16[1024,640]{1,0:T(8,128)(2,1)}, u32[]{:S(2)}, u32[]{:S(2)}) collective-permute-start(bf16[1024,640]{1,0:T(8,128)(2,1)} %collective-permute-done.18.refs_22_), channel_id=1, source_target_pairs={{0,96},{32,0},{64,32},{96,64},{1,97},{33,1},{65,33},{97,65},{2,98}... | collective-permute-start | bytes 3932168 | tf_op jit(solution)/shard_map/ppermute | solution.py:24
  231.7 31.6 %collective-permute-start.31 = (bf16[1024,640]{1,0:T(8,128)(2,1)}, bf16[1024,640]{1,0:T(8,128)(2,1)}, u32[]{:S(2)}, u32[]{:S(2)}) collective-permute-start(bf16[1024,640]{1,0:T(8,128)(2,1)} %collective-permute-done.27.refs_32_.refs_13_), channel_id=1, source_target_pairs={{0,16},{16,0},{1,17},{17,1},{2,18},{18,2},{3,19},{19,3},{4,20},{20... | collective-permute-start | bytes 3932168 | tf_op jit(solution)/shard_map/ppermute | solution.py:24
  232.9 32.9 %collective-permute-start.22 = (bf16[1024,640]{1,0:T(8,128)(2,1)}, bf16[1024,640]{1,0:T(8,128)(2,1)}, u32[]{:S(2)}, u32[]{:S(2)}) collective-permute-start(bf16[1024,640]{1,0:T(8,128)(2,1)} %collective-permute-done.18.refs_22_), channel_id=1, source_target_pairs={{0,16},{16,0},{1,17},{17,1},{2,18},{18,2},{3,19},{19,3},{4,20},{20... | collective-permute-start | bytes 3932168 | tf_op jit(solution)/shard_map/ppermute | solution.py:24
  237.2 26.3 %copy-start.9 = (f32[576,64]{1,0:T(8,128)S(1)}, f32[576,64]{1,0:T(8,128)}, u32[]{:S(2)}) copy-start(f32[576,64]{1,0:T(8,128)} %get-tuple-element.34) | copy-start | bytes 442372
  237.2 26.3 %copy-start.10 = (f32[576,64]{1,0:T(8,128)S(1)}, f32[576,64]{1,0:T(8,128)}, u32[]{:S(2)}) copy-start(f32[576,64]{1,0:T(8,128)} %get-tuple-element.35) | copy-start | bytes 442372
  250.7 20.1 %collective-permute-start.15 = (bf16[1024,640]{1,0:T(8,128)(2,1)}, bf16[1024,640]{1,0:T(8,128)(2,1)S(1)}, u32[]{:S(2)}, u32[]{:S(2)}) collective-permute-start(bf16[1024,640]{1,0:T(8,128)(2,1)} %collective-permute-done.11.refs_16_.refs_5_), channel_id=1, source_target_pairs={{0,16},{16,0},{1,17},{17,1},{2,18},{18,2},{3,19},{19,3},{4,20},{20... | collective-permute-start | bytes 3932168 | tf_op jit(solution)/shard_map/ppermute | solution.py:24
  256.5 34.1 %collective-permute-start.23 = (bf16[1024,640]{1,0:T(8,128)(2,1)}, bf16[1024,640]{1,0:T(8,128)(2,1)}, u32[]{:S(2)}, u32[]{:S(2)}) collective-permute-start(bf16[1024,640]{1,0:T(8,128)(2,1)} %collective-permute-done.19.refs_23_), channel_id=1, source_target_pairs={{0,16},{16,0},{1,17},{17,1},{2,18},{18,2},{3,19},{19,3},{4,20},{20... | collective-permute-start | bytes 3932168 | tf_op jit(solution)/shard_map/ppermute | solution.py:24
  260.0 30.5 %collective-permute-start.24 = (bf16[1024,640]{1,0:T(8,128)(2,1)}, bf16[1024,640]{1,0:T(8,128)(2,1)}, u32[]{:S(2)}, u32[]{:S(2)}) collective-permute-start(bf16[1024,640]{1,0:T(8,128)(2,1)} %collective-permute-done.20.refs_24_), channel_id=1, source_target_pairs={{0,16},{16,0},{1,17},{17,1},{2,18},{18,2},{3,19},{19,3},{4,20},{20... | collective-permute-start | bytes 3932168 | tf_op jit(solution)/shard_map/ppermute | solution.py:24
  263.3 27.3 %collective-permute-start.6 = (bf16[4,16,8192]{2,1,0:T(8,128)(2,1)}, bf16[4,16,8192]{2,1,0:T(8,128)(2,1)}, u32[]{:S(2)}, u32[]{:S(2)}) collective-permute-start(bf16[4,16,8192]{2,1,0:T(8,128)(2,1)} %slice.50), channel_id=1, source_target_pairs={{0,4},{4,8},{8,12},{12,0},{1,5},{5,9},{9,13},{13,1},{2,6},{6,10},{... | collective-permute-start | bytes 3145736 | tf_op jit(solution)/shard_map/ppermute | solution.py:24
  265.8 20.5 %collective-permute-start.7 = (bf16[3,16,8192]{2,1,0:T(8,128)(2,1)}, bf16[3,16,8192]{2,1,0:T(8,128)(2,1)S(1)}, u32[]{:S(2)}, u32[]{:S(2)}) collective-permute-start(bf16[3,16,8192]{2,1,0:T(8,128)(2,1)} %slice.51), channel_id=1, source_target_pairs={{0,12},{4,0},{8,4},{12,8},{1,13},{5,1},{9,5},{13,9},{2,14},{6,2},{... | collective-permute-start | bytes 2359304 | tf_op jit(solution)/shard_map/ppermute | solution.py:24
  270.7 19.8 %copy-start.8 = (bf16[1024,640]{1,0:T(8,128)(2,1)}, bf16[1024,640]{1,0:T(8,128)(2,1)S(1)}, u32[]{:S(2)}) copy-start(bf16[1024,640]{1,0:T(8,128)(2,1)S(1)} %collective-permute-done.15.refs_20_.refs_9_) | copy-start | bytes 3932164
  310.9 20.1 %copy-start = (bf16[2,576,256]{2,1,0:T(8,128)(2,1)}, bf16[2,576,256]{2,1,0:T(8,128)(2,1)S(1)}, u32[]{:S(2)}) copy-start(bf16[2,576,256]{2,1,0:T(8,128)(2,1)S(1)} %get-tuple-element.22.refs_18_.kv_ref) | copy-start | bytes 1769476
  330.9 21.0 %collective-permute-start.35 = (bf16[576,768]{1,0:T(8,128)(2,1)}, bf16[576,768]{1,0:T(8,128)(2,1)S(1)}, u32[]{:S(2)}, u32[]{:S(2)}) collective-permute-start(bf16[576,768]{1,0:T(8,128)(2,1)} %get-tuple-element.23), channel_id=1, source_target_pairs={{0,3},{1,0},{2,1},{3,2},{4,7},{5,4},{6,5},{7,6},{8,11},{9,8},{10,9... | collective-permute-start | bytes 2654216 | tf_op jit(solution)/shard_map/ppermute | solution.py:24
  331.0 41.2 %collective-permute-start.37 = (bf16[576,768]{1,0:T(8,128)(2,1)}, bf16[576,768]{1,0:T(8,128)(2,1)S(1)}, u32[]{:S(2)}, u32[]{:S(2)}) collective-permute-start(bf16[576,768]{1,0:T(8,128)(2,1)} %get-tuple-element.21), channel_id=1, source_target_pairs={{0,1},{1,2},{2,3},{3,0},{4,5},{5,6},{6,7},{7,4},{8,9},{9,10},{10,1... | collective-permute-start | bytes 2654216 | tf_op jit(solution)/shard_map/ppermute | solution.py:24
  332.5 39.8 %collective-permute-start.36 = (bf16[576,768]{1,0:T(8,128)(2,1)}, bf16[576,768]{1,0:T(8,128)(2,1)S(1)}, u32[]{:S(2)}, u32[]{:S(2)}) collective-permute-start(bf16[576,768]{1,0:T(8,128)(2,1)} %get-tuple-element.24), channel_id=1, source_target_pairs={{0,2},{1,3},{2,0},{3,1},{4,6},{5,7},{6,4},{7,5},{8,10},{9,11},{10,... | collective-permute-start | bytes 2654216 | tf_op jit(solution)/shard_map/ppermute | solution.py:24
  (9 other events, 21.4 us)

commit v2 on v1

--- a/solution.py
+++ b/solution.py
@@ -34,19 +34,18 @@
     out_ref[...] = rms_norm(rows_ref[...], gain_ref[...])
 
 
-def norm_text(rows, gain):
-    count, features = rows.shape
+def norm_text(rows, gain, first, count):
+    features = rows.shape[1]
     step = 2 * UNIT
     return pl.pallas_call(
         norm_text_kernel,
         grid=(count // step,),
         in_specs=[
-            pl.BlockSpec((step, features), lambda i: (i, 0)),
+            pl.BlockSpec((step, features), lambda i: (first // step + i, 0)),
             pl.BlockSpec((1, features), lambda i: (0, 0)),
         ],
         out_specs=pl.BlockSpec((step, features), lambda i: (i, 0)),
-        out_shape=jax.ShapeDtypeStruct(rows.shape, jnp.bfloat16),
-        name="norm_text",
+        out_shape=jax.ShapeDtypeStruct((count, features), jnp.bfloat16),
     )(rows, gain)
 
 
@@ -73,24 +72,33 @@
     )(chosen, pieces, gain)
 
 
-def pick_kernel(chosen_ref, rows_ref, out_ref):
-    out_ref[...] = rows_ref[...]
-
-
-def pick_slots(pieces, chosen):
-    _, piece_rows, features = pieces.shape
+def spread_kernel(chosen_ref, pieces_ref, out_ref, sems):
+    def copy(index):
+        return pltpu.make_async_copy(
+            pieces_ref.at[chosen_ref[index]], out_ref.at[index], sems.at[index]
+        )
+
+    for index in range(out_ref.shape[0]):
+        copy(index).start()
+    for index in range(out_ref.shape[0]):
+        copy(index).wait()
+
+
+def spread(pieces, chosen):
     count = chosen.shape[0]
+    far_spec = pl.BlockSpec(memory_space=pltpu.HBM)
     return pl.pallas_call(
-        pick_kernel,
+        spread_kernel,
         grid_spec=pltpu.PrefetchScalarGridSpec(
             num_scalar_prefetch=1,
-            grid=(count,),
-            in_specs=[pl.BlockSpec((1, piece_rows, features), lambda i, chosen: (chosen[i], 0, 0))],
-            out_specs=pl.BlockSpec((1, piece_rows, features), lambda i, chosen: (i, 0, 0)),
+            grid=(1,),
+            in_specs=[far_spec],
+            out_specs=far_spec,
+            scratch_shapes=[pltpu.SemaphoreType.DMA((count,))],
         ),
-        out_shape=jax.ShapeDtypeStruct((count, piece_rows, features), jnp.bfloat16),
-        name="pick_slots",
-    )(chosen, pieces)
+        out_shape=pltpu.HBM((count,) + pieces.shape[1:], jnp.bfloat16),
+        name="spread",
+    )(chosen, *far([pieces]))
 
 
 def rotated(values, cosine, sine):
@@ -161,24 +169,21 @@
 
 def project_first_kernel(*refs):
     place_ref = refs[0]
-    t0, t1, t2a, t2b, t3, i0, i1, i2a, i2b, i3 = refs[1:11]
-    own_q, own_kv = refs[11:13]
-    pieces = {1: refs[13:21], 2: refs[21:29], 3: refs[29:37]}
-    kv_bias_ref, q_bias_ref, cos_ref, sin_ref, out_ref, kv_ref, compact_ref = refs[37:44]
-    rows_ref, weight_buf, sum_ref, sems, weight_sems, copy_sem = refs[44:]
+    sources = refs[1:17]
+    own_q, own_kv = refs[17:19]
+    pieces = {1: refs[19:27], 2: refs[27:35], 3: refs[35:43]}
+    kv_bias_ref, q_bias_ref, cos_ref, sin_ref, out_ref, kv_ref, compact_ref = refs[43:50]
+    rows_ref, weight_buf, sum_ref, sems, weight_sems, copy_sem = refs[50:]
     copies = weight_tile(own_q, own_kv, pieces, place_ref, weight_buf, weight_sems)
     width = q_bias_ref.shape[1]
     copy_out = pltpu.make_async_copy(rows_ref, compact_ref, copy_sem)
 
     def unit_copy(index):
-        delta, slot = index % 32 // 8, index % 8
+        slot = index % 4
+        source = sources[index // 4]
         if index < 32:
-            source = (t0, t1, t2a if slot < 4 else t2b, t3)[delta]
-            slot = slot % 4 if delta == 2 else slot
             source = source.at[pl.ds(UNIT * slot, UNIT), :]
         else:
-            source = (i0, i1, i2a if slot < 4 else i2b, i3)[delta]
-            slot = slot % 4 if delta == 2 else slot
             source = source.at[slot]
         row = pl.multiple_of(UNIT * jnp.maximum(place_ref[index], 0), UNIT)
         return pltpu.make_async_copy(source, rows_ref.at[pl.ds(row, UNIT), :], sems.at[index])
@@ -268,7 +273,7 @@
         grid_spec=pltpu.PrefetchScalarGridSpec(
             num_scalar_prefetch=1,
             grid=(1,),
-            in_specs=[far_spec] * (12 + len(flat))
+            in_specs=[far_spec] * (18 + len(flat))
             + [whole((1, width)), whole((1, width)), whole((ROWS, HD)), whole((ROWS, HD))],
             out_specs=(whole((ROWS, width + 2 * HD)), whole((2, ROWS, 2 * HD)), far_spec),
             scratch_shapes=[
@@ -473,18 +478,22 @@
         keys = merged_ref[window, 4 * HD:5 * HD]
         values = merged_ref[window, 5 * HD:6 * HD]
         factor = HD ** (-0.5) * math.log2(math.e)
+        heads = [merged_ref[queries, head * HD:(head + 1) * HD] for head in range(4)]
+        scores = lax.dot_general(
+            jnp.concatenate(heads, axis=0), keys, (((1,), (1,)), ((), ())),
+            preferred_element_type=jnp.float32,
+        )
+        scores = scores.reshape(4, block, span) + mask_ref[:, :span][None]
+        peak = jnp.max(scores, axis=-1, keepdims=True)
+        exponent = jnp.exp2((scores - peak) * factor)
+        inverse = 1.0 / jnp.sum(exponent, axis=-1, keepdims=True)
+        probs = (exponent * inverse).astype(jnp.bfloat16).reshape(4 * block, span)
+        mixed = jnp.dot(probs, values, preferred_element_type=jnp.float32)
         for head in range(4):
-            lanes = slice(head * HD, (head + 1) * HD)
-            scores = lax.dot_general(
-                merged_ref[queries, lanes], keys, (((1,), (1,)), ((), ())),
-                preferred_element_type=jnp.float32,
-            ) + mask_ref[:, :span]
-            peak = jnp.max(scores, axis=-1, keepdims=True)
-            exponent = jnp.exp2((scores - peak) * factor)
-            inverse = 1.0 / jnp.sum(exponent, axis=-1, keepdims=True)
-            probs = (exponent * inverse).astype(jnp.bfloat16)
-            mixed = jnp.dot(probs, values, preferred_element_type=jnp.float32)
-            out_ref[:, lanes] = jnp.where(position < used, mixed, 0.0).astype(jnp.bfloat16)
+            rows = mixed[head * block:(head + 1) * block]
+            out_ref[:, head * HD:(head + 1) * HD] = jnp.where(position < used, rows, 0.0).astype(
+                jnp.bfloat16
+            )
 
     for extra in (1, 2, 3, 4):
         within = reach <= 1 if extra == 1 else reach == extra
@@ -579,12 +588,19 @@
     y = lax.axis_index("y")
     gain = norm_gain.reshape(1, -1)
 
-    t0 = norm_text(text_rows, gain)
-    t3 = shifted(t0, "z", 1)
-    t1 = shifted(t0, "z", -1)
+    row_groups = lax.dynamic_slice_in_dim(tile_group, group * 4, 4)
+    matches = row_groups[None, :] == jnp.arange(8, dtype=jnp.int32)[:, None]
+    chosen = jnp.sum(jnp.where(matches, jnp.arange(4, dtype=jnp.int32)[None, :], 0), axis=1)
+    outgoing = spread(image_rows, chosen.astype(jnp.int32))
+    arrived = lax.all_to_all(outgoing, ("x", "c"), split_axis=0, concat_axis=0, tiled=True)
+
+    outgoing, text_rows = lax.optimization_barrier((outgoing, text_rows))
+    t_low = norm_text(text_rows, gain, 0, 64)
+    t3_low = shifted(t_low, "z", 1)
+    t1_low = shifted(t_low, "z", -1)
 
     quarter = 2 * core + x % 2
-    begin, t0 = lax.optimization_barrier((quarter * 2 * PIECE, t0))
+    begin, t_low = lax.optimization_barrier((quarter * 2 * PIECE, t_low))
     own_kv = jnp.concatenate([k_weight, v_weight], axis=1)
 
     def own_part(half):
@@ -603,6 +619,14 @@
     direct[3, 1] = shifted(high, "y", 1)
     direct[1, 1] = shifted(high, "y", -1)
     direct[3, 0] = shifted(low, "y", 1)
+
+    low, high, text_rows = lax.optimization_barrier((low, high, text_rows))
+    t_high = norm_text(text_rows, gain, 64, 64)
+    t3_high = shifted(t_high, "z", 1)
+    t1_high = shifted(t_high, "z", -1)
+    t2_low = shifted(t3_low, "z", 1)
+    t2_high = shifted(t1_high, "z", -1)
+
     direct[2, 0] = shifted(direct[1, 0], "y", -1)
     direct[2, 1] = shifted(direct[3, 1], "y", 1)
     across = {key: shifted(value, "x", -1 if key[1] else 1) for key, value in direct.items()}
@@ -619,22 +643,21 @@
     place, slots, text_index, info, in_doc = tables(
         tile_group, tile_offset, seq_len, doc_ids, group, z, y, quarters
     )
-    row_groups = lax.dynamic_slice_in_dim(tile_group, group * 4, 4)
-    matches = row_groups[None, :] == jnp.arange(8, dtype=jnp.int32)[:, None]
-    chosen = jnp.sum(jnp.where(matches, jnp.arange(4, dtype=jnp.int32)[None, :], 0), axis=1)
-    image_rows, t0 = lax.optimization_barrier((image_rows, t0))
-    outgoing = norm_image(image_rows, gain, chosen.astype(jnp.int32))
-    arrived = lax.all_to_all(outgoing, ("x", "c"), split_axis=0, concat_axis=0, tiled=True)
-    i0 = pick_slots(arrived, slots)
-    i3 = shifted(i0, "z", 1)
-    i1 = shifted(i0, "z", -1)
-    t2a = shifted(t3[:64], "z", 1)
-    t2b = shifted(t1[64:], "z", -1)
-    i2a = shifted(i3[:4], "z", 1)
-    i2b = shifted(i1[4:], "z", -1)
+    i_low = norm_image(arrived, gain, slots[:4])
+    i_high = norm_image(arrived, gain, slots[4:])
+    i3_low = shifted(i_low, "z", 1)
+    i1_low = shifted(i_low, "z", -1)
+    i3_high = shifted(i_high, "z", 1)
+    i1_high = shifted(i_high, "z", -1)
+    i2_low = shifted(i3_low, "z", 1)
+    i2_high = shifted(i1_high, "z", -1)
 
     bias = jnp.concatenate([q_bias, k_bias, v_bias])
-    biases = [bias, shifted(bias, "y", -1), shifted(bias, "y", 2), shifted(bias, "y", 1)]
+    bias, i_high = lax.optimization_barrier((bias, i_high))
+    biases = [
+        bias, shifted(bias, "y", -1), shifted(bias, "y", 2),
+        shifted(bias, "y", 1),
+    ]
     q_biases = [value[None, :4 * HD] for value in biases]
     kv_bias = jnp.concatenate([value[None, 4 * HD:] for value in biases], axis=1)
     frequency = THETA ** (-(jnp.arange(HD // 2, dtype=jnp.float32) * 2.0) / HD)
@@ -642,9 +665,10 @@
     cosine = jnp.concatenate([jnp.cos(angles), jnp.cos(angles)], axis=-1)
     sine = jnp.concatenate([-jnp.sin(angles), jnp.sin(angles)], axis=-1)
 
+    texts = (t_low, t_high, t1_low, t1_high, t2_low, t2_high, t3_low, t3_high)
+    images = (i_low, i_high, i1_low, i1_high, i2_low, i2_high, i3_low, i3_high)
     out2, kv, compact = project_first(
-        place, (t0, t1, t2a, t2b, t3), (i0, i1, i2a, i2b, i3), (q_weight, own_kv),
-        pieces, kv_bias, q_biases[2], cosine, sine,
+        place, texts, images, (q_weight, own_kv), pieces, kv_bias, q_biases[2], cosine, sine
     )
     part2 = shifted(out2, "y", 2)
     out1, out3 = project_near(place, compact, pieces, kv, q_biases[1], q_biases[3], cosine, sine)

time: 398 us -> 407 us (1.023)
  Pallas kernels: 92.4 us -> 147 us
  waiting for transfers between devices: 207 us -> 154 us
  starting transfers between devices: 60.3 us -> 71.8 us
  local copies, waits for them, and re-layouts: 19.6 us -> 11.4 us
  other arithmetic: 13.3 us -> 18.2 us
    pallas_call x1, Pallas kernels: 4.96 us -> 65.4 us  [spread(): pl.pallas_call(spread_kernel, grid_spec=pltpu.PrefetchScalarGridSpec(num_...]
    ppermute x38 -> x42, waiting for transfers between devices: 190 us -> 154 us  [shifted(): lax.ppermute(block, axis, [(low, (low + step) % count) for low in range(c...]
    all_to_all x1, waiting for transfers between devices: 16.5 us -> 0.01 us  [one_device(): lax.all_to_all(outgoing, ('x', 'c'), split_axis=0, concat_axis=0, tiled=T...]
    ppermute x38 -> x42, starting transfers between devices: 55.6 us -> 66.4 us  [shifted(): lax.ppermute(block, axis, [(low, (low + step) % count) for low in range(c...]
    slice x4 -> x1, local copies, waits for them, and re-layouts: 8.92 us -> 0.58 us  [one_device(): i_high = norm_image(arrived, gain, slots[4:])]
    pallas_call x1, Pallas kernels: 24.4 us -> 16.4 us  [attend(): pl.pallas_call(attend_kernel, grid_spec=pltpu.PrefetchScalarGridSpec(num_...]
    pallas_call x1 -> x2, Pallas kernels: 6.77 us -> 8.24 us  [norm_image(): pl.pallas_call(norm_image_kernel, grid_spec=pltpu.PrefetchScalarGridSpec(...]
  transfers between devices with their start and end apart: 39 -> 43, of which waited for: 13 -> 18; matrix products, arithmetic and copies ran while one was open for 6% -> 6% of each run, Pallas kernels for 6% -> 5%
where the time goes in v2:
time: 407 us; the launch traced here: 406 us
  waiting for transfers between devices  154 us (38%)
  Pallas kernels  147 us (36%)
  starting transfers between devices  71.8 us (18%)
  other arithmetic  18.2 us (4%)
  local copies, waits for them, and re-layouts  11.4 us (3%)
  between operations  4.36 us (1%)
    ppermute x42, waiting for transfers between devices, shifted(): lax.ppermute(block, axis, [(low, (low + step) % count) for low in range(c...  154 us
    ppermute x42, starting transfers between devices, shifted(): lax.ppermute(block, axis, [(low, (low + step) % count) for low in range(c...  66.4 us
    pallas_call x1, Pallas kernels, spread(): pl.pallas_call(spread_kernel, grid_spec=pltpu.PrefetchScalarGridSpec(num_...  65.4 us
    pallas_call x1, Pallas kernels, project_first(): pl.pallas_call(project_first_kernel, grid_spec=pltpu.PrefetchScalarGridSp...  20.1 us
    pallas_call x1, Pallas kernels, project_near(): pl.pallas_call(project_near_kernel, grid_spec=pltpu.PrefetchScalarGridSpe...  19.9 us
    pallas_call x1, Pallas kernels, attend(): pl.pallas_call(attend_kernel, grid_spec=pltpu.PrefetchScalarGridSpec(num_...  16.4 us
    pallas_call x1, Pallas kernels, project_own(): pl.pallas_call(project_own_kernel, grid_spec=pltpu.PrefetchScalarGridSpec...  11.5 us
    pallas_call x2, Pallas kernels, norm_image(): pl.pallas_call(norm_image_kernel, grid_spec=pltpu.PrefetchScalarGridSpec(...  8.24 us
  transfers between devices with their start and end apart: 43, of which 18 were waited for; matrix products, arithmetic and copies ran while one was open for 6% of the time, Pallas kernels for 5%

profile of v2, /device:TPU:1, one launch (start us, length us, event | category | flops | bytes accessed | tf_op | source)
XLA Modules:
  0.0 406.3 jit_solution(12221258076917549378)
XLA Ops:
  1.4 65.4 %spread.1 = bf16[8,16,8192]{2,1,0:T(8,128)(2,1)} custom-call(s32[8]{0:T(128)} %select_reduce_fusion.2.chosen_ref, bf16[4,16,8192]{2,1,0:T(8,128)(2,1)} %pieces_ref.1), custom_call_target="tpu_custom_call" | custom-call | tf_op jit(solution)/shard_map/spread/pallas_call | solution.py:90
  66.8 2.6 shard_map.127.refs_1_
  69.4 2.5 collective-permute-start.2
  71.9 2.1 collective-permute-start
  75.1 2.7 copy.19
  77.8 1.5 fusion.1
  79.3 2.0 constant_dynamic-slice_fusion
  83.7 2.5 shard_map.128.refs_2_
  86.4 5.4 %all-to-all-start = ((bf16[8,16,8192]{2,1,0:T(8,128)(2,1)}), bf16[8,16,8192]{2,1,0:T(8,128)(2,1)}, u32[]{:S(2)}, u32[]{:S(2)}) async-start(bf16[8,16,8192]{2,1,0:T(8,128)(2,1)} %spread.1), calls=%async_computation | async-start | bytes 4194304 | tf_op jit(solution)/shard_map/all_to_all | solution.py:595
  91.7 1.3 collective-permute-start.29
  93.0 2.8 collective-permute-start.1
  95.8 1.3 collective-permute-done.2.refs_7_
  97.2 2.7 collective-permute-start.12
  99.9 19.7 %collective-permute-done.5.refs_8_ = bf16[64,8192]{1,0:T(8,128)(2,1)} collective-permute-done((bf16[64,8192]{1,0:T(8,128)(2,1)}, bf16[64,8192]{1,0:T(8,128)(2,1)}, u32[]{:S(2)}, u32[]{:S(2)}) %collective-permute-start.5) | collective-permute-done | bytes 1048608 | tf_op jit(solution)/shard_map/ppermute | solution.py:24
  119.6 2.7 collective-permute-start.13
  123.6 2.8 collective-permute-start.4
  128.2 3.6 norm_image.3.refs_10_
  131.9 19.7 %collective-permute-done.21.refs_36_.refs_11_ = bf16[1024,640]{1,0:T(8,128)(2,1)} collective-permute-done((bf16[1024,640]{1,0:T(8,128)(2,1)}, bf16[1024,640]{1,0:T(8,128)(2,1)}, u32[]{:S(2)}, u32[]{:S(2)}) %collective-permute-start.21) | collective-permute-done | bytes 1310752 | tf_op jit(solution)/shard_map/ppermute | solution.py:24
  152.7 1.6 collective-permute-done.13.refs_20_.refs_3_
  155.1 3.9 collective-permute-done.38
  159.7 3.3 collective-permute-done.37
  163.0 1.5 collective-permute-start.36
  164.5 1.3 collective-permute-done.36
  167.0 2.4 collective-permute-start.20
  170.1 7.4 %collective-permute-start.16 = (bf16[1024,640]{1,0:T(8,128)(2,1)}, bf16[1024,640]{1,0:T(8,128)(2,1)}, u32[]{:S(2)}, u32[]{:S(2)}) collective-permute-start(bf16[1024,640]{1,0:T(8,128)(2,1)} %collective-permute-done.12.refs_19_.refs_2_), channel_id=1, source_target_pairs={{0,16},{16,0},{1,17},{17,1},{2,18},{18,2},{3,19},{19,3},{4,20},{20... | collective-permute-start | bytes 3932168 | tf_op jit(solution)/shard_map/ppermute | solution.py:24
  177.5 4.5 %collective-permute-done.7.refs_12_ = bf16[3,16,8192]{2,1,0:T(8,128)(2,1)S(1)} collective-permute-done((bf16[3,16,8192]{2,1,0:T(8,128)(2,1)}, bf16[3,16,8192]{2,1,0:T(8,128)(2,1)S(1)}, u32[]{:S(2)}, u32[]{:S(2)}) %collective-permute-start.7) | collective-permute-done | bytes 786464 | tf_op jit(solution)/shard_map/ppermute | solution.py:24
  183.3 7.8 %collective-permute-start.33 = (bf16[1024,640]{1,0:T(8,128)(2,1)}, bf16[1024,640]{1,0:T(8,128)(2,1)}, u32[]{:S(2)}, u32[]{:S(2)}) collective-permute-start(bf16[1024,640]{1,0:T(8,128)(2,1)} %collective-permute-done.21.refs_36_.refs_11_), channel_id=1, source_target_pairs={{0,16},{16,0},{1,17},{17,1},{2,18},{18,2},{3,19},{19,3},{4,20},{20... | collective-permute-start | bytes 3932168 | tf_op jit(solution)/shard_map/ppermute | solution.py:24
  193.3 4.6 %norm_image.2.refs_9_ = bf16[4,16,8192]{2,1,0:T(8,128)(2,1)} custom-call(s32[4]{0:T(128)} %bitcast.37, bf16[8,16,8192]{2,1,0:T(8,128)(2,1)} %all-to-all-done.rows_ref, f32[1,8192]{1,0:T(1,128)} %bitcast.35), custom_call_target="tpu_custom_call" | custom-call | tf_op jit(solution)/shard_map/norm_image/pallas_call | solution.py:59
  201.2 19.0 %collective-permute-done.14.refs_21_.refs_4_ = bf16[1024,640]{1,0:T(8,128)(2,1)} collective-permute-done((bf16[1024,640]{1,0:T(8,128)(2,1)}, bf16[1024,640]{1,0:T(8,128)(2,1)}, u32[]{:S(2)}, u32[]{:S(2)}) %collective-permute-start.14) | collective-permute-done | bytes 1310752 | tf_op jit(solution)/shard_map/ppermute | solution.py:24
  220.1 6.4 %collective-permute-start.17 = (bf16[1024,640]{1,0:T(8,128)(2,1)}, bf16[1024,640]{1,0:T(8,128)(2,1)}, u32[]{:S(2)}, u32[]{:S(2)}) collective-permute-start(bf16[1024,640]{1,0:T(8,128)(2,1)} %collective-permute-done.13.refs_20_.refs_3_), channel_id=1, source_target_pairs={{0,16},{16,0},{1,17},{17,1},{2,18},{18,2},{3,19},{19,3},{4,20},{20... | collective-permute-start | bytes 3932168 | tf_op jit(solution)/shard_map/ppermute | solution.py:24
  226.6 1.3 collective-permute-start.15
  228.1 1.3 collective-permute-start.9
  232.5 1.5 collective-permute-start.10
  237.4 19.8 %collective-permute-done.15.refs_22_.refs_5_ = bf16[1024,640]{1,0:T(8,128)(2,1)} collective-permute-done((bf16[1024,640]{1,0:T(8,128)(2,1)}, bf16[1024,640]{1,0:T(8,128)(2,1)}, u32[]{:S(2)}, u32[]{:S(2)}) %collective-permute-start.15) | collective-permute-done | bytes 1310752 | tf_op jit(solution)/shard_map/ppermute | solution.py:24
  258.4 11.2 %collective-permute-done.10.refs_14_ = bf16[3,16,8192]{2,1,0:T(8,128)(2,1)S(1)} collective-permute-done((bf16[3,16,8192]{2,1,0:T(8,128)(2,1)}, bf16[3,16,8192]{2,1,0:T(8,128)(2,1)S(1)}, u32[]{:S(2)}, u32[]{:S(2)}) %collective-permute-start.10) | collective-permute-done | bytes 786464 | tf_op jit(solution)/shard_map/ppermute | solution.py:24
  272.7 2.0 fusion.2
  274.7 4.1 pad_maximum_fusion.refs_18_
  280.0 8.2 %collective-permute-done.23.refs_29_ = bf16[1024,640]{1,0:T(8,128)(2,1)} collective-permute-done((bf16[1024,640]{1,0:T(8,128)(2,1)}, bf16[1024,640]{1,0:T(8,128)(2,1)}, u32[]{:S(2)}, u32[]{:S(2)}) %collective-permute-start.23) | collective-permute-done | bytes 1310752 | tf_op jit(solution)/shard_map/ppermute | solution.py:24
  288.2 1.7 collective-permute-start.19
  289.9 10.2 %collective-permute-done.24.refs_30_ = bf16[1024,640]{1,0:T(8,128)(2,1)} collective-permute-done((bf16[1024,640]{1,0:T(8,128)(2,1)S(1)}, bf16[1024,640]{1,0:T(8,128)(2,1)}, u32[]{:S(2)}, u32[]{:S(2)}) %collective-permute-start.24) | collective-permute-done | bytes 1310752 | tf_op jit(solution)/shard_map/ppermute | solution.py:24
  300.1 1.7 collective-permute-start.28
  305.6 20.1 %project_first.1 = (bf16[576,768]{1,0:T(8,128)(2,1)}, bf16[2,576,256]{2,1,0:T(8,128)(2,1)S(1)}, bf16[576,8192]{1,0:T(8,128)(2,1)}) custom-call(s32[70]{0:T(128)S(1)} %concatenate.28.refs_0_.place_ref, bf16[64,8192]{1,0:T(8,128)(2,1)} %shard_map.127.refs_1_, bf16[64,8192]{1,0:T(8,128)(2,1)} %shard_map.128.refs_2_, ...), custom_call_target="tpu_custom_call" | custom-call | flops 9663676416 | bytes 26214400 | tf_op jit(solution)/shard_map/project_first/pallas_call | solution.py:271
  325.7 19.9 %project_near.1 = (bf16[576,768]{1,0:T(8,128)(2,1)}, bf16[576,768]{1,0:T(8,128)(2,1)}) custom-call(s32[70]{0:T(128)S(1)} %concatenate.28.refs_0_.place_ref, bf16[576,8192]{1,0:T(8,128)(2,1)} %get-tuple-element.23.refs_1_.compact_ref, bf16[1024,640]{1,0:T(8,128)(2,1)} %collective-permute-done.12.refs_19_.refs_2_, ...), custom_call_target="tpu_custom_call" | custom-call | flops 9663676416 | bytes 26214400 | tf_op jit(solution)/shard_map/project_near/pallas_call | solution.py:326
  345.6 2.6 collective-permute-start.39
  350.8 11.5 %project_own.1.part0 = bf16[576,768]{1,0:T(8,128)(2,1)S(1)} custom-call(s32[70]{0:T(128)S(1)} %concatenate.28.refs_0_.place_ref, bf16[576,8192]{1,0:T(8,128)(2,1)} %get-tuple-element.23.refs_1_.compact_ref, bf16[8192,512]{1,0:T(8,128)(2,1)} %own_q.1, bf16[2,576,256]{2,1,0:T(8,128)(2,1)S(1)} %copy-done.1, f32[1,512]{1,0:T(1,128)S(1)} %bitcast.29, ...), custom_call_target="tpu_custom_call" | custom-call | flops 4831838208 | bytes 17825792 | tf_op jit(solution)/shard_map/project_own/pallas_call | solution.py:373
  362.3 24.3 %collective-permute-done.39.part1 = bf16[576,768]{1,0:T(8,128)(2,1)S(1)} collective-permute-done((bf16[576,768]{1,0:T(8,128)(2,1)}, bf16[576,768]{1,0:T(8,128)(2,1)S(1)}, u32[]{:S(2)}, u32[]{:S(2)}) %collective-permute-start.39) | collective-permute-done | bytes 884768 | tf_op jit(solution)/shard_map/ppermute | solution.py:24
  386.6 3.2 collective-permute-done.41.part3
  389.8 16.4 %attend.1 = bf16[2048,512]{1,0:T(8,128)(2,1)} custom-call(s32[12]{0:T(128)S(1)} %concatenate.27.info_ref, s32[128]{0:T(128)S(1)} %reshape.320.text_ref, bf16[576,768]{1,0:T(8,128)(2,1)S(1)} %project_own.1.part0, bf16[576,768]{1,0:T(8,128)(2,1)S(1)} %collective-permute-done.39.part1, bf16[576,768]{1,0:T(8,128)(2,1)S(1)} %collective-permute-done.40.part2, ...), custom_call_target="tpu_custom_call" | custom-call | tf_op jit(solution)/shard_map/attend/pallas_call | solution.py:514
  (142 shorter events, 33.7 us)
Async XLA Ops:
  69.4 27.8 %collective-permute-start.2 = (bf16[64,8192]{1,0:T(8,128)(2,1)}, bf16[64,8192]{1,0:T(8,128)(2,1)}, u32[]{:S(2)}, u32[]{:S(2)}) collective-permute-start(bf16[64,8192]{1,0:T(8,128)(2,1)} %shard_map.127.refs_1_), channel_id=1, source_target_pairs={{0,4},{4,8},{8,12},{12,0},{1,5},{5,9},{9,13},{13,1},{2,6},{6,10},{... | collective-permute-start | bytes 3145736 | tf_op jit(solution)/shard_map/ppermute | solution.py:24
  71.9 28.0 %collective-permute-start = (bf16[64,8192]{1,0:T(8,128)(2,1)}, bf16[64,8192]{1,0:T(8,128)(2,1)}, u32[]{:S(2)}, u32[]{:S(2)}) collective-permute-start(bf16[64,8192]{1,0:T(8,128)(2,1)} %shard_map.127.refs_1_), channel_id=1, source_target_pairs={{0,12},{4,0},{8,4},{12,8},{1,13},{5,1},{9,5},{13,9},{2,14},{6,2},{... | collective-permute-start | bytes 3145736 | tf_op jit(solution)/shard_map/ppermute | solution.py:24
  86.3 40.1 %copy-start.15 = (s32[32]{0:T(128)S(1)}, s32[32]{0:T(128)}, u32[]{:S(2)}) copy-start(s32[32]{0:T(128)} %param.16) | copy-start | bytes 388
  86.3 40.1 %copy-start.16 = (s32[32]{0:T(128)S(1)}, s32[32]{0:T(128)}, u32[]{:S(2)}) copy-start(s32[32]{0:T(128)} %param.15) | copy-start | bytes 388
  86.3 33.4 %collective-permute-start.5 = (bf16[64,8192]{1,0:T(8,128)(2,1)}, bf16[64,8192]{1,0:T(8,128)(2,1)}, u32[]{:S(2)}, u32[]{:S(2)}) collective-permute-start(bf16[64,8192]{1,0:T(8,128)(2,1)} %shard_map.128.refs_2_), channel_id=1, source_target_pairs={{0,4},{4,8},{8,12},{12,0},{1,5},{5,9},{9,13},{13,1},{2,6},{6,10},{... | collective-permute-start | bytes 3145736 | tf_op jit(solution)/shard_map/ppermute | solution.py:24
  86.4 41.9 %all-to-all-start = ((bf16[8,16,8192]{2,1,0:T(8,128)(2,1)}), bf16[8,16,8192]{2,1,0:T(8,128)(2,1)}, u32[]{:S(2)}, u32[]{:S(2)}) async-start(bf16[8,16,8192]{2,1,0:T(8,128)(2,1)} %spread.1), calls=%async_computation | async-start | bytes 4194304 | tf_op jit(solution)/shard_map/all_to_all | solution.py:595
  91.7 31.8 %collective-permute-start.29 = (bf16[1024,640]{1,0:T(8,128)(2,1)}, bf16[1024,640]{1,0:T(8,128)(2,1)}, u32[]{:S(2)}, u32[]{:S(2)}) collective-permute-start(bf16[1024,640]{1,0:T(8,128)(2,1)} %pad_maximum_fusion.1), channel_id=1, source_target_pairs={{0,1},{1,2},{2,3},{3,0},{4,5},{5,6},{6,7},{7,4},{8,9},{9,10},{10,1... | collective-permute-start | bytes 3932168 | tf_op jit(solution)/shard_map/ppermute | solution.py:24
  93.0 29.3 %collective-permute-start.1 = (bf16[64,8192]{1,0:T(8,128)(2,1)S(1)}, bf16[64,8192]{1,0:T(8,128)(2,1)}, u32[]{:S(2)}, u32[]{:S(2)}) collective-permute-start(bf16[64,8192]{1,0:T(8,128)(2,1)S(1)} %copy-done.2), channel_id=1, source_target_pairs={{0,12},{4,0},{8,4},{12,8},{1,13},{5,1},{9,5},{13,9},{2,14},{6,2},{... | collective-permute-start | bytes 3145736 | tf_op jit(solution)/shard_map/ppermute | solution.py:24
  97.2 34.7 %collective-permute-start.12 = (bf16[1024,640]{1,0:T(8,128)(2,1)}, bf16[1024,640]{1,0:T(8,128)(2,1)}, u32[]{:S(2)}, u32[]{:S(2)}) collective-permute-start(bf16[1024,640]{1,0:T(8,128)(2,1)} %pad_maximum_fusion.1), channel_id=1, source_target_pairs={{0,3},{1,0},{2,1},{3,2},{4,7},{5,4},{6,5},{7,6},{8,11},{9,8},{10,9... | collective-permute-start | bytes 3932168 | tf_op jit(solution)/shard_map/ppermute | solution.py:24
  99.9 51.8 %collective-permute-start.21 = (bf16[1024,640]{1,0:T(8,128)(2,1)}, bf16[1024,640]{1,0:T(8,128)(2,1)}, u32[]{:S(2)}, u32[]{:S(2)}) collective-permute-start(bf16[1024,640]{1,0:T(8,128)(2,1)} %pad_maximum_fusion.2), channel_id=1, source_target_pairs={{0,1},{1,2},{2,3},{3,0},{4,5},{5,6},{6,7},{7,4},{8,9},{9,10},{10,1... | collective-permute-start | bytes 3932168 | tf_op jit(solution)/shard_map/ppermute | solution.py:24
  119.6 34.7 %collective-permute-start.13 = (bf16[1024,640]{1,0:T(8,128)(2,1)}, bf16[1024,640]{1,0:T(8,128)(2,1)}, u32[]{:S(2)}, u32[]{:S(2)}) collective-permute-start(bf16[1024,640]{1,0:T(8,128)(2,1)} %pad_maximum_fusion.2), channel_id=1, source_target_pairs={{0,3},{1,0},{2,1},{3,2},{4,7},{5,4},{6,5},{7,6},{8,11},{9,8},{10,9... | collective-permute-start | bytes 3932168 | tf_op jit(solution)/shard_map/ppermute | solution.py:24
  122.4 44.6 %collective-permute-start.3 = (bf16[64,8192]{1,0:T(8,128)(2,1)}, bf16[64,8192]{1,0:T(8,128)(2,1)}, u32[]{:S(2)}, u32[]{:S(2)}) collective-permute-start(bf16[64,8192]{1,0:T(8,128)(2,1)} %collective-permute-done.2.refs_7_), channel_id=1, source_target_pairs={{0,4},{4,8},{8,12},{12,0},{1,5},{5,9},{9,13},{13,1},{2,6},{6,10},{... | collective-permute-start | bytes 3145736 | tf_op jit(solution)/shard_map/ppermute | solution.py:24
  123.6 45.7 %collective-permute-start.4 = (bf16[64,8192]{1,0:T(8,128)(2,1)}, bf16[64,8192]{1,0:T(8,128)(2,1)}, u32[]{:S(2)}, u32[]{:S(2)}) collective-permute-start(bf16[64,8192]{1,0:T(8,128)(2,1)} %collective-permute-done.1.refs_4_), channel_id=1, source_target_pairs={{0,12},{4,0},{8,4},{12,8},{1,13},{5,1},{9,5},{13,9},{2,14},{6,2},{... | collective-permute-start | bytes 3145736 | tf_op jit(solution)/shard_map/ppermute | solution.py:24
  128.2 24.4 %copy-start.14 = (f32[64]{0:T(128)S(1)}, f32[64]{0:T(128)}, u32[]{:S(2)}) copy-start(f32[64]{0:T(128)} %param.24) | copy-start | bytes 772
  131.9 38.2 %collective-permute-start.11 = (bf16[3,16,8192]{2,1,0:T(8,128)(2,1)}, bf16[3,16,8192]{2,1,0:T(8,128)(2,1)S(1)}, u32[]{:S(2)}, u32[]{:S(2)}) collective-permute-start(bf16[3,16,8192]{2,1,0:T(8,128)(2,1)} %norm_image.3.refs_10_), channel_id=1, source_target_pairs={{0,4},{4,8},{8,12},{12,0},{1,5},{5,9},{9,13},{13,1},{2,6},{6,10},{... | collective-permute-start | bytes 2359304 | tf_op jit(solution)/shard_map/ppermute | solution.py:24
  151.7 31.6 %collective-permute-start.32 = (bf16[1024,640]{1,0:T(8,128)(2,1)}, bf16[1024,640]{1,0:T(8,128)(2,1)S(1)}, u32[]{:S(2)}, u32[]{:S(2)}) collective-permute-start(bf16[1024,640]{1,0:T(8,128)(2,1)} %collective-permute-done.29.refs_35_.refs_10_), channel_id=1, source_target_pairs={{0,16},{16,0},{1,17},{17,1},{2,18},{18,2},{3,19},{19,3},{4,20},{20... | collective-permute-start | bytes 3932168 | tf_op jit(solution)/shard_map/ppermute | solution.py:24
  154.3 4.7 %collective-permute-start.38 = (f32[640]{0:T(1024)S(1)}, f32[640]{0:T(1024)S(1)}, u32[]{:S(2)}, u32[]{:S(2)}) collective-permute-start(f32[640]{0:T(1024)S(1)} %pad_maximum_fusion.5), channel_id=1, source_target_pairs={{0,1},{1,2},{2,3},{3,0},{4,5},{5,6},{6,7},{7,4},{8,9},{9,10},{10,1... | collective-permute-start | bytes 7688 | tf_op jit(solution)/shard_map/ppermute | solution.py:24
  159.0 4.0 collective-permute-start.37
  163.0 2.8 collective-permute-start.36
  165.7 26.3 %collective-permute-start.30 = (bf16[1024,640]{1,0:T(8,128)(2,1)}, bf16[1024,640]{1,0:T(8,128)(2,1)}, u32[]{:S(2)}, u32[]{:S(2)}) collective-permute-start(bf16[1024,640]{1,0:T(8,128)(2,1)} %collective-permute-done.29.refs_35_.refs_10_), channel_id=1, source_target_pairs={{0,32},{32,64},{64,96},{96,0},{1,33},{33,65},{65,97},{97,1},{2,34}... | collective-permute-start | bytes 3932168 | tf_op jit(solution)/shard_map/ppermute | solution.py:24
  167.0 31.0 %collective-permute-start.20 = (bf16[1024,640]{1,0:T(8,128)(2,1)}, bf16[1024,640]{1,0:T(8,128)(2,1)}, u32[]{:S(2)}, u32[]{:S(2)}) collective-permute-start(bf16[1024,640]{1,0:T(8,128)(2,1)} %collective-permute-done.12.refs_19_.refs_2_), channel_id=1, source_target_pairs={{0,3},{1,0},{2,1},{3,2},{4,7},{5,4},{6,5},{7,6},{8,11},{9,8},{10,9... | collective-permute-start | bytes 3932168 | tf_op jit(solution)/shard_map/ppermute | solution.py:24
  169.3 12.7 %collective-permute-start.7 = (bf16[3,16,8192]{2,1,0:T(8,128)(2,1)}, bf16[3,16,8192]{2,1,0:T(8,128)(2,1)S(1)}, u32[]{:S(2)}, u32[]{:S(2)}) collective-permute-start(bf16[3,16,8192]{2,1,0:T(8,128)(2,1)} %norm_image.3.refs_10_), channel_id=1, source_target_pairs={{0,12},{4,0},{8,4},{12,8},{1,13},{5,1},{9,5},{13,9},{2,14},{6,2},{... | collective-permute-start | bytes 2359304 | tf_op jit(solution)/shard_map/ppermute | solution.py:24
  170.1 28.1 %collective-permute-start.16 = (bf16[1024,640]{1,0:T(8,128)(2,1)}, bf16[1024,640]{1,0:T(8,128)(2,1)}, u32[]{:S(2)}, u32[]{:S(2)}) collective-permute-start(bf16[1024,640]{1,0:T(8,128)(2,1)} %collective-permute-done.12.refs_19_.refs_2_), channel_id=1, source_target_pairs={{0,16},{16,0},{1,17},{17,1},{2,18},{18,2},{3,19},{19,3},{4,20},{20... | collective-permute-start | bytes 3932168 | tf_op jit(solution)/shard_map/ppermute | solution.py:24
  182.0 38.1 %collective-permute-start.14 = (bf16[1024,640]{1,0:T(8,128)(2,1)}, bf16[1024,640]{1,0:T(8,128)(2,1)}, u32[]{:S(2)}, u32[]{:S(2)}) collective-permute-start(bf16[1024,640]{1,0:T(8,128)(2,1)} %collective-permute-done.12.refs_19_.refs_2_), channel_id=1, source_target_pairs={{0,32},{32,64},{64,96},{96,0},{1,33},{33,65},{65,97},{97,1},{2,34}... | collective-permute-start | bytes 3932168 | tf_op jit(solution)/shard_map/ppermute | solution.py:24
  183.3 43.3 %collective-permute-start.33 = (bf16[1024,640]{1,0:T(8,128)(2,1)}, bf16[1024,640]{1,0:T(8,128)(2,1)}, u32[]{:S(2)}, u32[]{:S(2)}) collective-permute-start(bf16[1024,640]{1,0:T(8,128)(2,1)} %collective-permute-done.21.refs_36_.refs_11_), channel_id=1, source_target_pairs={{0,16},{16,0},{1,17},{17,1},{2,18},{18,2},{3,19},{19,3},{4,20},{20... | collective-permute-start | bytes 3932168 | tf_op jit(solution)/shard_map/ppermute | solution.py:24
  192.0 35.9 %collective-permute-start.31 = (bf16[1024,640]{1,0:T(8,128)(2,1)}, bf16[1024,640]{1,0:T(8,128)(2,1)}, u32[]{:S(2)}, u32[]{:S(2)}) collective-permute-start(bf16[1024,640]{1,0:T(8,128)(2,1)} %collective-permute-done.21.refs_36_.refs_11_), channel_id=1, source_target_pairs={{0,96},{32,0},{64,32},{96,64},{1,97},{33,1},{65,33},{97,65},{2,98}... | collective-permute-start | bytes 3932168 | tf_op jit(solution)/shard_map/ppermute | solution.py:24
  193.3 41.4 %copy-start.10 = (s32[1,2048]{1,0:T(1,128)S(1)}, s32[1,2048]{1,0:T(1,128)}, u32[]{:S(2)}) copy-start(s32[1,2048]{1,0:T(1,128)} %param.18) | copy-start | bytes 24580
  197.9 30.2 %collective-permute-start.8 = (bf16[4,16,8192]{2,1,0:T(8,128)(2,1)}, bf16[4,16,8192]{2,1,0:T(8,128)(2,1)}, u32[]{:S(2)}, u32[]{:S(2)}) collective-permute-start(bf16[4,16,8192]{2,1,0:T(8,128)(2,1)} %norm_image.2.refs_9_), channel_id=1, source_target_pairs={{0,4},{4,8},{8,12},{12,0},{1,5},{5,9},{9,13},{13,1},{2,6},{6,10},{... | collective-permute-start | bytes 3145736 | tf_op jit(solution)/shard_map/ppermute | solution.py:24
  198.2 34.3 %collective-permute-start.22 = (bf16[1024,640]{1,0:T(8,128)(2,1)}, bf16[1024,640]{1,0:T(8,128)(2,1)S(1)}, u32[]{:S(2)}, u32[]{:S(2)}) collective-permute-start(bf16[1024,640]{1,0:T(8,128)(2,1)} %collective-permute-done.21.refs_36_.refs_11_), channel_id=1, source_target_pairs={{0,1},{1,2},{2,3},{3,0},{4,5},{5,6},{6,7},{7,4},{8,9},{9,10},{10,1... | collective-permute-start | bytes 3932168 | tf_op jit(solution)/shard_map/ppermute | solution.py:24
  220.1 16.1 %collective-permute-start.17 = (bf16[1024,640]{1,0:T(8,128)(2,1)}, bf16[1024,640]{1,0:T(8,128)(2,1)}, u32[]{:S(2)}, u32[]{:S(2)}) collective-permute-start(bf16[1024,640]{1,0:T(8,128)(2,1)} %collective-permute-done.13.refs_20_.refs_3_), channel_id=1, source_target_pairs={{0,16},{16,0},{1,17},{17,1},{2,18},{18,2},{3,19},{19,3},{4,20},{20... | collective-permute-start | bytes 3932168 | tf_op jit(solution)/shard_map/ppermute | solution.py:24
  226.6 30.6 %collective-permute-start.15 = (bf16[1024,640]{1,0:T(8,128)(2,1)}, bf16[1024,640]{1,0:T(8,128)(2,1)}, u32[]{:S(2)}, u32[]{:S(2)}) collective-permute-start(bf16[1024,640]{1,0:T(8,128)(2,1)} %collective-permute-done.13.refs_20_.refs_3_), channel_id=1, source_target_pairs={{0,96},{32,0},{64,32},{96,64},{1,97},{33,1},{65,33},{97,65},{2,98}... | collective-permute-start | bytes 3932168 | tf_op jit(solution)/shard_map/ppermute | solution.py:24
  227.9 29.3 %collective-permute-start.6 = (bf16[4,16,8192]{2,1,0:T(8,128)(2,1)}, bf16[4,16,8192]{2,1,0:T(8,128)(2,1)}, u32[]{:S(2)}, u32[]{:S(2)}) collective-permute-start(bf16[4,16,8192]{2,1,0:T(8,128)(2,1)} %norm_image.2.refs_9_), channel_id=1, source_target_pairs={{0,12},{4,0},{8,4},{12,8},{1,13},{5,1},{9,5},{13,9},{2,14},{6,2},{... | collective-permute-start | bytes 3145736 | tf_op jit(solution)/shard_map/ppermute | solution.py:24
  228.1 42.4 %collective-permute-start.9 = (bf16[4,16,8192]{2,1,0:T(8,128)(2,1)}, bf16[4,16,8192]{2,1,0:T(8,128)(2,1)}, u32[]{:S(2)}, u32[]{:S(2)}) collective-permute-start(bf16[4,16,8192]{2,1,0:T(8,128)(2,1)} %collective-permute-done.8.refs_15_), channel_id=1, source_target_pairs={{0,4},{4,8},{8,12},{12,0},{1,5},{5,9},{9,13},{13,1},{2,6},{6,10},{... | collective-permute-start | bytes 3145736 | tf_op jit(solution)/shard_map/ppermute | solution.py:24
  232.5 46.3 %copy-start.4 = (bf16[1024,640]{1,0:T(8,128)(2,1)}, bf16[1024,640]{1,0:T(8,128)(2,1)S(1)}, u32[]{:S(2)}) copy-start(bf16[1024,640]{1,0:T(8,128)(2,1)S(1)} %collective-permute-done.22.refs_28_) | copy-start | bytes 3932164
  232.5 37.0 %collective-permute-start.10 = (bf16[3,16,8192]{2,1,0:T(8,128)(2,1)}, bf16[3,16,8192]{2,1,0:T(8,128)(2,1)S(1)}, u32[]{:S(2)}, u32[]{:S(2)}) collective-permute-start(bf16[3,16,8192]{2,1,0:T(8,128)(2,1)} %copy-done.8), channel_id=1, source_target_pairs={{0,12},{4,0},{8,4},{12,8},{1,13},{5,1},{9,5},{13,9},{2,14},{6,2},{... | collective-permute-start | bytes 2359304 | tf_op jit(solution)/shard_map/ppermute | solution.py:24
  236.2 43.7 %collective-permute-start.25 = (bf16[1024,640]{1,0:T(8,128)(2,1)}, bf16[1024,640]{1,0:T(8,128)(2,1)}, u32[]{:S(2)}, u32[]{:S(2)}) collective-permute-start(bf16[1024,640]{1,0:T(8,128)(2,1)} %collective-permute-done.20.refs_27_), channel_id=1, source_target_pairs={{0,16},{16,0},{1,17},{17,1},{2,18},{18,2},{3,19},{19,3},{4,20},{20... | collective-permute-start | bytes 3932168 | tf_op jit(solution)/shard_map/ppermute | solution.py:24
  257.2 31.0 %collective-permute-start.23 = (bf16[1024,640]{1,0:T(8,128)(2,1)}, bf16[1024,640]{1,0:T(8,128)(2,1)}, u32[]{:S(2)}, u32[]{:S(2)}) collective-permute-start(bf16[1024,640]{1,0:T(8,128)(2,1)} %collective-permute-done.20.refs_27_), channel_id=1, source_target_pairs={{0,32},{32,64},{64,96},{96,0},{1,33},{33,65},{65,97},{97,1},{2,34}... | collective-permute-start | bytes 3932168 | tf_op jit(solution)/shard_map/ppermute | solution.py:24
  257.2 21.5 %collective-permute-start.34 = (bf16[1024,640]{1,0:T(8,128)(2,1)}, bf16[1024,640]{1,0:T(8,128)(2,1)}, u32[]{:S(2)}, u32[]{:S(2)}) collective-permute-start(bf16[1024,640]{1,0:T(8,128)(2,1)} %collective-permute-done.30.refs_37_.refs_12_), channel_id=1, source_target_pairs={{0,16},{16,0},{1,17},{17,1},{2,18},{18,2},{3,19},{19,3},{4,20},{20... | collective-permute-start | bytes 3932168 | tf_op jit(solution)/shard_map/ppermute | solution.py:24
  269.5 20.4 %collective-permute-start.18 = (bf16[1024,640]{1,0:T(8,128)(2,1)}, bf16[1024,640]{1,0:T(8,128)(2,1)}, u32[]{:S(2)}, u32[]{:S(2)}) collective-permute-start(bf16[1024,640]{1,0:T(8,128)(2,1)} %collective-permute-done.14.refs_21_.refs_4_), channel_id=1, source_target_pairs={{0,16},{16,0},{1,17},{17,1},{2,18},{18,2},{3,19},{19,3},{4,20},{20... | collective-permute-start | bytes 3932168 | tf_op jit(solution)/shard_map/ppermute | solution.py:24
  270.6 29.6 %collective-permute-start.24 = (bf16[1024,640]{1,0:T(8,128)(2,1)S(1)}, bf16[1024,640]{1,0:T(8,128)(2,1)}, u32[]{:S(2)}, u32[]{:S(2)}) collective-permute-start(bf16[1024,640]{1,0:T(8,128)(2,1)S(1)} %collective-permute-done.22.refs_28_), channel_id=1, source_target_pairs={{0,96},{32,0},{64,32},{96,64},{1,97},{33,1},{65,33},{97,65},{2,98}... | collective-permute-start | bytes 3932168 | tf_op jit(solution)/shard_map/ppermute | solution.py:24
  278.7 25.8 %collective-permute-start.26 = (bf16[1024,640]{1,0:T(8,128)(2,1)S(1)}, bf16[1024,640]{1,0:T(8,128)(2,1)}, u32[]{:S(2)}, u32[]{:S(2)}) collective-permute-start(bf16[1024,640]{1,0:T(8,128)(2,1)S(1)} %collective-permute-done.22.refs_28_), channel_id=1, source_target_pairs={{0,16},{16,0},{1,17},{17,1},{2,18},{18,2},{3,19},{19,3},{4,20},{20... | collective-permute-start | bytes 3932168 | tf_op jit(solution)/shard_map/ppermute | solution.py:24
  279.9 24.6 %collective-permute-start.35 = (bf16[1024,640]{1,0:T(8,128)(2,1)}, bf16[1024,640]{1,0:T(8,128)(2,1)S(1)}, u32[]{:S(2)}, u32[]{:S(2)}) collective-permute-start(bf16[1024,640]{1,0:T(8,128)(2,1)} %collective-permute-done.31.refs_38_.refs_13_), channel_id=1, source_target_pairs={{0,16},{16,0},{1,17},{17,1},{2,18},{18,2},{3,19},{19,3},{4,20},{20... | collective-permute-start | bytes 3932168 | tf_op jit(solution)/shard_map/ppermute | solution.py:24
  288.2 16.3 %collective-permute-start.19 = (bf16[1024,640]{1,0:T(8,128)(2,1)}, bf16[1024,640]{1,0:T(8,128)(2,1)}, u32[]{:S(2)}, u32[]{:S(2)}) collective-permute-start(bf16[1024,640]{1,0:T(8,128)(2,1)} %collective-permute-done.15.refs_22_.refs_5_), channel_id=1, source_target_pairs={{0,16},{16,0},{1,17},{17,1},{2,18},{18,2},{3,19},{19,3},{4,20},{20... | collective-permute-start | bytes 3932168 | tf_op jit(solution)/shard_map/ppermute | solution.py:24
  289.9 14.6 %collective-permute-start.27 = (bf16[1024,640]{1,0:T(8,128)(2,1)}, bf16[1024,640]{1,0:T(8,128)(2,1)}, u32[]{:S(2)}, u32[]{:S(2)}) collective-permute-start(bf16[1024,640]{1,0:T(8,128)(2,1)} %collective-permute-done.23.refs_29_), channel_id=1, source_target_pairs={{0,16},{16,0},{1,17},{17,1},{2,18},{18,2},{3,19},{19,3},{4,20},{20... | collective-permute-start | bytes 3932168 | tf_op jit(solution)/shard_map/ppermute | solution.py:24
  300.1 4.7 %collective-permute-start.28 = (bf16[1024,640]{1,0:T(8,128)(2,1)}, bf16[1024,640]{1,0:T(8,128)(2,1)}, u32[]{:S(2)}, u32[]{:S(2)}) collective-permute-start(bf16[1024,640]{1,0:T(8,128)(2,1)} %collective-permute-done.24.refs_30_), channel_id=1, source_target_pairs={{0,16},{16,0},{1,17},{17,1},{2,18},{18,2},{3,19},{19,3},{4,20},{20... | collective-permute-start | bytes 3932168 | tf_op jit(solution)/shard_map/ppermute | solution.py:24
  345.6 41.0 %collective-permute-start.39 = (bf16[576,768]{1,0:T(8,128)(2,1)}, bf16[576,768]{1,0:T(8,128)(2,1)S(1)}, u32[]{:S(2)}, u32[]{:S(2)}) collective-permute-start(bf16[576,768]{1,0:T(8,128)(2,1)} %get-tuple-element.27), channel_id=1, source_target_pairs={{0,3},{1,0},{2,1},{3,2},{4,7},{5,4},{6,5},{7,6},{8,11},{9,8},{10,9... | collective-permute-start | bytes 2654216 | tf_op jit(solution)/shard_map/ppermute | solution.py:24
  348.2 41.6 %collective-permute-start.41 = (bf16[576,768]{1,0:T(8,128)(2,1)}, bf16[576,768]{1,0:T(8,128)(2,1)S(1)}, u32[]{:S(2)}, u32[]{:S(2)}) collective-permute-start(bf16[576,768]{1,0:T(8,128)(2,1)} %get-tuple-element.25), channel_id=1, source_target_pairs={{0,1},{1,2},{2,3},{3,0},{4,5},{5,6},{6,7},{7,4},{8,9},{9,10},{10,1... | collective-permute-start | bytes 2654216 | tf_op jit(solution)/shard_map/ppermute | solution.py:24
  348.2 41.6 %collective-permute-start.40 = (bf16[576,768]{1,0:T(8,128)(2,1)}, bf16[576,768]{1,0:T(8,128)(2,1)S(1)}, u32[]{:S(2)}, u32[]{:S(2)}) collective-permute-start(bf16[576,768]{1,0:T(8,128)(2,1)} %get-tuple-element.28), channel_id=1, source_target_pairs={{0,2},{1,3},{2,0},{3,1},{4,6},{5,7},{6,4},{7,5},{8,10},{9,11},{10,... | collective-permute-start | bytes 2654216 | tf_op jit(solution)/shard_map/ppermute | solution.py:24
  (12 other events, 127.0 us)

commit v3 on v2

--- a/solution.py
+++ b/solution.py
@@ -72,10 +72,14 @@
     )(chosen, pieces, gain)
 
 
-def spread_kernel(chosen_ref, pieces_ref, out_ref, sems):
+def spread_kernel(chosen_ref, pieces_ref, out_ref, held_ref, in_sem, sems):
+    copy_in = pltpu.make_async_copy(pieces_ref, held_ref, in_sem)
+    copy_in.start()
+    copy_in.wait()
+
     def copy(index):
         return pltpu.make_async_copy(
-            pieces_ref.at[chosen_ref[index]], out_ref.at[index], sems.at[index]
+            held_ref.at[chosen_ref[index]], out_ref.at[index], sems.at[index]
         )
 
     for index in range(out_ref.shape[0]):
@@ -94,7 +98,11 @@
             grid=(1,),
             in_specs=[far_spec],
             out_specs=far_spec,
-            scratch_shapes=[pltpu.SemaphoreType.DMA((count,))],
+            scratch_shapes=[
+                pltpu.VMEM(pieces.shape, jnp.bfloat16),
+                pltpu.SemaphoreType.DMA,
+                pltpu.SemaphoreType.DMA((count,)),
+            ],
         ),
         out_shape=pltpu.HBM((count,) + pieces.shape[1:], jnp.bfloat16),
         name="spread",
@@ -138,10 +146,12 @@
 
 def run_tiles(tiles, copies, rows_ref, weight_buf, sum_ref, finish, before):
     slots = weight_buf.shape[0]
-    for index in range(min(slots, len(tiles))):
+    for copy in copies(tiles[0], 0):
+        copy.start()
+    before()
+    for index in range(1, min(slots, len(tiles))):
         for copy in copies(tiles[index], index):
             copy.start()
-    before()
 
     def step(number, carry):
         slot = number % slots
@@ -151,9 +161,25 @@
                 for copy in copies(tile, index % slots):
                     copy.wait()
 
-        sum_ref[slot] = jnp.dot(
-            rows_ref[...], weight_buf[slot], preferred_element_type=jnp.float32
-        )
+        half = rows_ref.shape[1] // 2
+
+        def half_step(part, carry):
+            inner = pl.ds(pl.multiple_of(part * half, half), half)
+            product = jnp.dot(
+                rows_ref[:, inner], weight_buf[slot, inner, :], preferred_element_type=jnp.float32
+            )
+
+            @pl.when(part == 0)
+            def _():
+                sum_ref[slot] = product
+
+            @pl.when(part == 1)
+            def _():
+                sum_ref[slot] += product
+
+            return carry
+
+        lax.fori_loop(0, 2, half_step, 0)
         for index in range(len(tiles)):
             @pl.when(number == index)
             def _(index=index):
@@ -167,15 +193,15 @@
     lax.fori_loop(0, len(tiles), step, 0)
 
 
-def project_first_kernel(*refs):
+def project_kv_kernel(*refs):
     place_ref = refs[0]
     sources = refs[1:17]
-    own_q, own_kv = refs[17:19]
-    pieces = {1: refs[19:27], 2: refs[27:35], 3: refs[35:43]}
-    kv_bias_ref, q_bias_ref, cos_ref, sin_ref, out_ref, kv_ref, compact_ref = refs[43:50]
+    own_kv = refs[17]
+    pieces = {1: refs[18:26], 2: refs[26:34], 3: refs[34:42]}
+    bias_ref, cos_ref, sin_ref = refs[42:45]
+    outs, compact_ref = refs[45:49], refs[49]
     rows_ref, weight_buf, sum_ref, sems, weight_sems, copy_sem = refs[50:]
-    copies = weight_tile(own_q, own_kv, pieces, place_ref, weight_buf, weight_sems)
-    width = q_bias_ref.shape[1]
+    copies = weight_tile(None, own_kv, pieces, place_ref, weight_buf, weight_sems)
     copy_out = pltpu.make_async_copy(rows_ref, compact_ref, copy_sem)
 
     def unit_copy(index):
@@ -209,33 +235,31 @@
         copy_out.start()
 
     def finish(index, product):
-        if index == 1:
-            odd = place_ref[65] == 1
-            halves = [
-                sum_ref[delta // 2, :, pl.ds(delta % 2 * HD, HD)]
-                + kv_bias_ref[:, pl.ds(delta * HD, HD)]
-                for delta in range(4)
-            ]
-            in_low = lax.broadcasted_iota(jnp.int32, halves[0].shape, 1) < HD // 2
-            ends = (
-                (jnp.where(odd, halves[3], halves[0]), jnp.where(odd, halves[0], halves[1])),
-                (jnp.where(odd, halves[1], halves[2]), jnp.where(odd, halves[2], halves[3])),
-            )
-            for head, (low, high) in enumerate(ends):
-                key = jnp.where(in_low, low, pltpu.roll(high, HD // 2, 1))
-                value = jnp.where(in_low, pltpu.roll(low, HD // 2, 1), high)
-                kv_ref[head, :, :HD] = rotated(key, cos_ref[...], sin_ref[...]).astype(
-                    jnp.bfloat16
-                )
-                kv_ref[head, :, HD:] = value.astype(jnp.bfloat16)
-            out_ref[:, width:] = kv_ref[1]
-        if index >= 2:
-            store_heads(out_ref, index - 2, product, q_bias_ref, cos_ref, sin_ref)
-
-    tiles = [
-        [(0, 512, HD), (1, 512, HD)], [(2, 512, HD), (3, 512, HD)],
-        [(2, 0, COLUMNS)], [(2, COLUMNS, COLUMNS)],
-    ]
+        if index == 0:
+            return
+        odd = place_ref[65] == 1
+        halves = [
+            sum_ref[delta // 2, :, pl.ds(delta % 2 * HD, HD)] + bias_ref[:, pl.ds(delta * HD, HD)]
+            for delta in range(4)
+        ]
+        in_low = lax.broadcasted_iota(jnp.int32, halves[0].shape, 1) < HD // 2
+        ends = (
+            (jnp.where(odd, halves[3], halves[0]), jnp.where(odd, halves[0], halves[1])),
+            (jnp.where(odd, halves[1], halves[2]), jnp.where(odd, halves[2], halves[3])),
+        )
+        near, away = [], []
+        for group, (low, high) in zip((near, away), ends):
+            key = jnp.where(in_low, low, pltpu.roll(high, HD // 2, 1))
+            value = jnp.where(in_low, pltpu.roll(low, HD // 2, 1), high)
+            group += [rotated(key, cos_ref[...], sin_ref[...]), value]
+        for part in range(2):
+            lanes = slice(part * HD, (part + 1) * HD)
+            outs[0][:, lanes] = near[part].astype(jnp.bfloat16)
+            outs[1][:, lanes] = jnp.where(odd, away[part], near[part]).astype(jnp.bfloat16)
+            outs[2][:, lanes] = away[part].astype(jnp.bfloat16)
+            outs[3][:, lanes] = jnp.where(odd, near[part], away[part]).astype(jnp.bfloat16)
+
+    tiles = [[(0, 512, HD), (1, 512, HD)], [(2, 512, HD), (3, 512, HD)]]
     run_tiles(tiles, copies, rows_ref, weight_buf, sum_ref, finish, assemble)
     copy_out.wait()
 
@@ -263,19 +287,19 @@
     return pl.BlockSpec(shape, lambda i, place: (0,) * len(shape))
 
 
-def project_first(place, texts, images, own, pieces, kv_bias, q_bias, cosine, sine):
-    width = q_bias.shape[1]
+def project_kv(place, texts, images, own_kv, pieces, bias, cosine, sine):
     features = texts[0].shape[1]
     far_spec = pl.BlockSpec(memory_space=pltpu.HBM)
     flat = [piece for delta in (1, 2, 3) for piece in pieces[delta]]
+    shape = (ROWS, 2 * HD)
     return pl.pallas_call(
-        project_first_kernel,
+        project_kv_kernel,
         grid_spec=pltpu.PrefetchScalarGridSpec(
             num_scalar_prefetch=1,
             grid=(1,),
-            in_specs=[far_spec] * (18 + len(flat))
-            + [whole((1, width)), whole((1, width)), whole((ROWS, HD)), whole((ROWS, HD))],
-            out_specs=(whole((ROWS, width + 2 * HD)), whole((2, ROWS, 2 * HD)), far_spec),
+            in_specs=[far_spec] * (17 + len(flat))
+            + [whole(bias.shape), whole((ROWS, HD)), whole((ROWS, HD))],
+            out_specs=(whole(shape),) * 4 + (far_spec,),
             scratch_shapes=[
                 pltpu.VMEM((ROWS, features), jnp.bfloat16),
                 pltpu.VMEM((2, features, COLUMNS), jnp.bfloat16),
@@ -285,55 +309,51 @@
                 pltpu.SemaphoreType.DMA,
             ],
         ),
-        out_shape=(
-            jax.ShapeDtypeStruct((ROWS, width + 2 * HD), jnp.bfloat16),
-            jax.ShapeDtypeStruct((2, ROWS, 2 * HD), jnp.bfloat16),
-            pltpu.HBM((ROWS, features), jnp.bfloat16),
-        ),
+        out_shape=(jax.ShapeDtypeStruct(shape, jnp.bfloat16),) * 4
+        + (pltpu.HBM((ROWS, features), jnp.bfloat16),),
         compiler_params=pltpu.CompilerParams(vmem_limit_bytes=40 << 20),
-        cost_estimate=cost(2 * width, features),
-        name="project_first",
-    )(place, *far([*texts, *images, *own, *flat]), kv_bias, q_bias, cosine, sine)
-
-
-def project_near_kernel(*refs):
-    place_ref, compact_ref = refs[:2]
-    pieces = {1: refs[2:10], 3: refs[10:18]}
-    kv_ref, bias1_ref, bias3_ref, cos_ref, sin_ref, out1_ref, out3_ref = refs[18:25]
-    rows_ref, weight_buf, sum_ref, row_sem, weight_sems = refs[25:]
-    copies = weight_tile(None, None, pieces, place_ref, weight_buf, weight_sems)
-    copy_in = pltpu.make_async_copy(compact_ref, rows_ref, row_sem)
-    copy_in.start()
-    width = bias1_ref.shape[1]
-    odd = place_ref[65]
-    out1_ref[:, width:] = kv_ref[odd]
-    out3_ref[:, width:] = kv_ref[1 - odd]
-
-    def finish(index, product):
-        out_ref, bias_ref = ((out1_ref, bias1_ref), (out3_ref, bias3_ref))[index // 2]
-        store_heads(out_ref, index % 2, product, bias_ref, cos_ref, sin_ref)
-
-    tiles = [[(delta, first, COLUMNS)] for delta in (1, 3) for first in (0, COLUMNS)]
-    run_tiles(tiles, copies, rows_ref, weight_buf, sum_ref, finish, copy_in.wait)
-
-
-def project_near(place, compact, pieces, kv, bias1, bias3, cosine, sine):
-    width = bias1.shape[1]
+        cost_estimate=cost(2 * COLUMNS, features),
+        name="project_kv",
+    )(place, *far([*texts, *images, own_kv, *flat]), bias, cosine, sine)
+
+
+def project_q(place, compact, own_q, pieces, biases, cosine, sine):
+    deltas = list(biases)
+    width = biases[deltas[0]].shape[1]
     features = compact.shape[1]
     far_spec = pl.BlockSpec(memory_space=pltpu.HBM)
-    flat = [piece for delta in (1, 3) for piece in pieces[delta]]
-    shape = (ROWS, width + 2 * HD)
+    weights = [own_q] if deltas == [0] else [p for delta in deltas for p in pieces[delta]]
+    shape = (ROWS, width)
+
+    def kernel(*refs):
+        place_ref, compact_ref = refs[:2]
+        weight_refs, refs = refs[2:2 + len(weights)], refs[2 + len(weights):]
+        bias_refs, refs = refs[:len(deltas)], refs[len(deltas):]
+        cos_ref, sin_ref = refs[:2]
+        outs, refs = refs[2:2 + len(deltas)], refs[2 + len(deltas):]
+        rows_ref, weight_buf, sum_ref, row_sem, weight_sems = refs
+        found = {delta: weight_refs[8 * i:8 * i + 8] for i, delta in enumerate(deltas)}
+        copies = weight_tile(weight_refs[0], None, found, place_ref, weight_buf, weight_sems)
+        copy_in = pltpu.make_async_copy(compact_ref, rows_ref, row_sem)
+        copy_in.start()
+
+        def finish(index, product):
+            store_heads(
+                outs[index // 2], index % 2, product, bias_refs[index // 2], cos_ref, sin_ref
+            )
+
+        tiles = [[(delta, first, COLUMNS)] for delta in deltas for first in (0, COLUMNS)]
+        run_tiles(tiles, copies, rows_ref, weight_buf, sum_ref, finish, copy_in.wait)
+
     return pl.pallas_call(
-        project_near_kernel,
+        kernel,
         grid_spec=pltpu.PrefetchScalarGridSpec(
             num_scalar_prefetch=1,
             grid=(1,),
-            in_specs=[far_spec] * (1 + len(flat))
-            + [
-                whole((2, ROWS, 2 * HD)), whole((1, width)), whole((1, width)),
-                whole((ROWS, HD)), whole((ROWS, HD)),
-            ],
-            out_specs=(whole(shape), whole(shape)),
+            in_specs=[far_spec] * (1 + len(weights))
+            + [whole((1, width))] * len(deltas)
+            + [whole((ROWS, HD)), whole((ROWS, HD))],
+            out_specs=(whole(shape),) * len(deltas),
             scratch_shapes=[
                 pltpu.VMEM((ROWS, features), jnp.bfloat16),
                 pltpu.VMEM((2, features, COLUMNS), jnp.bfloat16),
@@ -342,66 +362,21 @@
                 pltpu.SemaphoreType.DMA((2, 16)),
             ],
         ),
-        out_shape=(jax.ShapeDtypeStruct(shape, jnp.bfloat16),) * 2,
+        out_shape=(jax.ShapeDtypeStruct(shape, jnp.bfloat16),) * len(deltas),
         compiler_params=pltpu.CompilerParams(vmem_limit_bytes=40 << 20),
-        cost_estimate=cost(2 * width, features),
-        name="project_near",
-    )(place, *far([compact, *flat]), kv, bias1, bias3, cosine, sine)
-
-
-def project_own_kernel(
-    place_ref, compact_ref, own_q, kv_ref, bias_ref, cos_ref, sin_ref, out_ref,
-    rows_ref, weight_buf, sum_ref, row_sem, weight_sems,
+        cost_estimate=cost(width * len(deltas), features),
+        name="project_q",
+    )(place, *far([compact, *weights]), *biases.values(), cosine, sine)
+
+
+def attend_kernel(
+    info_ref, text_ref, q0, q1, q2, q3, kv0, kv1, kv2, kv3, out_ref, merged_ref, run_ref, mask_ref
 ):
-    copies = weight_tile(own_q, None, {}, place_ref, weight_buf, weight_sems)
-    copy_in = pltpu.make_async_copy(compact_ref, rows_ref, row_sem)
-    copy_in.start()
-    out_ref[:, bias_ref.shape[1]:] = kv_ref[0]
-
-    def finish(index, product):
-        store_heads(out_ref, index, product, bias_ref, cos_ref, sin_ref)
-
-    tiles = [[(0, 0, COLUMNS)], [(0, COLUMNS, COLUMNS)]]
-    run_tiles(tiles, copies, rows_ref, weight_buf, sum_ref, finish, copy_in.wait)
-
-
-def project_own(place, compact, own_q, kv, bias, cosine, sine):
-    width = bias.shape[1]
-    features = compact.shape[1]
-    far_spec = pl.BlockSpec(memory_space=pltpu.HBM)
-    shape = (ROWS, width + 2 * HD)
-    return pl.pallas_call(
-        project_own_kernel,
-        grid_spec=pltpu.PrefetchScalarGridSpec(
-            num_scalar_prefetch=1,
-            grid=(1,),
-            in_specs=[far_spec] * 2
-            + [
-                whole((2, ROWS, 2 * HD)), whole((1, width)), whole((ROWS, HD)), whole((ROWS, HD)),
-            ],
-            out_specs=whole(shape),
-            scratch_shapes=[
-                pltpu.VMEM((ROWS, features), jnp.bfloat16),
-                pltpu.VMEM((2, features, COLUMNS), jnp.bfloat16),
-                pltpu.VMEM((2, ROWS, COLUMNS), jnp.float32),
-                pltpu.SemaphoreType.DMA,
-                pltpu.SemaphoreType.DMA((2, 16)),
-            ],
-        ),
-        out_shape=jax.ShapeDtypeStruct(shape, jnp.bfloat16),
-        compiler_params=pltpu.CompilerParams(vmem_limit_bytes=40 << 20),
-        cost_estimate=cost(width, features),
-        name="project_own",
-    )(place, *far([compact, own_q]), kv, bias, cosine, sine)
-
-
-def attend_kernel(
-    info_ref, text_ref, part0, part1, part2, part3, out_ref, merged_ref, run_ref, mask_ref
-):
-    parts = (part0, part1, part2, part3)
+    parts = ((q0, kv0), (q1, kv1), (q2, kv2), (q3, kv3))
+    q_width = q0.shape[1]
     step = pl.program_id(0)
     block = out_ref.shape[0]
-    width = part0.shape[1]
+    width = merged_ref.shape[1]
     mine = info_ref[11]
     run_start = info_ref[8]
     run_end = info_ref[9]
@@ -421,7 +396,9 @@
                 member = (mine + delta) % 4
                 source = pl.multiple_of(tile * 64 + level * UNIT, UNIT)
                 target = pl.multiple_of(128 + tile * TR + (4 * level + member) * UNIT, UNIT)
-                run_ref[pl.ds(target, UNIT), :] = parts[delta][pl.ds(source, UNIT), :]
+                query, pair = parts[delta]
+                run_ref[pl.ds(target, UNIT), :q_width] = query[pl.ds(source, UNIT), :]
+                run_ref[pl.ds(target, UNIT), q_width:] = pair[pl.ds(source, UNIT), :]
             return carry
 
         lax.fori_loop(0, (run_end - run_start) // TR, tile_step, 0)
@@ -440,7 +417,9 @@
                 for unit in range(8):
                     source = pl.multiple_of(text_ref[number * 8 + unit] * UNIT, UNIT)
                     target = pl.multiple_of(WINDOW + begin + unit * UNIT, UNIT)
-                    merged_ref[pl.ds(target, UNIT), :] = parts[delta][pl.ds(source, UNIT), :]
+                    query, pair = parts[delta]
+                    merged_ref[pl.ds(target, UNIT), :q_width] = query[pl.ds(source, UNIT), :]
+                    merged_ref[pl.ds(target, UNIT), q_width:] = pair[pl.ds(source, UNIT), :]
 
                 @pl.when((begin < run_end) & (begin + 128 > run_start))
                 def _():
@@ -509,14 +488,13 @@
 
 def attend(info, text_index, parts):
     block = 128
-    shape = parts[0].shape
-    width = shape[1]
+    width = parts[0].shape[1] + parts[4].shape[1]
     return pl.pallas_call(
         attend_kernel,
         grid_spec=pltpu.PrefetchScalarGridSpec(
             num_scalar_prefetch=2,
             grid=(LENGTH // block,),
-            in_specs=[pl.BlockSpec(shape, lambda i, a, b: (0, 0))] * 4,
+            in_specs=[pl.BlockSpec(part.shape, lambda i, a, b: (0, 0)) for part in parts],
             out_specs=pl.BlockSpec((block, 4 * HD), lambda i, a, b: (i, 0)),
             scratch_shapes=[
                 pltpu.VMEM((WINDOW + LENGTH, width), jnp.bfloat16),
@@ -667,16 +645,21 @@
 
     texts = (t_low, t_high, t1_low, t1_high, t2_low, t2_high, t3_low, t3_high)
     images = (i_low, i_high, i1_low, i1_high, i2_low, i2_high, i3_low, i3_high)
-    out2, kv, compact = project_first(
-        place, texts, images, (q_weight, own_kv), pieces, kv_bias, q_biases[2], cosine, sine
-    )
-    part2 = shifted(out2, "y", 2)
-    out1, out3 = project_near(place, compact, pieces, kv, q_biases[1], q_biases[3], cosine, sine)
-    part3 = shifted(out1, "y", 1)
-    part1 = shifted(out3, "y", -1)
-    kv, out1 = lax.optimization_barrier((kv, out1))
-    part0 = project_own(place, compact, q_weight, kv, q_biases[0], cosine, sine)
-    return attend(info, text_index, (part0, part1, part2, part3))
+    *pairs, compact = project_kv(place, texts, images, own_kv, pieces, kv_bias, cosine, sine)
+    queries = {}
+    after = compact
+    for deltas in ((2,), (1, 3), (0,)):
+        found = project_q(
+            place, after, q_weight, pieces,
+            {delta: q_biases[delta] for delta in deltas}, cosine, sine,
+        )
+        after, *found = lax.optimization_barrier((after, *found))
+        queries.update(zip(deltas, found))
+    parts = []
+    for values in (queries, pairs):
+        parts.append(values[0])
+        parts += [shifted(values[4 - delta], "y", -delta) for delta in (1, 2, 3)]
+    return attend(info, text_index, parts)
 
 
 def solution(mesh):

time: 407 us -> 353 us (0.87)
  Pallas kernels: 147 us -> 92.6 us
    pallas_call x1, Pallas kernels: 65.4 us -> 3.27 us  [spread(): pl.pallas_call(spread_kernel, grid_spec=pltpu.PrefetchScalarGridSpec(num_...]
    pallas_call x3 -> x4, Pallas kernels: 51.5 us -> 59.4 us  [the longest x3 43.4 us: project_q(): pl.pallas_call(kernel, grid_spec=pltpu.PrefetchScalarGridSpec(num_scalar_...]
    ppermute x42 -> x45, starting transfers between devices: 66.4 us -> 68.1 us  [shifted(): lax.ppermute(block, axis, [(low, (low + step) % count) for low in range(c...]
    ppermute x42 -> x45, waiting for transfers between devices: 154 us -> 154 us  [shifted(): lax.ppermute(block, axis, [(low, (low + step) % count) for low in range(c...]
  transfers between devices with their start and end apart: 43 -> 46, of which waited for: 18 -> 18; matrix products, arithmetic and copies ran while one was open for 6% -> 7% of each run, Pallas kernels for 5% -> 12%
where the time goes in v3:
time: 353 us; the launch traced here: 352 us
  waiting for transfers between devices  154 us (44%)
  Pallas kernels  92.6 us (26%)
  starting transfers between devices  73.5 us (21%)
  other arithmetic  15.3 us (4%)
  local copies, waits for them, and re-layouts  12.1 us (3%)
  between operations  4.53 us (1%)
    ppermute x45, waiting for transfers between devices, shifted(): lax.ppermute(block, axis, [(low, (low + step) % count) for low in range(c...  154 us
    ppermute x45, starting transfers between devices, shifted(): lax.ppermute(block, axis, [(low, (low + step) % count) for low in range(c...  68.1 us
    pallas_call x3, Pallas kernels, project_q(): pl.pallas_call(kernel, grid_spec=pltpu.PrefetchScalarGridSpec(num_scalar_...  43.4 us
    pallas_call x1, Pallas kernels, attend(): pl.pallas_call(attend_kernel, grid_spec=pltpu.PrefetchScalarGridSpec(num_...  16.6 us
    pallas_call x1, Pallas kernels, project_kv(): pl.pallas_call(project_kv_kernel, grid_spec=pltpu.PrefetchScalarGridSpec(...  16 us
    pallas_call x2, Pallas kernels, norm_image(): pl.pallas_call(norm_image_kernel, grid_spec=pltpu.PrefetchScalarGridSpec(...  8.25 us
  transfers between devices with their start and end apart: 46, of which 18 were waited for; matrix products, arithmetic and copies ran while one was open for 7% of the time, Pallas kernels for 12%

profile of v3, /device:TPU:1, one launch (start us, length us, event | category | flops | bytes accessed | tf_op | source)
XLA Modules:
  0.0 352.1 jit_solution(8645038507926337694)
XLA Ops:
  1.3 3.3 spread.1
  4.6 2.6 shard_map.127.refs_1_
  7.2 2.5 collective-permute-start.2
  9.7 2.1 collective-permute-start
  13.0 2.8 copy.19
  15.7 1.5 fusion.1
  17.2 2.0 constant_dynamic-slice_fusion
  21.6 2.5 shard_map.128.refs_2_
  24.2 5.4 %all-to-all-start = ((bf16[8,16,8192]{2,1,0:T(8,128)(2,1)}), bf16[8,16,8192]{2,1,0:T(8,128)(2,1)}, u32[]{:S(2)}, u32[]{:S(2)}) async-start(bf16[8,16,8192]{2,1,0:T(8,128)(2,1)} %spread.1), calls=%async_computation | async-start | bytes 4194304 | tf_op jit(solution)/shard_map/all_to_all | solution.py:573
  30.9 2.8 collective-permute-start.1
  35.0 2.7 collective-permute-start.12
  37.7 19.7 %collective-permute-done.5.refs_8_ = bf16[64,8192]{1,0:T(8,128)(2,1)} collective-permute-done((bf16[64,8192]{1,0:T(8,128)(2,1)}, bf16[64,8192]{1,0:T(8,128)(2,1)}, u32[]{:S(2)}, u32[]{:S(2)}) %collective-permute-start.5) | collective-permute-done | bytes 1048608 | tf_op jit(solution)/shard_map/ppermute | solution.py:24
  57.5 2.7 collective-permute-start.13
  61.5 2.8 collective-permute-start.4
  66.1 3.6 %norm_image.3.refs_10_ = bf16[3,16,8192]{2,1,0:T(8,128)(2,1)} custom-call(s32[3]{0:T(128)} %slice.35.chosen_ref, bf16[8,16,8192]{2,1,0:T(8,128)(2,1)} %all-to-all-done.rows_ref, f32[1,8192]{1,0:T(1,128)} %bitcast.34), custom_call_target="tpu_custom_call" | custom-call | tf_op jit(solution)/shard_map/norm_image/pallas_call | solution.py:59
  69.8 19.7 %collective-permute-done.21.refs_35_.refs_11_ = bf16[1024,640]{1,0:T(8,128)(2,1)} collective-permute-done((bf16[1024,640]{1,0:T(8,128)(2,1)}, bf16[1024,640]{1,0:T(8,128)(2,1)}, u32[]{:S(2)}, u32[]{:S(2)}) %collective-permute-start.21) | collective-permute-done | bytes 1310752 | tf_op jit(solution)/shard_map/ppermute | solution.py:24
  90.6 1.6 collective-permute-done.13.refs_19_.refs_3_
  92.9 4.0 %collective-permute-done.38 = f32[640]{0:T(1024)S(1)} collective-permute-done((f32[640]{0:T(1024)S(1)}, f32[640]{0:T(1024)S(1)}, u32[]{:S(2)}, u32[]{:S(2)}) %collective-permute-start.38) | collective-permute-done | bytes 2592 | tf_op jit(solution)/shard_map/ppermute | solution.py:24
  97.5 3.4 collective-permute-done.37
  100.9 1.5 collective-permute-start.36
  102.4 1.4 collective-permute-done.36
  105.0 2.3 collective-permute-start.20
  107.9 7.4 %collective-permute-start.16 = (bf16[1024,640]{1,0:T(8,128)(2,1)}, bf16[1024,640]{1,0:T(8,128)(2,1)}, u32[]{:S(2)}, u32[]{:S(2)}) collective-permute-start(bf16[1024,640]{1,0:T(8,128)(2,1)} %collective-permute-done.12.refs_18_.refs_2_), channel_id=1, source_target_pairs={{0,16},{16,0},{1,17},{17,1},{2,18},{18,2},{3,19},{19,3},{4,20},{20... | collective-permute-start | bytes 3932168 | tf_op jit(solution)/shard_map/ppermute | solution.py:24
  115.4 4.7 %collective-permute-done.7.refs_12_ = bf16[3,16,8192]{2,1,0:T(8,128)(2,1)} collective-permute-done((bf16[3,16,8192]{2,1,0:T(8,128)(2,1)}, bf16[3,16,8192]{2,1,0:T(8,128)(2,1)}, u32[]{:S(2)}, u32[]{:S(2)}) %collective-permute-start.7) | collective-permute-done | bytes 786464 | tf_op jit(solution)/shard_map/ppermute | solution.py:24
  121.3 7.7 %collective-permute-start.33 = (bf16[1024,640]{1,0:T(8,128)(2,1)}, bf16[1024,640]{1,0:T(8,128)(2,1)}, u32[]{:S(2)}, u32[]{:S(2)}) collective-permute-start(bf16[1024,640]{1,0:T(8,128)(2,1)} %collective-permute-done.21.refs_35_.refs_11_), channel_id=1, source_target_pairs={{0,16},{16,0},{1,17},{17,1},{2,18},{18,2},{3,19},{19,3},{4,20},{20... | collective-permute-start | bytes 3932168 | tf_op jit(solution)/shard_map/ppermute | solution.py:24
  133.5 4.6 %norm_image.2.refs_9_ = bf16[4,16,8192]{2,1,0:T(8,128)(2,1)} custom-call(s32[4]{0:T(128)} %bitcast.37, bf16[8,16,8192]{2,1,0:T(8,128)(2,1)} %all-to-all-done.rows_ref, f32[1,8192]{1,0:T(1,128)} %bitcast.35), custom_call_target="tpu_custom_call" | custom-call | tf_op jit(solution)/shard_map/norm_image/pallas_call | solution.py:59
  139.3 19.0 %collective-permute-done.14.refs_20_.refs_4_ = bf16[1024,640]{1,0:T(8,128)(2,1)} collective-permute-done((bf16[1024,640]{1,0:T(8,128)(2,1)}, bf16[1024,640]{1,0:T(8,128)(2,1)}, u32[]{:S(2)}, u32[]{:S(2)}) %collective-permute-start.14) | collective-permute-done | bytes 1310752 | tf_op jit(solution)/shard_map/ppermute | solution.py:24
  158.3 6.3 %collective-permute-start.17 = (bf16[1024,640]{1,0:T(8,128)(2,1)}, bf16[1024,640]{1,0:T(8,128)(2,1)}, u32[]{:S(2)}, u32[]{:S(2)}) collective-permute-start(bf16[1024,640]{1,0:T(8,128)(2,1)} %collective-permute-done.13.refs_19_.refs_3_), channel_id=1, source_target_pairs={{0,16},{16,0},{1,17},{17,1},{2,18},{18,2},{3,19},{19,3},{4,20},{20... | collective-permute-start | bytes 3932168 | tf_op jit(solution)/shard_map/ppermute | solution.py:24
  166.0 1.4 collective-permute-start.9
  171.5 1.4 collective-permute-start.10
  174.5 2.0 collective-permute-start.25
  176.5 18.7 %collective-permute-done.15.refs_21_.refs_5_ = bf16[1024,640]{1,0:T(8,128)(2,1)} collective-permute-done((bf16[1024,640]{1,0:T(8,128)(2,1)}, bf16[1024,640]{1,0:T(8,128)(2,1)}, u32[]{:S(2)}, u32[]{:S(2)}) %collective-permute-start.15) | collective-permute-done | bytes 1310752 | tf_op jit(solution)/shard_map/ppermute | solution.py:24
  196.4 11.2 %collective-permute-done.10.refs_14_ = bf16[3,16,8192]{2,1,0:T(8,128)(2,1)} collective-permute-done((bf16[3,16,8192]{2,1,0:T(8,128)(2,1)}, bf16[3,16,8192]{2,1,0:T(8,128)(2,1)}, u32[]{:S(2)}, u32[]{:S(2)}) %collective-permute-start.10) | collective-permute-done | bytes 786464 | tf_op jit(solution)/shard_map/ppermute | solution.py:24
  212.0 4.1 %pad_maximum_fusion.refs_17_ = bf16[8192,128]{1,0:T(8,128)(2,1)} fusion(bf16[8192,64]{1,0:T(8,128)(2,1)} %copy.19, bf16[8192,64]{1,0:T(8,128)(2,1)S(1)} %copy.18), kind=kLoop, calls=%fused_computation.3 | loop fusion | flops 4194304 | bytes 4194304 | tf_op jit(solution)/shard_map/concatenate | solution.py:582
  216.6 9.4 %collective-permute-done.23.refs_28_.refs_4_ = bf16[1024,640]{1,0:T(8,128)(2,1)} collective-permute-done((bf16[1024,640]{1,0:T(8,128)(2,1)S(1)}, bf16[1024,640]{1,0:T(8,128)(2,1)}, u32[]{:S(2)}, u32[]{:S(2)}) %collective-permute-start.23) | collective-permute-done | bytes 1310752 | tf_op jit(solution)/shard_map/ppermute | solution.py:24
  226.0 1.7 collective-permute-start.19
  227.7 11.6 %collective-permute-done.24.refs_29_.refs_5_ = bf16[1024,640]{1,0:T(8,128)(2,1)} collective-permute-done((bf16[1024,640]{1,0:T(8,128)(2,1)}, bf16[1024,640]{1,0:T(8,128)(2,1)}, u32[]{:S(2)}, u32[]{:S(2)}) %collective-permute-start.24) | collective-permute-done | bytes 1310752 | tf_op jit(solution)/shard_map/ppermute | solution.py:24
  240.7 2.4 collective-permute-done.28.refs_33_.refs_9_
  244.1 16.0 %project_kv.1 = (bf16[576,256]{1,0:T(8,128)(2,1)S(1)}, bf16[576,256]{1,0:T(8,128)(2,1)S(1)}, bf16[576,256]{1,0:T(8,128)(2,1)S(1)}, bf16[576,256]{1,0:T(8,128)(2,1)}, bf16[576,8192]{1,0:T(8,128)(2,1)}) custom-call(s32[70]{0:T(128)S(1)} %concatenate.28.refs_0_, bf16[64,8192]{1,0:T(8,128)(2,1)} %shard_map.127.refs_1_, bf16[64,8192]{1,0:T(8,128)(2,1)} %shard_map.128.refs_2_, ...), custom_call_target="tpu_custom_call" | custom-call | flops 4831838208 | bytes 17825792 | tf_op jit(solution)/shard_map/project_kv/pallas_call | solution.py:295
  260.2 12.0 %project_q.3 = bf16[576,512]{1,0:T(8,128)(2,1)S(1)} custom-call(s32[70]{0:T(128)S(1)} %concatenate.28.refs_0_, bf16[576,8192]{1,0:T(8,128)(2,1)} %get-tuple-element.34.refs_1_, bf16[1024,640]{1,0:T(8,128)(2,1)} %copy-done.2, bf16[1024,640]{1,0:T(8,128)(2,1)} %collective-permute-done.22.refs_27_.refs_3_, ...), custom_call_target="tpu_custom_call" | custom-call | flops 4831838208 | bytes 17825792 | tf_op jit(solution)/shard_map/project_q/pallas_call | solution.py:348
  272.2 2.5 collective-permute-start.42
  274.7 19.5 %project_q.4 = (bf16[576,512]{1,0:T(8,128)(2,1)}, bf16[576,512]{1,0:T(8,128)(2,1)}) custom-call(s32[70]{0:T(128)S(1)} %concatenate.28.refs_0_, bf16[576,8192]{1,0:T(8,128)(2,1)} %get-tuple-element.34.refs_1_, bf16[1024,640]{1,0:T(8,128)(2,1)} %collective-permute-done.12.refs_18_.refs_2_, bf16[1024,640]{1,0:T(8,128)(2,1)} %collective-permute-done.13.refs_19_.refs_3_, ...), custom_call_target="tpu_custom_call" | custom-call | flops 9663676416 | bytes 26214400 | tf_op jit(solution)/shard_map/project_q/pallas_call | solution.py:348
  294.3 1.4 collective-permute-start.41
  297.3 3.0 collective-permute-start.43
  300.3 11.9 %project_q.5.q0 = bf16[576,512]{1,0:T(8,128)(2,1)S(1)} custom-call(s32[70]{0:T(128)S(1)} %concatenate.28.refs_0_, bf16[576,8192]{1,0:T(8,128)(2,1)} %get-tuple-element.34.refs_1_, bf16[8192,512]{1,0:T(8,128)(2,1)} %refs_2_.1, f32[1,512]{1,0:T(1,128)S(1)} %bitcast.29, f32[576,128]{1,0:T(8,128)S(1)} %pad_maximum_fusion.3.refs_43_.refs_11_.refs_20_.refs_4_, ...), custom_call_target="tpu_custom_call" | custom-call | flops 4831838208 | bytes 17825792 | tf_op jit(solution)/shard_map/project_q/pallas_call | solution.py:348
  312.2 15.9 %collective-permute-done.43.kv2 = bf16[576,256]{1,0:T(8,128)(2,1)S(1)} collective-permute-done((bf16[576,256]{1,0:T(8,128)(2,1)}, bf16[576,256]{1,0:T(8,128)(2,1)S(1)}, u32[]{:S(2)}, u32[]{:S(2)}) %collective-permute-start.43) | collective-permute-done | bytes 294944 | tf_op jit(solution)/shard_map/ppermute | solution.py:24
  328.1 7.4 %collective-permute-done.44.kv3 = bf16[576,256]{1,0:T(8,128)(2,1)S(1)} collective-permute-done((bf16[576,256]{1,0:T(8,128)(2,1)}, bf16[576,256]{1,0:T(8,128)(2,1)S(1)}, u32[]{:S(2)}, u32[]{:S(2)}) %collective-permute-start.44) | collective-permute-done | bytes 294944 | tf_op jit(solution)/shard_map/ppermute | solution.py:24
  335.6 16.6 %attend.1 = bf16[2048,512]{1,0:T(8,128)(2,1)} custom-call(s32[12]{0:T(128)S(1)} %concatenate.27.info_ref, s32[128]{0:T(128)S(1)} %reshape.320.text_ref, bf16[576,512]{1,0:T(8,128)(2,1)S(1)} %project_q.5.q0, bf16[576,512]{1,0:T(8,128)(2,1)S(1)} %collective-permute-done.39.q1, bf16[576,512]{1,0:T(8,128)(2,1)S(1)} %collective-permute-done.40.q2, ...), custom_call_target="tpu_custom_call" | custom-call | tf_op jit(solution)/shard_map/attend/pallas_call | solution.py:492
  (157 shorter events, 34.7 us)
Async XLA Ops:
  7.2 27.8 %collective-permute-start.2 = (bf16[64,8192]{1,0:T(8,128)(2,1)}, bf16[64,8192]{1,0:T(8,128)(2,1)}, u32[]{:S(2)}, u32[]{:S(2)}) collective-permute-start(bf16[64,8192]{1,0:T(8,128)(2,1)} %shard_map.127.refs_1_), channel_id=1, source_target_pairs={{0,4},{4,8},{8,12},{12,0},{1,5},{5,9},{9,13},{13,1},{2,6},{6,10},{... | collective-permute-start | bytes 3145736 | tf_op jit(solution)/shard_map/ppermute | solution.py:24
  9.7 28.0 %collective-permute-start = (bf16[64,8192]{1,0:T(8,128)(2,1)}, bf16[64,8192]{1,0:T(8,128)(2,1)}, u32[]{:S(2)}, u32[]{:S(2)}) collective-permute-start(bf16[64,8192]{1,0:T(8,128)(2,1)} %shard_map.127.refs_1_), channel_id=1, source_target_pairs={{0,12},{4,0},{8,4},{12,8},{1,13},{5,1},{9,5},{13,9},{2,14},{6,2},{... | collective-permute-start | bytes 3145736 | tf_op jit(solution)/shard_map/ppermute | solution.py:24
  24.1 33.3 %collective-permute-start.5 = (bf16[64,8192]{1,0:T(8,128)(2,1)}, bf16[64,8192]{1,0:T(8,128)(2,1)}, u32[]{:S(2)}, u32[]{:S(2)}) collective-permute-start(bf16[64,8192]{1,0:T(8,128)(2,1)} %shard_map.128.refs_2_), channel_id=1, source_target_pairs={{0,4},{4,8},{8,12},{12,0},{1,5},{5,9},{9,13},{13,1},{2,6},{6,10},{... | collective-permute-start | bytes 3145736 | tf_op jit(solution)/shard_map/ppermute | solution.py:24
  24.2 41.9 %all-to-all-start = ((bf16[8,16,8192]{2,1,0:T(8,128)(2,1)}), bf16[8,16,8192]{2,1,0:T(8,128)(2,1)}, u32[]{:S(2)}, u32[]{:S(2)}) async-start(bf16[8,16,8192]{2,1,0:T(8,128)(2,1)} %spread.1), calls=%async_computation | async-start | bytes 4194304 | tf_op jit(solution)/shard_map/all_to_all | solution.py:573
  29.6 31.8 %collective-permute-start.29 = (bf16[1024,640]{1,0:T(8,128)(2,1)}, bf16[1024,640]{1,0:T(8,128)(2,1)}, u32[]{:S(2)}, u32[]{:S(2)}) collective-permute-start(bf16[1024,640]{1,0:T(8,128)(2,1)} %pad_maximum_fusion.1), channel_id=1, source_target_pairs={{0,1},{1,2},{2,3},{3,0},{4,5},{5,6},{6,7},{7,4},{8,9},{9,10},{10,1... | collective-permute-start | bytes 3932168 | tf_op jit(solution)/shard_map/ppermute | solution.py:24
  30.9 29.3 %collective-permute-start.1 = (bf16[64,8192]{1,0:T(8,128)(2,1)S(1)}, bf16[64,8192]{1,0:T(8,128)(2,1)}, u32[]{:S(2)}, u32[]{:S(2)}) collective-permute-start(bf16[64,8192]{1,0:T(8,128)(2,1)S(1)} %copy-done.6), channel_id=1, source_target_pairs={{0,12},{4,0},{8,4},{12,8},{1,13},{5,1},{9,5},{13,9},{2,14},{6,2},{... | collective-permute-start | bytes 3145736 | tf_op jit(solution)/shard_map/ppermute | solution.py:24
  35.0 34.7 %collective-permute-start.12 = (bf16[1024,640]{1,0:T(8,128)(2,1)}, bf16[1024,640]{1,0:T(8,128)(2,1)}, u32[]{:S(2)}, u32[]{:S(2)}) collective-permute-start(bf16[1024,640]{1,0:T(8,128)(2,1)} %pad_maximum_fusion.1), channel_id=1, source_target_pairs={{0,3},{1,0},{2,1},{3,2},{4,7},{5,4},{6,5},{7,6},{8,11},{9,8},{10,9... | collective-permute-start | bytes 3932168 | tf_op jit(solution)/shard_map/ppermute | solution.py:24
  37.7 51.8 %collective-permute-start.21 = (bf16[1024,640]{1,0:T(8,128)(2,1)}, bf16[1024,640]{1,0:T(8,128)(2,1)}, u32[]{:S(2)}, u32[]{:S(2)}) collective-permute-start(bf16[1024,640]{1,0:T(8,128)(2,1)} %pad_maximum_fusion.2), channel_id=1, source_target_pairs={{0,1},{1,2},{2,3},{3,0},{4,5},{5,6},{6,7},{7,4},{8,9},{9,10},{10,1... | collective-permute-start | bytes 3932168 | tf_op jit(solution)/shard_map/ppermute | solution.py:24
  57.5 34.7 %collective-permute-start.13 = (bf16[1024,640]{1,0:T(8,128)(2,1)}, bf16[1024,640]{1,0:T(8,128)(2,1)}, u32[]{:S(2)}, u32[]{:S(2)}) collective-permute-start(bf16[1024,640]{1,0:T(8,128)(2,1)} %pad_maximum_fusion.2), channel_id=1, source_target_pairs={{0,3},{1,0},{2,1},{3,2},{4,7},{5,4},{6,5},{7,6},{8,11},{9,8},{10,9... | collective-permute-start | bytes 3932168 | tf_op jit(solution)/shard_map/ppermute | solution.py:24
  60.2 44.8 %collective-permute-start.3 = (bf16[64,8192]{1,0:T(8,128)(2,1)}, bf16[64,8192]{1,0:T(8,128)(2,1)}, u32[]{:S(2)}, u32[]{:S(2)}) collective-permute-start(bf16[64,8192]{1,0:T(8,128)(2,1)} %collective-permute-done.2.refs_7_), channel_id=1, source_target_pairs={{0,4},{4,8},{8,12},{12,0},{1,5},{5,9},{9,13},{13,1},{2,6},{6,10},{... | collective-permute-start | bytes 3145736 | tf_op jit(solution)/shard_map/ppermute | solution.py:24
  61.5 45.8 %collective-permute-start.4 = (bf16[64,8192]{1,0:T(8,128)(2,1)}, bf16[64,8192]{1,0:T(8,128)(2,1)}, u32[]{:S(2)}, u32[]{:S(2)}) collective-permute-start(bf16[64,8192]{1,0:T(8,128)(2,1)} %collective-permute-done.1.refs_4_), channel_id=1, source_target_pairs={{0,12},{4,0},{8,4},{12,8},{1,13},{5,1},{9,5},{13,9},{2,14},{6,2},{... | collective-permute-start | bytes 3145736 | tf_op jit(solution)/shard_map/ppermute | solution.py:24
  69.7 38.2 %collective-permute-start.11 = (bf16[3,16,8192]{2,1,0:T(8,128)(2,1)}, bf16[3,16,8192]{2,1,0:T(8,128)(2,1)}, u32[]{:S(2)}, u32[]{:S(2)}) collective-permute-start(bf16[3,16,8192]{2,1,0:T(8,128)(2,1)} %norm_image.3.refs_10_), channel_id=1, source_target_pairs={{0,4},{4,8},{8,12},{12,0},{1,5},{5,9},{9,13},{13,1},{2,6},{6,10},{... | collective-permute-start | bytes 2359304 | tf_op jit(solution)/shard_map/ppermute | solution.py:24
  89.5 31.8 %collective-permute-start.32 = (bf16[1024,640]{1,0:T(8,128)(2,1)}, bf16[1024,640]{1,0:T(8,128)(2,1)}, u32[]{:S(2)}, u32[]{:S(2)}) collective-permute-start(bf16[1024,640]{1,0:T(8,128)(2,1)} %collective-permute-done.29.refs_34_.refs_10_), channel_id=1, source_target_pairs={{0,16},{16,0},{1,17},{17,1},{2,18},{18,2},{3,19},{19,3},{4,20},{20... | collective-permute-start | bytes 3932168 | tf_op jit(solution)/shard_map/ppermute | solution.py:24
  90.6 149.9 %copy-start.10 = (f32[640]{0:T(1024)}, f32[640]{0:T(1024)S(1)}, u32[]{:S(2)}) copy-start(f32[640]{0:T(1024)S(1)} %pad_maximum_fusion.5) | copy-start | bytes 7684
  92.2 4.8 %collective-permute-start.38 = (f32[640]{0:T(1024)S(1)}, f32[640]{0:T(1024)S(1)}, u32[]{:S(2)}, u32[]{:S(2)}) collective-permute-start(f32[640]{0:T(1024)S(1)} %pad_maximum_fusion.5), channel_id=1, source_target_pairs={{0,1},{1,2},{2,3},{3,0},{4,5},{5,6},{6,7},{7,4},{8,9},{9,10},{10,1... | collective-permute-start | bytes 7688 | tf_op jit(solution)/shard_map/ppermute | solution.py:24
  97.0 4.0 %collective-permute-start.37 = (f32[640]{0:T(1024)S(1)}, f32[640]{0:T(1024)S(1)}, u32[]{:S(2)}, u32[]{:S(2)}) collective-permute-start(f32[640]{0:T(1024)S(1)} %pad_maximum_fusion.5), channel_id=1, source_target_pairs={{0,2},{1,3},{2,0},{3,1},{4,6},{5,7},{6,4},{7,5},{8,10},{9,11},{10,... | collective-permute-start | bytes 7688 | tf_op jit(solution)/shard_map/ppermute | solution.py:24
  100.9 2.8 collective-permute-start.36
  103.8 26.5 %collective-permute-start.30 = (bf16[1024,640]{1,0:T(8,128)(2,1)}, bf16[1024,640]{1,0:T(8,128)(2,1)}, u32[]{:S(2)}, u32[]{:S(2)}) collective-permute-start(bf16[1024,640]{1,0:T(8,128)(2,1)} %collective-permute-done.29.refs_34_.refs_10_), channel_id=1, source_target_pairs={{0,32},{32,64},{64,96},{96,0},{1,33},{33,65},{65,97},{97,1},{2,34}... | collective-permute-start | bytes 3932168 | tf_op jit(solution)/shard_map/ppermute | solution.py:24
  105.0 33.2 %collective-permute-start.20 = (bf16[1024,640]{1,0:T(8,128)(2,1)}, bf16[1024,640]{1,0:T(8,128)(2,1)S(1)}, u32[]{:S(2)}, u32[]{:S(2)}) collective-permute-start(bf16[1024,640]{1,0:T(8,128)(2,1)} %collective-permute-done.12.refs_18_.refs_2_), channel_id=1, source_target_pairs={{0,3},{1,0},{2,1},{3,2},{4,7},{5,4},{6,5},{7,6},{8,11},{9,8},{10,9... | collective-permute-start | bytes 3932168 | tf_op jit(solution)/shard_map/ppermute | solution.py:24
  107.3 12.8 %collective-permute-start.7 = (bf16[3,16,8192]{2,1,0:T(8,128)(2,1)}, bf16[3,16,8192]{2,1,0:T(8,128)(2,1)}, u32[]{:S(2)}, u32[]{:S(2)}) collective-permute-start(bf16[3,16,8192]{2,1,0:T(8,128)(2,1)} %norm_image.3.refs_10_), channel_id=1, source_target_pairs={{0,12},{4,0},{8,4},{12,8},{1,13},{5,1},{9,5},{13,9},{2,14},{6,2},{... | collective-permute-start | bytes 2359304 | tf_op jit(solution)/shard_map/ppermute | solution.py:24
  107.9 31.2 %collective-permute-start.16 = (bf16[1024,640]{1,0:T(8,128)(2,1)}, bf16[1024,640]{1,0:T(8,128)(2,1)}, u32[]{:S(2)}, u32[]{:S(2)}) collective-permute-start(bf16[1024,640]{1,0:T(8,128)(2,1)} %collective-permute-done.12.refs_18_.refs_2_), channel_id=1, source_target_pairs={{0,16},{16,0},{1,17},{17,1},{2,18},{18,2},{3,19},{19,3},{4,20},{20... | collective-permute-start | bytes 3932168 | tf_op jit(solution)/shard_map/ppermute | solution.py:24
  120.1 38.2 %collective-permute-start.14 = (bf16[1024,640]{1,0:T(8,128)(2,1)}, bf16[1024,640]{1,0:T(8,128)(2,1)}, u32[]{:S(2)}, u32[]{:S(2)}) collective-permute-start(bf16[1024,640]{1,0:T(8,128)(2,1)} %collective-permute-done.12.refs_18_.refs_2_), channel_id=1, source_target_pairs={{0,32},{32,64},{64,96},{96,0},{1,33},{33,65},{65,97},{97,1},{2,34}... | collective-permute-start | bytes 3932168 | tf_op jit(solution)/shard_map/ppermute | solution.py:24
  121.3 43.3 %collective-permute-start.33 = (bf16[1024,640]{1,0:T(8,128)(2,1)}, bf16[1024,640]{1,0:T(8,128)(2,1)}, u32[]{:S(2)}, u32[]{:S(2)}) collective-permute-start(bf16[1024,640]{1,0:T(8,128)(2,1)} %collective-permute-done.21.refs_35_.refs_11_), channel_id=1, source_target_pairs={{0,16},{16,0},{1,17},{17,1},{2,18},{18,2},{3,19},{19,3},{4,20},{20... | collective-permute-start | bytes 3932168 | tf_op jit(solution)/shard_map/ppermute | solution.py:24
  130.2 35.7 %collective-permute-start.31 = (bf16[1024,640]{1,0:T(8,128)(2,1)}, bf16[1024,640]{1,0:T(8,128)(2,1)}, u32[]{:S(2)}, u32[]{:S(2)}) collective-permute-start(bf16[1024,640]{1,0:T(8,128)(2,1)} %collective-permute-done.21.refs_35_.refs_11_), channel_id=1, source_target_pairs={{0,96},{32,0},{64,32},{96,64},{1,97},{33,1},{65,33},{97,65},{2,98}... | collective-permute-start | bytes 3932168 | tf_op jit(solution)/shard_map/ppermute | solution.py:24
  138.1 77.9 %copy-start.2 = (bf16[1024,640]{1,0:T(8,128)(2,1)}, bf16[1024,640]{1,0:T(8,128)(2,1)S(1)}, u32[]{:S(2)}) copy-start(bf16[1024,640]{1,0:T(8,128)(2,1)S(1)} %collective-permute-done.20.refs_26_.refs_2_) | copy-start | bytes 3932164
  138.1 27.8 %collective-permute-start.8 = (bf16[4,16,8192]{2,1,0:T(8,128)(2,1)}, bf16[4,16,8192]{2,1,0:T(8,128)(2,1)}, u32[]{:S(2)}, u32[]{:S(2)}) collective-permute-start(bf16[4,16,8192]{2,1,0:T(8,128)(2,1)} %norm_image.2.refs_9_), channel_id=1, source_target_pairs={{0,4},{4,8},{8,12},{12,0},{1,5},{5,9},{9,13},{13,1},{2,6},{6,10},{... | collective-permute-start | bytes 3145736 | tf_op jit(solution)/shard_map/ppermute | solution.py:24
  139.1 32.4 %collective-permute-start.22 = (bf16[1024,640]{1,0:T(8,128)(2,1)}, bf16[1024,640]{1,0:T(8,128)(2,1)}, u32[]{:S(2)}, u32[]{:S(2)}) collective-permute-start(bf16[1024,640]{1,0:T(8,128)(2,1)} %collective-permute-done.21.refs_35_.refs_11_), channel_id=1, source_target_pairs={{0,1},{1,2},{2,3},{3,0},{4,5},{5,6},{6,7},{7,4},{8,9},{9,10},{10,1... | collective-permute-start | bytes 3932168 | tf_op jit(solution)/shard_map/ppermute | solution.py:24
  158.3 16.1 %collective-permute-start.17 = (bf16[1024,640]{1,0:T(8,128)(2,1)}, bf16[1024,640]{1,0:T(8,128)(2,1)}, u32[]{:S(2)}, u32[]{:S(2)}) collective-permute-start(bf16[1024,640]{1,0:T(8,128)(2,1)} %collective-permute-done.13.refs_19_.refs_3_), channel_id=1, source_target_pairs={{0,16},{16,0},{1,17},{17,1},{2,18},{18,2},{3,19},{19,3},{4,20},{20... | collective-permute-start | bytes 3932168 | tf_op jit(solution)/shard_map/ppermute | solution.py:24
  164.6 30.6 %collective-permute-start.15 = (bf16[1024,640]{1,0:T(8,128)(2,1)}, bf16[1024,640]{1,0:T(8,128)(2,1)}, u32[]{:S(2)}, u32[]{:S(2)}) collective-permute-start(bf16[1024,640]{1,0:T(8,128)(2,1)} %collective-permute-done.13.refs_19_.refs_3_), channel_id=1, source_target_pairs={{0,96},{32,0},{64,32},{96,64},{1,97},{33,1},{65,33},{97,65},{2,98}... | collective-permute-start | bytes 3932168 | tf_op jit(solution)/shard_map/ppermute | solution.py:24
  165.9 29.3 %collective-permute-start.6 = (bf16[4,16,8192]{2,1,0:T(8,128)(2,1)}, bf16[4,16,8192]{2,1,0:T(8,128)(2,1)}, u32[]{:S(2)}, u32[]{:S(2)}) collective-permute-start(bf16[4,16,8192]{2,1,0:T(8,128)(2,1)} %norm_image.2.refs_9_), channel_id=1, source_target_pairs={{0,12},{4,0},{8,4},{12,8},{1,13},{5,1},{9,5},{13,9},{2,14},{6,2},{... | collective-permute-start | bytes 3145736 | tf_op jit(solution)/shard_map/ppermute | solution.py:24
  166.0 42.7 %collective-permute-start.9 = (bf16[4,16,8192]{2,1,0:T(8,128)(2,1)}, bf16[4,16,8192]{2,1,0:T(8,128)(2,1)}, u32[]{:S(2)}, u32[]{:S(2)}) collective-permute-start(bf16[4,16,8192]{2,1,0:T(8,128)(2,1)} %collective-permute-done.8.refs_15_), channel_id=1, source_target_pairs={{0,4},{4,8},{8,12},{12,0},{1,5},{5,9},{9,13},{13,1},{2,6},{6,10},{... | collective-permute-start | bytes 3145736 | tf_op jit(solution)/shard_map/ppermute | solution.py:24
  171.5 36.0 %collective-permute-start.10 = (bf16[3,16,8192]{2,1,0:T(8,128)(2,1)}, bf16[3,16,8192]{2,1,0:T(8,128)(2,1)}, u32[]{:S(2)}, u32[]{:S(2)}) collective-permute-start(bf16[3,16,8192]{2,1,0:T(8,128)(2,1)} %collective-permute-done.7.refs_12_), channel_id=1, source_target_pairs={{0,12},{4,0},{8,4},{12,8},{1,13},{5,1},{9,5},{13,9},{2,14},{6,2},{... | collective-permute-start | bytes 2359304 | tf_op jit(solution)/shard_map/ppermute | solution.py:24
  174.5 41.9 %collective-permute-start.25 = (bf16[1024,640]{1,0:T(8,128)(2,1)S(1)}, bf16[1024,640]{1,0:T(8,128)(2,1)}, u32[]{:S(2)}, u32[]{:S(2)}) collective-permute-start(bf16[1024,640]{1,0:T(8,128)(2,1)S(1)} %collective-permute-done.20.refs_26_.refs_2_), channel_id=1, source_target_pairs={{0,16},{16,0},{1,17},{17,1},{2,18},{18,2},{3,19},{19,3},{4,20},{20... | collective-permute-start | bytes 3932168 | tf_op jit(solution)/shard_map/ppermute | solution.py:24
  195.2 30.8 %collective-permute-start.23 = (bf16[1024,640]{1,0:T(8,128)(2,1)S(1)}, bf16[1024,640]{1,0:T(8,128)(2,1)}, u32[]{:S(2)}, u32[]{:S(2)}) collective-permute-start(bf16[1024,640]{1,0:T(8,128)(2,1)S(1)} %collective-permute-done.20.refs_26_.refs_2_), channel_id=1, source_target_pairs={{0,32},{32,64},{64,96},{96,0},{1,33},{33,65},{65,97},{97,1},{2,34}... | collective-permute-start | bytes 3932168 | tf_op jit(solution)/shard_map/ppermute | solution.py:24
  195.2 20.8 %collective-permute-start.34 = (bf16[1024,640]{1,0:T(8,128)(2,1)}, bf16[1024,640]{1,0:T(8,128)(2,1)}, u32[]{:S(2)}, u32[]{:S(2)}) collective-permute-start(bf16[1024,640]{1,0:T(8,128)(2,1)} %collective-permute-done.30.refs_36_.refs_12_), channel_id=1, source_target_pairs={{0,16},{16,0},{1,17},{17,1},{2,18},{18,2},{3,19},{19,3},{4,20},{20... | collective-permute-start | bytes 3932168 | tf_op jit(solution)/shard_map/ppermute | solution.py:24
  207.5 20.2 %collective-permute-start.18 = (bf16[1024,640]{1,0:T(8,128)(2,1)}, bf16[1024,640]{1,0:T(8,128)(2,1)}, u32[]{:S(2)}, u32[]{:S(2)}) collective-permute-start(bf16[1024,640]{1,0:T(8,128)(2,1)} %collective-permute-done.14.refs_20_.refs_4_), channel_id=1, source_target_pairs={{0,16},{16,0},{1,17},{17,1},{2,18},{18,2},{3,19},{19,3},{4,20},{20... | collective-permute-start | bytes 3932168 | tf_op jit(solution)/shard_map/ppermute | solution.py:24
  208.7 30.6 %collective-permute-start.24 = (bf16[1024,640]{1,0:T(8,128)(2,1)}, bf16[1024,640]{1,0:T(8,128)(2,1)}, u32[]{:S(2)}, u32[]{:S(2)}) collective-permute-start(bf16[1024,640]{1,0:T(8,128)(2,1)} %collective-permute-done.22.refs_27_.refs_3_), channel_id=1, source_target_pairs={{0,96},{32,0},{64,32},{96,64},{1,97},{33,1},{65,33},{97,65},{2,98}... | collective-permute-start | bytes 3932168 | tf_op jit(solution)/shard_map/ppermute | solution.py:24
  216.1 24.6 %collective-permute-start.26 = (bf16[1024,640]{1,0:T(8,128)(2,1)}, bf16[1024,640]{1,0:T(8,128)(2,1)S(1)}, u32[]{:S(2)}, u32[]{:S(2)}) collective-permute-start(bf16[1024,640]{1,0:T(8,128)(2,1)} %collective-permute-done.22.refs_27_.refs_3_), channel_id=1, source_target_pairs={{0,16},{16,0},{1,17},{17,1},{2,18},{18,2},{3,19},{19,3},{4,20},{20... | collective-permute-start | bytes 3932168 | tf_op jit(solution)/shard_map/ppermute | solution.py:24
  216.4 24.2 %collective-permute-start.35 = (bf16[1024,640]{1,0:T(8,128)(2,1)}, bf16[1024,640]{1,0:T(8,128)(2,1)S(1)}, u32[]{:S(2)}, u32[]{:S(2)}) collective-permute-start(bf16[1024,640]{1,0:T(8,128)(2,1)} %collective-permute-done.31.refs_37_.refs_13_), channel_id=1, source_target_pairs={{0,16},{16,0},{1,17},{17,1},{2,18},{18,2},{3,19},{19,3},{4,20},{20... | collective-permute-start | bytes 3932168 | tf_op jit(solution)/shard_map/ppermute | solution.py:24
  226.0 14.6 %collective-permute-start.19 = (bf16[1024,640]{1,0:T(8,128)(2,1)}, bf16[1024,640]{1,0:T(8,128)(2,1)S(1)}, u32[]{:S(2)}, u32[]{:S(2)}) collective-permute-start(bf16[1024,640]{1,0:T(8,128)(2,1)} %collective-permute-done.15.refs_21_.refs_5_), channel_id=1, source_target_pairs={{0,16},{16,0},{1,17},{17,1},{2,18},{18,2},{3,19},{19,3},{4,20},{20... | collective-permute-start | bytes 3932168 | tf_op jit(solution)/shard_map/ppermute | solution.py:24
  227.7 12.9 %collective-permute-start.27 = (bf16[1024,640]{1,0:T(8,128)(2,1)}, bf16[1024,640]{1,0:T(8,128)(2,1)S(1)}, u32[]{:S(2)}, u32[]{:S(2)}) collective-permute-start(bf16[1024,640]{1,0:T(8,128)(2,1)} %collective-permute-done.23.refs_28_.refs_4_), channel_id=1, source_target_pairs={{0,16},{16,0},{1,17},{17,1},{2,18},{18,2},{3,19},{19,3},{4,20},{20... | collective-permute-start | bytes 3932168 | tf_op jit(solution)/shard_map/ppermute | solution.py:24
  239.3 3.7 %collective-permute-start.28 = (bf16[1024,640]{1,0:T(8,128)(2,1)}, bf16[1024,640]{1,0:T(8,128)(2,1)S(1)}, u32[]{:S(2)}, u32[]{:S(2)}) collective-permute-start(bf16[1024,640]{1,0:T(8,128)(2,1)} %collective-permute-done.24.refs_29_.refs_5_), channel_id=1, source_target_pairs={{0,16},{16,0},{1,17},{17,1},{2,18},{18,2},{3,19},{19,3},{4,20},{20... | collective-permute-start | bytes 3932168 | tf_op jit(solution)/shard_map/ppermute | solution.py:24
  272.2 28.1 %collective-permute-start.42 = (bf16[576,256]{1,0:T(8,128)(2,1)}, bf16[576,256]{1,0:T(8,128)(2,1)S(1)}, u32[]{:S(2)}, u32[]{:S(2)}) collective-permute-start(bf16[576,256]{1,0:T(8,128)(2,1)} %get-tuple-element.40), channel_id=1, source_target_pairs={{0,3},{1,0},{2,1},{3,2},{4,7},{5,4},{6,5},{7,6},{8,11},{9,8},{10,9... | collective-permute-start | bytes 884744 | tf_op jit(solution)/shard_map/ppermute | solution.py:24
  294.2 41.4 %collective-permute-start.39 = (bf16[576,512]{1,0:T(8,128)(2,1)}, bf16[576,512]{1,0:T(8,128)(2,1)S(1)}, u32[]{:S(2)}, u32[]{:S(2)}) collective-permute-start(bf16[576,512]{1,0:T(8,128)(2,1)} %get-tuple-element.36), channel_id=1, source_target_pairs={{0,3},{1,0},{2,1},{3,2},{4,7},{5,4},{6,5},{7,6},{8,11},{9,8},{10,9... | collective-permute-start | bytes 1769480 | tf_op jit(solution)/shard_map/ppermute | solution.py:24
  294.3 41.3 %collective-permute-start.41 = (bf16[576,512]{1,0:T(8,128)(2,1)}, bf16[576,512]{1,0:T(8,128)(2,1)S(1)}, u32[]{:S(2)}, u32[]{:S(2)}) collective-permute-start(bf16[576,512]{1,0:T(8,128)(2,1)} %get-tuple-element.38), channel_id=1, source_target_pairs={{0,1},{1,2},{2,3},{3,0},{4,5},{5,6},{6,7},{7,4},{8,9},{9,10},{10,1... | collective-permute-start | bytes 1769480 | tf_op jit(solution)/shard_map/ppermute | solution.py:24
  295.7 39.8 %collective-permute-start.40 = (bf16[576,512]{1,0:T(8,128)(2,1)S(1)}, bf16[576,512]{1,0:T(8,128)(2,1)S(1)}, u32[]{:S(2)}, u32[]{:S(2)}) collective-permute-start(bf16[576,512]{1,0:T(8,128)(2,1)S(1)} %project_q.3), channel_id=1, source_target_pairs={{0,2},{1,3},{2,0},{3,1},{4,6},{5,7},{6,4},{7,5},{8,10},{9,11},{10,... | collective-permute-start | bytes 1769480 | tf_op jit(solution)/shard_map/ppermute | solution.py:24
  297.3 30.8 %collective-permute-start.43 = (bf16[576,256]{1,0:T(8,128)(2,1)}, bf16[576,256]{1,0:T(8,128)(2,1)S(1)}, u32[]{:S(2)}, u32[]{:S(2)}) collective-permute-start(bf16[576,256]{1,0:T(8,128)(2,1)} %copy-done.1), channel_id=1, source_target_pairs={{0,2},{1,3},{2,0},{3,1},{4,6},{5,7},{6,4},{7,5},{8,10},{9,11},{10,... | collective-permute-start | bytes 884744 | tf_op jit(solution)/shard_map/ppermute | solution.py:24
  300.2 35.3 %collective-permute-start.44 = (bf16[576,256]{1,0:T(8,128)(2,1)}, bf16[576,256]{1,0:T(8,128)(2,1)S(1)}, u32[]{:S(2)}, u32[]{:S(2)}) collective-permute-start(bf16[576,256]{1,0:T(8,128)(2,1)} %copy-done), channel_id=1, source_target_pairs={{0,1},{1,2},{2,3},{3,0},{4,5},{5,6},{6,7},{7,4},{8,9},{9,10},{10,1... | collective-permute-start | bytes 884744 | tf_op jit(solution)/shard_map/ppermute | solution.py:24
  (19 other events, 300.6 us)

commit v4 on v3

--- a/solution.py
+++ b/solution.py
@@ -124,9 +124,13 @@
         for delta, first, count in tile:
             lanes = pl.ds(lane, count)
             lane += count
-            if delta == 0:
-                source = own_kv if first == 512 else own_q.at[:, pl.ds(first, count)]
-                found.append((source, weight_buf.at[slot, :, lanes]))
+            if delta == 0 and first == 512:
+                found.append((own_kv, weight_buf.at[slot, :, lanes]))
+            elif delta == 0:
+                for index in range(8):
+                    rows = pl.ds(index * PIECE, PIECE)
+                    source = own_q.at[rows, pl.ds(first, count)]
+                    found.append((source, weight_buf.at[slot, rows, lanes]))
             else:
                 for index, piece in enumerate(pieces[delta]):
                     row = pl.multiple_of(place_ref[66 + index // 2] + index % 2 * PIECE, PIECE)
@@ -161,25 +165,9 @@
                 for copy in copies(tile, index % slots):
                     copy.wait()
 
-        half = rows_ref.shape[1] // 2
-
-        def half_step(part, carry):
-            inner = pl.ds(pl.multiple_of(part * half, half), half)
-            product = jnp.dot(
-                rows_ref[:, inner], weight_buf[slot, inner, :], preferred_element_type=jnp.float32
-            )
-
-            @pl.when(part == 0)
-            def _():
-                sum_ref[slot] = product
-
-            @pl.when(part == 1)
-            def _():
-                sum_ref[slot] += product
-
-            return carry
-
-        lax.fori_loop(0, 2, half_step, 0)
+        sum_ref[slot] = jnp.dot(
+            rows_ref[...], weight_buf[slot], preferred_element_type=jnp.float32
+        )
         for index in range(len(tiles)):
             @pl.when(number == index)
             def _(index=index):
@@ -198,9 +186,9 @@
     sources = refs[1:17]
     own_kv = refs[17]
     pieces = {1: refs[18:26], 2: refs[26:34], 3: refs[34:42]}
-    bias_ref, cos_ref, sin_ref = refs[42:45]
-    outs, compact_ref = refs[45:49], refs[49]
-    rows_ref, weight_buf, sum_ref, sems, weight_sems, copy_sem = refs[50:]
+    bias_ref, q_bias_ref, cos_ref, sin_ref = refs[42:46]
+    outs, out_ref, compact_ref = refs[46:50], refs[50], refs[51]
+    rows_ref, weight_buf, sum_ref, sems, weight_sems, copy_sem = refs[52:]
     copies = weight_tile(None, own_kv, pieces, place_ref, weight_buf, weight_sems)
     copy_out = pltpu.make_async_copy(rows_ref, compact_ref, copy_sem)
 
@@ -235,7 +223,9 @@
         copy_out.start()
 
     def finish(index, product):
-        if index == 0:
+        if index >= 2:
+            store_heads(out_ref, index - 2, product, q_bias_ref, cos_ref, sin_ref)
+        if index != 1:
             return
         odd = place_ref[65] == 1
         halves = [
@@ -259,7 +249,10 @@
             outs[2][:, lanes] = away[part].astype(jnp.bfloat16)
             outs[3][:, lanes] = jnp.where(odd, near[part], away[part]).astype(jnp.bfloat16)
 
-    tiles = [[(0, 512, HD), (1, 512, HD)], [(2, 512, HD), (3, 512, HD)]]
+    tiles = [
+        [(0, 512, HD), (1, 512, HD)], [(2, 512, HD), (3, 512, HD)],
+        [(2, 0, COLUMNS)], [(2, COLUMNS, COLUMNS)],
+    ]
     run_tiles(tiles, copies, rows_ref, weight_buf, sum_ref, finish, assemble)
     copy_out.wait()
 
@@ -287,7 +280,8 @@
     return pl.BlockSpec(shape, lambda i, place: (0,) * len(shape))
 
 
-def project_kv(place, texts, images, own_kv, pieces, bias, cosine, sine):
+def project_kv(place, texts, images, own_kv, pieces, bias, q_bias, cosine, sine):
+    query_shape = (ROWS, q_bias.shape[1])
     features = texts[0].shape[1]
     far_spec = pl.BlockSpec(memory_space=pltpu.HBM)
     flat = [piece for delta in (1, 2, 3) for piece in pieces[delta]]
@@ -298,8 +292,8 @@
             num_scalar_prefetch=1,
             grid=(1,),
             in_specs=[far_spec] * (17 + len(flat))
-            + [whole(bias.shape), whole((ROWS, HD)), whole((ROWS, HD))],
-            out_specs=(whole(shape),) * 4 + (far_spec,),
+            + [whole(bias.shape), whole(q_bias.shape), whole((ROWS, HD)), whole((ROWS, HD))],
+            out_specs=(whole(shape),) * 4 + (whole(query_shape), far_spec),
             scratch_shapes=[
                 pltpu.VMEM((ROWS, features), jnp.bfloat16),
                 pltpu.VMEM((2, features, COLUMNS), jnp.bfloat16),
@@ -310,11 +304,14 @@
             ],
         ),
         out_shape=(jax.ShapeDtypeStruct(shape, jnp.bfloat16),) * 4
-        + (pltpu.HBM((ROWS, features), jnp.bfloat16),),
+        + (
+            jax.ShapeDtypeStruct(query_shape, jnp.bfloat16),
+            pltpu.HBM((ROWS, features), jnp.bfloat16),
+        ),
         compiler_params=pltpu.CompilerParams(vmem_limit_bytes=40 << 20),
-        cost_estimate=cost(2 * COLUMNS, features),
+        cost_estimate=cost(4 * COLUMNS, features),
         name="project_kv",
-    )(place, *far([*texts, *images, own_kv, *flat]), bias, cosine, sine)
+    )(place, *far([*texts, *images, own_kv, *flat]), bias, q_bias, cosine, sine)
 
 
 def project_q(place, compact, own_q, pieces, biases, cosine, sine):
@@ -334,8 +331,21 @@
         rows_ref, weight_buf, sum_ref, row_sem, weight_sems = refs
         found = {delta: weight_refs[8 * i:8 * i + 8] for i, delta in enumerate(deltas)}
         copies = weight_tile(weight_refs[0], None, found, place_ref, weight_buf, weight_sems)
-        copy_in = pltpu.make_async_copy(compact_ref, rows_ref, row_sem)
-        copy_in.start()
+        share = ROWS // 6
+        copies_in = [
+            pltpu.make_async_copy(
+                compact_ref.at[pl.ds(part * share, share), :],
+                rows_ref.at[pl.ds(part * share, share), :],
+                row_sem.at[part],
+            )
+            for part in range(6)
+        ]
+        for copy in copies_in:
+            copy.start()
+
+        def rows_here():
+            for copy in copies_in:
+                copy.wait()
 
         def finish(index, product):
             store_heads(
@@ -343,7 +353,7 @@
             )
 
         tiles = [[(delta, first, COLUMNS)] for delta in deltas for first in (0, COLUMNS)]
-        run_tiles(tiles, copies, rows_ref, weight_buf, sum_ref, finish, copy_in.wait)
+        run_tiles(tiles, copies, rows_ref, weight_buf, sum_ref, finish, rows_here)
 
     return pl.pallas_call(
         kernel,
@@ -358,7 +368,7 @@
                 pltpu.VMEM((ROWS, features), jnp.bfloat16),
                 pltpu.VMEM((2, features, COLUMNS), jnp.bfloat16),
                 pltpu.VMEM((2, ROWS, COLUMNS), jnp.float32),
-                pltpu.SemaphoreType.DMA,
+                pltpu.SemaphoreType.DMA((6,)),
                 pltpu.SemaphoreType.DMA((2, 16)),
             ],
         ),
@@ -566,23 +576,11 @@
     y = lax.axis_index("y")
     gain = norm_gain.reshape(1, -1)
 
-    row_groups = lax.dynamic_slice_in_dim(tile_group, group * 4, 4)
-    matches = row_groups[None, :] == jnp.arange(8, dtype=jnp.int32)[:, None]
-    chosen = jnp.sum(jnp.where(matches, jnp.arange(4, dtype=jnp.int32)[None, :], 0), axis=1)
-    outgoing = spread(image_rows, chosen.astype(jnp.int32))
-    arrived = lax.all_to_all(outgoing, ("x", "c"), split_axis=0, concat_axis=0, tiled=True)
-
-    outgoing, text_rows = lax.optimization_barrier((outgoing, text_rows))
-    t_low = norm_text(text_rows, gain, 0, 64)
-    t3_low = shifted(t_low, "z", 1)
-    t1_low = shifted(t_low, "z", -1)
-
     quarter = 2 * core + x % 2
-    begin, t_low = lax.optimization_barrier((quarter * 2 * PIECE, t_low))
     own_kv = jnp.concatenate([k_weight, v_weight], axis=1)
 
     def own_part(half):
-        first = begin + half * PIECE
+        first = quarter * 2 * PIECE + half * PIECE
         return jnp.concatenate(
             [
                 lax.dynamic_slice_in_dim(weight, first, PIECE, 0)
@@ -599,6 +597,18 @@
     direct[3, 0] = shifted(low, "y", 1)
 
     low, high, text_rows = lax.optimization_barrier((low, high, text_rows))
+    t_low = norm_text(text_rows, gain, 0, 64)
+    t3_low = shifted(t_low, "z", 1)
+    t1_low = shifted(t_low, "z", -1)
+
+    row_groups = lax.dynamic_slice_in_dim(tile_group, group * 4, 4)
+    matches = row_groups[None, :] == jnp.arange(8, dtype=jnp.int32)[:, None]
+    chosen = jnp.sum(jnp.where(matches, jnp.arange(4, dtype=jnp.int32)[None, :], 0), axis=1)
+    image_rows, t_low = lax.optimization_barrier((image_rows, t_low))
+    outgoing = spread(image_rows, chosen.astype(jnp.int32))
+    arrived = lax.all_to_all(outgoing, ("x", "c"), split_axis=0, concat_axis=0, tiled=True)
+
+    outgoing, text_rows = lax.optimization_barrier((outgoing, text_rows))
     t_high = norm_text(text_rows, gain, 64, 64)
     t3_high = shifted(t_high, "z", 1)
     t1_high = shifted(t_high, "z", -1)
@@ -618,6 +628,7 @@
     }
     quarters = jnp.stack([quarter ^ 0, quarter ^ 1, quarter ^ 2, quarter ^ 3]) * 2 * PIECE
 
+    doc_ids, direct[2, 0] = lax.optimization_barrier((doc_ids, direct[2, 0]))
     place, slots, text_index, info, in_doc = tables(
         tile_group, tile_offset, seq_len, doc_ids, group, z, y, quarters
     )
@@ -645,10 +656,12 @@
 
     texts = (t_low, t_high, t1_low, t1_high, t2_low, t2_high, t3_low, t3_high)
     images = (i_low, i_high, i1_low, i1_high, i2_low, i2_high, i3_low, i3_high)
-    *pairs, compact = project_kv(place, texts, images, own_kv, pieces, kv_bias, cosine, sine)
-    queries = {}
+    *pairs, far_query, compact = project_kv(
+        place, texts, images, own_kv, pieces, kv_bias, q_biases[2], cosine, sine
+    )
+    queries = {2: far_query}
     after = compact
-    for deltas in ((2,), (1, 3), (0,)):
+    for deltas in ((1, 3), (0,)):
         found = project_q(
             place, after, q_weight, pieces,
             {delta: q_biases[delta] for delta in deltas}, cosine, sine,

time: 353 us -> 383 us (1.085)
  waiting for transfers between devices: 154 us -> 194 us
  Pallas kernels: 92.6 us -> 84.4 us
    ppermute x45, waiting for transfers between devices: 154 us -> 194 us  [shifted(): lax.ppermute(block, axis, [(low, (low + step) % count) for low in range(c...]
    pallas_call x3 -> x2, Pallas kernels: 43.4 us -> 29.8 us  [project_q(): pl.pallas_call(kernel, grid_spec=pltpu.PrefetchScalarGridSpec(num_scalar_...]
    pallas_call x1, Pallas kernels: 16 us -> 21.6 us  [project_kv(): pl.pallas_call(project_kv_kernel, grid_spec=pltpu.PrefetchScalarGridSpec(...]
  transfers between devices with their start and end apart: 46 -> 46, of which waited for: 18 -> 16; matrix products, arithmetic and copies ran while one was open for 7% -> 4% of each run, Pallas kernels for 12% -> 11%
where the time goes in v4:
time: 383 us; the launch traced here: 382 us
  waiting for transfers between devices  194 us (51%)
  Pallas kernels  84.4 us (22%)
  starting transfers between devices  73.5 us (19%)
  local copies, waits for them, and re-layouts  13.8 us (4%)
  other arithmetic  12.9 us (3%)
  between operations  4.12 us (1%)
    ppermute x45, waiting for transfers between devices, shifted(): lax.ppermute(block, axis, [(low, (low + step) % count) for low in range(c...  194 us
    ppermute x45, starting transfers between devices, shifted(): lax.ppermute(block, axis, [(low, (low + step) % count) for low in range(c...  66.8 us
    pallas_call x2, Pallas kernels, project_q(): pl.pallas_call(kernel, grid_spec=pltpu.PrefetchScalarGridSpec(num_scalar_...  29.8 us
    pallas_call x1, Pallas kernels, project_kv(): pl.pallas_call(project_kv_kernel, grid_spec=pltpu.PrefetchScalarGridSpec(...  21.6 us
    pallas_call x1, Pallas kernels, attend(): pl.pallas_call(attend_kernel, grid_spec=pltpu.PrefetchScalarGridSpec(num_...  16.6 us
    pallas_call x2, Pallas kernels, norm_image(): pl.pallas_call(norm_image_kernel, grid_spec=pltpu.PrefetchScalarGridSpec(...  8.1 us
  transfers between devices with their start and end apart: 46, of which 16 were waited for; matrix products, arithmetic and copies ran while one was open for 4% of the time, Pallas kernels for 11%

profile of v4, /device:TPU:1, one launch (start us, length us, event | category | flops | bytes accessed | tf_op | source)
XLA Modules:
  0.0 382.5 jit_solution(9995660990710678144)
XLA Ops:
  0.0 2.1 copy.18
  2.1 1.8 copy.19
  3.9 1.8 constant_dynamic-slice_fusion
  7.8 2.5 shard_map.127.refs_1_
  10.4 2.5 collective-permute-start.4
  12.8 2.1 collective-permute-start.2
  15.7 3.3 spread.1
  19.0 2.6 shard_map.128.refs_2_
  21.6 1.4 collective-permute-start.29
  23.0 2.6 collective-permute-start.3
  25.6 12.5 %collective-permute-done.4.refs_7_ = bf16[64,8192]{1,0:T(8,128)(2,1)} collective-permute-done((bf16[64,8192]{1,0:T(8,128)(2,1)}, bf16[64,8192]{1,0:T(8,128)(2,1)}, u32[]{:S(2)}, u32[]{:S(2)}) %collective-permute-start.4) | collective-permute-done | bytes 1048608 | tf_op jit(solution)/shard_map/ppermute | solution.py:24
  38.1 2.7 collective-permute-start
  40.9 6.7 %all-to-all-start = ((bf16[8,16,8192]{2,1,0:T(8,128)(2,1)}), bf16[8,16,8192]{2,1,0:T(8,128)(2,1)}, u32[]{:S(2)}, u32[]{:S(2)}) async-start(bf16[8,16,8192]{2,1,0:T(8,128)(2,1)} %spread.1), calls=%async_computation | async-start | bytes 4194304 | tf_op jit(solution)/shard_map/all_to_all | solution.py:609
  47.5 13.0 %collective-permute-done.7.refs_8_ = bf16[64,8192]{1,0:T(8,128)(2,1)} collective-permute-done((bf16[64,8192]{1,0:T(8,128)(2,1)}, bf16[64,8192]{1,0:T(8,128)(2,1)}, u32[]{:S(2)}, u32[]{:S(2)}) %collective-permute-start.7) | collective-permute-done | bytes 1048608 | tf_op jit(solution)/shard_map/ppermute | solution.py:24
  60.6 2.7 collective-permute-start.14
  63.3 2.7 collective-permute-start.6
  67.2 5.5 %collective-permute-start.32 = (bf16[1024,640]{1,0:T(8,128)(2,1)}, bf16[1024,640]{1,0:T(8,128)(2,1)}, u32[]{:S(2)}, u32[]{:S(2)}) collective-permute-start(bf16[1024,640]{1,0:T(8,128)(2,1)} %collective-permute-done.29.refs_34_.refs_10_), channel_id=1, source_target_pairs={{0,16},{16,0},{1,17},{17,1},{2,18},{18,2},{3,19},{19,3},{4,20},{20... | collective-permute-start | bytes 3932168 | tf_op jit(solution)/shard_map/ppermute | solution.py:24
  74.6 3.5 norm_image.3.refs_10_
  78.1 2.7 collective-permute-done.21.refs_35_.refs_11_
  80.8 14.4 %collective-permute-done.14.refs_19_.refs_3_ = bf16[1024,640]{1,0:T(8,128)(2,1)} collective-permute-done((bf16[1024,640]{1,0:T(8,128)(2,1)S(1)}, bf16[1024,640]{1,0:T(8,128)(2,1)}, u32[]{:S(2)}, u32[]{:S(2)}) %collective-permute-start.14) | collective-permute-done | bytes 1310752 | tf_op jit(solution)/shard_map/ppermute | solution.py:24
  95.2 2.5 collective-permute-start.37
  100.4 4.4 %collective-permute-start.17 = (bf16[1024,640]{1,0:T(8,128)(2,1)}, bf16[1024,640]{1,0:T(8,128)(2,1)}, u32[]{:S(2)}, u32[]{:S(2)}) collective-permute-start(bf16[1024,640]{1,0:T(8,128)(2,1)} %collective-permute-done.refs_18_.refs_2_), channel_id=1, source_target_pairs={{0,16},{16,0},{1,17},{17,1},{2,18},{18,2},{3,19},{19,3},{4,20},{20... | collective-permute-start | bytes 3932168 | tf_op jit(solution)/shard_map/ppermute | solution.py:24
  106.0 3.5 collective-permute-start.1
  110.1 16.8 %collective-permute-done.30.refs_36_.refs_12_ = bf16[1024,640]{1,0:T(8,128)(2,1)} collective-permute-done((bf16[1024,640]{1,0:T(8,128)(2,1)}, bf16[1024,640]{1,0:T(8,128)(2,1)}, u32[]{:S(2)}, u32[]{:S(2)}) %collective-permute-start.30) | collective-permute-done | bytes 1310752 | tf_op jit(solution)/shard_map/ppermute | solution.py:24
  128.2 1.4 collective-permute-start.22
  132.5 22.5 %collective-permute-done.15.refs_20_.refs_4_ = bf16[1024,640]{1,0:T(8,128)(2,1)} collective-permute-done((bf16[1024,640]{1,0:T(8,128)(2,1)}, bf16[1024,640]{1,0:T(8,128)(2,1)}, u32[]{:S(2)}, u32[]{:S(2)}) %collective-permute-start.15) | collective-permute-done | bytes 1310752 | tf_op jit(solution)/shard_map/ppermute | solution.py:24
  155.0 5.0 %collective-permute-start.18 = (bf16[1024,640]{1,0:T(8,128)(2,1)}, bf16[1024,640]{1,0:T(8,128)(2,1)}, u32[]{:S(2)}, u32[]{:S(2)}) collective-permute-start(bf16[1024,640]{1,0:T(8,128)(2,1)} %collective-permute-done.14.refs_19_.refs_3_), channel_id=1, source_target_pairs={{0,16},{16,0},{1,17},{17,1},{2,18},{18,2},{3,19},{19,3},{4,20},{20... | collective-permute-start | bytes 3932168 | tf_op jit(solution)/shard_map/ppermute | solution.py:24
  164.4 4.6 %norm_image.2.refs_9_ = bf16[4,16,8192]{2,1,0:T(8,128)(2,1)} custom-call(s32[4]{0:T(128)} %bitcast.37, bf16[8,16,8192]{2,1,0:T(8,128)(2,1)} %all-to-all-done.rows_ref, f32[1,8192]{1,0:T(1,128)} %bitcast.35), custom_call_target="tpu_custom_call" | custom-call | tf_op jit(solution)/shard_map/norm_image/pallas_call | solution.py:59
  169.9 1.8 collective-permute-start.8
  172.4 18.2 %collective-permute-done.16.refs_21_.refs_5_ = bf16[1024,640]{1,0:T(8,128)(2,1)} collective-permute-done((bf16[1024,640]{1,0:T(8,128)(2,1)}, bf16[1024,640]{1,0:T(8,128)(2,1)}, u32[]{:S(2)}, u32[]{:S(2)}) %collective-permute-start.16) | collective-permute-done | bytes 1310752 | tf_op jit(solution)/shard_map/ppermute | solution.py:24
  192.1 4.1 %pad_maximum_fusion.refs_17_ = bf16[8192,128]{1,0:T(8,128)(2,1)} fusion(bf16[8192,64]{1,0:T(8,128)(2,1)} %copy.19, bf16[8192,64]{1,0:T(8,128)(2,1)S(1)} %copy.18), kind=kLoop, calls=%fused_computation.3 | loop fusion | flops 4194304 | bytes 4194304 | tf_op jit(solution)/shard_map/concatenate | solution.py:580
  196.2 15.3 %collective-permute-done.13.refs_16_ = bf16[3,16,8192]{2,1,0:T(8,128)(2,1)S(1)} collective-permute-done((bf16[3,16,8192]{2,1,0:T(8,128)(2,1)S(1)}, bf16[3,16,8192]{2,1,0:T(8,128)(2,1)S(1)}, u32[]{:S(2)}, u32[]{:S(2)}) %collective-permute-start.13) | collective-permute-done | bytes 786464 | tf_op jit(solution)/shard_map/ppermute | solution.py:24
  211.4 1.4 collective-permute-start.25
  213.8 6.7 %collective-permute-done.12.refs_14_ = bf16[3,16,8192]{2,1,0:T(8,128)(2,1)} collective-permute-done((bf16[3,16,8192]{2,1,0:T(8,128)(2,1)}, bf16[3,16,8192]{2,1,0:T(8,128)(2,1)}, u32[]{:S(2)}, u32[]{:S(2)}) %collective-permute-start.12) | collective-permute-done | bytes 786464 | tf_op jit(solution)/shard_map/ppermute | solution.py:24
  222.1 1.5 collective-permute-start.35
  225.5 19.1 %collective-permute-done.23.refs_28_ = bf16[1024,640]{1,0:T(8,128)(2,1)} collective-permute-done((bf16[1024,640]{1,0:T(8,128)(2,1)}, bf16[1024,640]{1,0:T(8,128)(2,1)}, u32[]{:S(2)}, u32[]{:S(2)}) %collective-permute-start.23) | collective-permute-done | bytes 1310752 | tf_op jit(solution)/shard_map/ppermute | solution.py:24
  245.6 4.5 %collective-permute-done.24.refs_29_ = bf16[1024,640]{1,0:T(8,128)(2,1)} collective-permute-done((bf16[1024,640]{1,0:T(8,128)(2,1)}, bf16[1024,640]{1,0:T(8,128)(2,1)}, u32[]{:S(2)}, u32[]{:S(2)}) %collective-permute-start.24) | collective-permute-done | bytes 1310752 | tf_op jit(solution)/shard_map/ppermute | solution.py:24
  250.1 2.0 collective-permute-start.28
  255.2 23.1 %collective-permute-done.11.refs_13_ = bf16[4,16,8192]{2,1,0:T(8,128)(2,1)S(1)} collective-permute-done((bf16[4,16,8192]{2,1,0:T(8,128)(2,1)}, bf16[4,16,8192]{2,1,0:T(8,128)(2,1)S(1)}, u32[]{:S(2)}, u32[]{:S(2)}) %collective-permute-start.11) | collective-permute-done | bytes 1048608 | tf_op jit(solution)/shard_map/ppermute | solution.py:24
  280.1 21.6 %project_kv.1 = (bf16[576,256]{1,0:T(8,128)(2,1)S(1)}, bf16[576,256]{1,0:T(8,128)(2,1)S(1)}, bf16[576,256]{1,0:T(8,128)(2,1)S(1)}, bf16[576,256]{1,0:T(8,128)(2,...) custom-call(s32[70]{0:T(128)S(1)} %concatenate.30.refs_0_, bf16[64,8192]{1,0:T(8,128)(2,1)} %shard_map.127.refs_1_, ...), custom_call_target="tpu_custom_call" | custom-call | flops 9663676416 | bytes 26214400 | tf_op jit(solution)/shard_map/project_kv/pallas_call | solution.py:289
  303.1 3.7 collective-permute-start.42
  306.7 18.3 %project_q.2 = (bf16[576,512]{1,0:T(8,128)(2,1)}, bf16[576,512]{1,0:T(8,128)(2,1)}) custom-call(s32[70]{0:T(128)S(1)} %concatenate.30.refs_0_, bf16[576,8192]{1,0:T(8,128)(2,1)} %get-tuple-element.34.refs_1_, bf16[1024,640]{1,0:T(8,128)(2,1)} %collective-permute-done.refs_18_.refs_2_, bf16[1024,640]{1,0:T(8,128)(2,1)} %collective-permute-done.14.refs_19_.refs_3_, ...), custom_call_target="tpu_custom_call" | custom-call | flops 9663676416 | bytes 26214400 | tf_op jit(solution)/shard_map/project_q/pallas_call | solution.py:358
  325.1 1.5 collective-permute-start.41
  328.2 3.0 collective-permute-start.43
  331.2 11.4 %project_q.3.q0 = bf16[576,512]{1,0:T(8,128)(2,1)S(1)} custom-call(s32[70]{0:T(128)S(1)} %concatenate.30.refs_0_, bf16[576,8192]{1,0:T(8,128)(2,1)} %get-tuple-element.34.refs_1_, bf16[8192,512]{1,0:T(8,128)(2,1)} %refs_2_.1, f32[1,512]{1,0:T(1,128)S(1)} %bitcast.28, f32[576,128]{1,0:T(8,128)S(1)} %pad_maximum_fusion.3.refs_44_.refs_20_.refs_4_, ...), custom_call_target="tpu_custom_call" | custom-call | flops 4831838208 | bytes 17825792 | tf_op jit(solution)/shard_map/project_q/pallas_call | solution.py:358
  342.6 15.7 %collective-permute-done.43.kv2 = bf16[576,256]{1,0:T(8,128)(2,1)S(1)} collective-permute-done((bf16[576,256]{1,0:T(8,128)(2,1)}, bf16[576,256]{1,0:T(8,128)(2,1)S(1)}, u32[]{:S(2)}, u32[]{:S(2)}) %collective-permute-start.43) | collective-permute-done | bytes 294944 | tf_op jit(solution)/shard_map/ppermute | solution.py:24
  358.3 7.6 %collective-permute-done.44.kv3 = bf16[576,256]{1,0:T(8,128)(2,1)S(1)} collective-permute-done((bf16[576,256]{1,0:T(8,128)(2,1)}, bf16[576,256]{1,0:T(8,128)(2,1)S(1)}, u32[]{:S(2)}, u32[]{:S(2)}) %collective-permute-start.44) | collective-permute-done | bytes 294944 | tf_op jit(solution)/shard_map/ppermute | solution.py:24
  365.9 16.6 %attend.1 = bf16[2048,512]{1,0:T(8,128)(2,1)} custom-call(s32[12]{0:T(128)S(1)} %concatenate.29.info_ref, s32[128]{0:T(128)S(1)} %reshape.320.text_ref, bf16[576,512]{1,0:T(8,128)(2,1)S(1)} %project_q.3.q0, bf16[576,512]{1,0:T(8,128)(2,1)S(1)} %collective-permute-done.39.q1, bf16[576,512]{1,0:T(8,128)(2,1)S(1)} %collective-permute-done.40.q2, ...), custom_call_target="tpu_custom_call" | custom-call | tf_op jit(solution)/shard_map/attend/pallas_call | solution.py:502
  (166 shorter events, 31.7 us)
Async XLA Ops:
  10.4 27.8 %collective-permute-start.4 = (bf16[64,8192]{1,0:T(8,128)(2,1)}, bf16[64,8192]{1,0:T(8,128)(2,1)}, u32[]{:S(2)}, u32[]{:S(2)}) collective-permute-start(bf16[64,8192]{1,0:T(8,128)(2,1)} %shard_map.127.refs_1_), channel_id=1, source_target_pairs={{0,4},{4,8},{8,12},{12,0},{1,5},{5,9},{9,13},{13,1},{2,6},{6,10},{... | collective-permute-start | bytes 3145736 | tf_op jit(solution)/shard_map/ppermute | solution.py:24
  12.8 34.7 %collective-permute-start.2 = (bf16[64,8192]{1,0:T(8,128)(2,1)}, bf16[64,8192]{1,0:T(8,128)(2,1)}, u32[]{:S(2)}, u32[]{:S(2)}) collective-permute-start(bf16[64,8192]{1,0:T(8,128)(2,1)} %shard_map.127.refs_1_), channel_id=1, source_target_pairs={{0,12},{4,0},{8,4},{12,8},{1,13},{5,1},{9,5},{13,9},{2,14},{6,2},{... | collective-permute-start | bytes 3145736 | tf_op jit(solution)/shard_map/ppermute | solution.py:24
  21.5 39.1 %collective-permute-start.7 = (bf16[64,8192]{1,0:T(8,128)(2,1)}, bf16[64,8192]{1,0:T(8,128)(2,1)}, u32[]{:S(2)}, u32[]{:S(2)}) collective-permute-start(bf16[64,8192]{1,0:T(8,128)(2,1)} %shard_map.128.refs_2_), channel_id=1, source_target_pairs={{0,4},{4,8},{8,12},{12,0},{1,5},{5,9},{9,13},{13,1},{2,6},{6,10},{... | collective-permute-start | bytes 3145736 | tf_op jit(solution)/shard_map/ppermute | solution.py:24
  21.6 41.7 %collective-permute-start.29 = (bf16[1024,640]{1,0:T(8,128)(2,1)}, bf16[1024,640]{1,0:T(8,128)(2,1)}, u32[]{:S(2)}, u32[]{:S(2)}) collective-permute-start(bf16[1024,640]{1,0:T(8,128)(2,1)} %pad_maximum_fusion.1), channel_id=1, source_target_pairs={{0,1},{1,2},{2,3},{3,0},{4,5},{5,6},{6,7},{7,4},{8,9},{9,10},{10,1... | collective-permute-start | bytes 3932168 | tf_op jit(solution)/shard_map/ppermute | solution.py:24
  23.0 40.3 %collective-permute-start.3 = (bf16[64,8192]{1,0:T(8,128)(2,1)}, bf16[64,8192]{1,0:T(8,128)(2,1)}, u32[]{:S(2)}, u32[]{:S(2)}) collective-permute-start(bf16[64,8192]{1,0:T(8,128)(2,1)} %shard_map.128.refs_2_), channel_id=1, source_target_pairs={{0,12},{4,0},{8,4},{12,8},{1,13},{5,1},{9,5},{13,9},{2,14},{6,2},{... | collective-permute-start | bytes 3145736 | tf_op jit(solution)/shard_map/ppermute | solution.py:24
  38.1 29.1 %collective-permute-start = (bf16[1024,640]{1,0:T(8,128)(2,1)}, bf16[1024,640]{1,0:T(8,128)(2,1)}, u32[]{:S(2)}, u32[]{:S(2)}) collective-permute-start(bf16[1024,640]{1,0:T(8,128)(2,1)} %pad_maximum_fusion.1), channel_id=1, source_target_pairs={{0,3},{1,0},{2,1},{3,2},{4,7},{5,4},{6,5},{7,6},{8,11},{9,8},{10,9... | collective-permute-start | bytes 3932168 | tf_op jit(solution)/shard_map/ppermute | solution.py:24
  40.9 33.8 %all-to-all-start = ((bf16[8,16,8192]{2,1,0:T(8,128)(2,1)}), bf16[8,16,8192]{2,1,0:T(8,128)(2,1)}, u32[]{:S(2)}, u32[]{:S(2)}) async-start(bf16[8,16,8192]{2,1,0:T(8,128)(2,1)} %spread.1), calls=%async_computation | async-start | bytes 4194304 | tf_op jit(solution)/shard_map/all_to_all | solution.py:609
  47.5 33.3 %collective-permute-start.21 = (bf16[1024,640]{1,0:T(8,128)(2,1)S(1)}, bf16[1024,640]{1,0:T(8,128)(2,1)}, u32[]{:S(2)}, u32[]{:S(2)}) collective-permute-start(bf16[1024,640]{1,0:T(8,128)(2,1)S(1)} %pad_maximum_fusion.2), channel_id=1, source_target_pairs={{0,1},{1,2},{2,3},{3,0},{4,5},{5,6},{6,7},{7,4},{8,9},{9,10},{10,1... | collective-permute-start | bytes 3932168 | tf_op jit(solution)/shard_map/ppermute | solution.py:24
  60.6 34.6 %collective-permute-start.14 = (bf16[1024,640]{1,0:T(8,128)(2,1)S(1)}, bf16[1024,640]{1,0:T(8,128)(2,1)}, u32[]{:S(2)}, u32[]{:S(2)}) collective-permute-start(bf16[1024,640]{1,0:T(8,128)(2,1)S(1)} %pad_maximum_fusion.2), channel_id=1, source_target_pairs={{0,3},{1,0},{2,1},{3,2},{4,7},{5,4},{6,5},{7,6},{8,11},{9,8},{10,9... | collective-permute-start | bytes 3932168 | tf_op jit(solution)/shard_map/ppermute | solution.py:24
  63.3 41.4 %collective-permute-start.5 = (bf16[64,8192]{1,0:T(8,128)(2,1)}, bf16[64,8192]{1,0:T(8,128)(2,1)}, u32[]{:S(2)}, u32[]{:S(2)}) collective-permute-start(bf16[64,8192]{1,0:T(8,128)(2,1)} %collective-permute-done.4.refs_7_), channel_id=1, source_target_pairs={{0,4},{4,8},{8,12},{12,0},{1,5},{5,9},{9,13},{13,1},{2,6},{6,10},{... | collective-permute-start | bytes 3145736 | tf_op jit(solution)/shard_map/ppermute | solution.py:24
  63.3 42.6 %collective-permute-start.6 = (bf16[64,8192]{1,0:T(8,128)(2,1)}, bf16[64,8192]{1,0:T(8,128)(2,1)}, u32[]{:S(2)}, u32[]{:S(2)}) collective-permute-start(bf16[64,8192]{1,0:T(8,128)(2,1)} %collective-permute-done.3.refs_4_), channel_id=1, source_target_pairs={{0,12},{4,0},{8,4},{12,8},{1,13},{5,1},{9,5},{13,9},{2,14},{6,2},{... | collective-permute-start | bytes 3145736 | tf_op jit(solution)/shard_map/ppermute | solution.py:24
  67.2 42.3 %collective-permute-start.32 = (bf16[1024,640]{1,0:T(8,128)(2,1)}, bf16[1024,640]{1,0:T(8,128)(2,1)}, u32[]{:S(2)}, u32[]{:S(2)}) collective-permute-start(bf16[1024,640]{1,0:T(8,128)(2,1)} %collective-permute-done.29.refs_34_.refs_10_), channel_id=1, source_target_pairs={{0,16},{16,0},{1,17},{17,1},{2,18},{18,2},{3,19},{19,3},{4,20},{20... | collective-permute-start | bytes 3932168 | tf_op jit(solution)/shard_map/ppermute | solution.py:24
  74.6 150.2 %copy-start.15 = (f32[640]{0:T(1024)}, f32[640]{0:T(1024)S(1)}, u32[]{:S(2)}) copy-start(f32[640]{0:T(1024)S(1)} %pad_maximum_fusion.5) | copy-start | bytes 7684
  80.8 16.9 %collective-permute-start.38 = (f32[640]{0:T(1024)S(1)}, f32[640]{0:T(1024)S(1)}, u32[]{:S(2)}, u32[]{:S(2)}) collective-permute-start(f32[640]{0:T(1024)S(1)} %pad_maximum_fusion.5), channel_id=1, source_target_pairs={{0,1},{1,2},{2,3},{3,0},{4,5},{5,6},{6,7},{7,4},{8,9},{9,10},{10,1... | collective-permute-start | bytes 7688 | tf_op jit(solution)/shard_map/ppermute | solution.py:24
  95.2 4.0 %collective-permute-start.37 = (f32[640]{0:T(1024)S(1)}, f32[640]{0:T(1024)S(1)}, u32[]{:S(2)}, u32[]{:S(2)}) collective-permute-start(f32[640]{0:T(1024)S(1)} %pad_maximum_fusion.5), channel_id=1, source_target_pairs={{0,2},{1,3},{2,0},{3,1},{4,6},{5,7},{6,4},{7,5},{8,10},{9,11},{10,... | collective-permute-start | bytes 7688 | tf_op jit(solution)/shard_map/ppermute | solution.py:24
  97.7 2.7 collective-permute-start.36
  99.2 27.8 %collective-permute-start.30 = (bf16[1024,640]{1,0:T(8,128)(2,1)}, bf16[1024,640]{1,0:T(8,128)(2,1)}, u32[]{:S(2)}, u32[]{:S(2)}) collective-permute-start(bf16[1024,640]{1,0:T(8,128)(2,1)} %collective-permute-done.29.refs_34_.refs_10_), channel_id=1, source_target_pairs={{0,32},{32,64},{64,96},{96,0},{1,33},{33,65},{65,97},{97,1},{2,34}... | collective-permute-start | bytes 3932168 | tf_op jit(solution)/shard_map/ppermute | solution.py:24
  100.4 27.8 %collective-permute-start.17 = (bf16[1024,640]{1,0:T(8,128)(2,1)}, bf16[1024,640]{1,0:T(8,128)(2,1)}, u32[]{:S(2)}, u32[]{:S(2)}) collective-permute-start(bf16[1024,640]{1,0:T(8,128)(2,1)} %collective-permute-done.refs_18_.refs_2_), channel_id=1, source_target_pairs={{0,16},{16,0},{1,17},{17,1},{2,18},{18,2},{3,19},{19,3},{4,20},{20... | collective-permute-start | bytes 3932168 | tf_op jit(solution)/shard_map/ppermute | solution.py:24
  104.8 50.2 %collective-permute-start.15 = (bf16[1024,640]{1,0:T(8,128)(2,1)}, bf16[1024,640]{1,0:T(8,128)(2,1)}, u32[]{:S(2)}, u32[]{:S(2)}) collective-permute-start(bf16[1024,640]{1,0:T(8,128)(2,1)} %collective-permute-done.refs_18_.refs_2_), channel_id=1, source_target_pairs={{0,32},{32,64},{64,96},{96,0},{1,33},{33,65},{65,97},{97,1},{2,34}... | collective-permute-start | bytes 3932168 | tf_op jit(solution)/shard_map/ppermute | solution.py:24
  106.0 54.0 %collective-permute-start.1 = (bf16[1024,640]{1,0:T(8,128)(2,1)}, bf16[1024,640]{1,0:T(8,128)(2,1)}, u32[]{:S(2)}, u32[]{:S(2)}) collective-permute-start(bf16[1024,640]{1,0:T(8,128)(2,1)} %collective-permute-done.refs_18_.refs_2_), channel_id=1, source_target_pairs={{0,3},{1,0},{2,1},{3,2},{4,7},{5,4},{6,5},{7,6},{8,11},{9,8},{10,9... | collective-permute-start | bytes 3932168 | tf_op jit(solution)/shard_map/ppermute | solution.py:24
  109.5 52.4 %collective-permute-start.33 = (bf16[1024,640]{1,0:T(8,128)(2,1)}, bf16[1024,640]{1,0:T(8,128)(2,1)S(1)}, u32[]{:S(2)}, u32[]{:S(2)}) collective-permute-start(bf16[1024,640]{1,0:T(8,128)(2,1)} %collective-permute-done.21.refs_35_.refs_11_), channel_id=1, source_target_pairs={{0,16},{16,0},{1,17},{17,1},{2,18},{18,2},{3,19},{19,3},{4,20},{20... | collective-permute-start | bytes 3932168 | tf_op jit(solution)/shard_map/ppermute | solution.py:24
  126.9 42.1 %collective-permute-start.31 = (bf16[1024,640]{1,0:T(8,128)(2,1)}, bf16[1024,640]{1,0:T(8,128)(2,1)}, u32[]{:S(2)}, u32[]{:S(2)}) collective-permute-start(bf16[1024,640]{1,0:T(8,128)(2,1)} %collective-permute-done.21.refs_35_.refs_11_), channel_id=1, source_target_pairs={{0,96},{32,0},{64,32},{96,64},{1,97},{33,1},{65,33},{97,65},{2,98}... | collective-permute-start | bytes 3932168 | tf_op jit(solution)/shard_map/ppermute | solution.py:24
  128.2 41.7 %collective-permute-start.22 = (bf16[1024,640]{1,0:T(8,128)(2,1)}, bf16[1024,640]{1,0:T(8,128)(2,1)}, u32[]{:S(2)}, u32[]{:S(2)}) collective-permute-start(bf16[1024,640]{1,0:T(8,128)(2,1)} %collective-permute-done.21.refs_35_.refs_11_), channel_id=1, source_target_pairs={{0,1},{1,2},{2,3},{3,0},{4,5},{5,6},{6,7},{7,4},{8,9},{9,10},{10,1... | collective-permute-start | bytes 3932168 | tf_op jit(solution)/shard_map/ppermute | solution.py:24
  155.0 17.3 %collective-permute-start.18 = (bf16[1024,640]{1,0:T(8,128)(2,1)}, bf16[1024,640]{1,0:T(8,128)(2,1)}, u32[]{:S(2)}, u32[]{:S(2)}) collective-permute-start(bf16[1024,640]{1,0:T(8,128)(2,1)} %collective-permute-done.14.refs_19_.refs_3_), channel_id=1, source_target_pairs={{0,16},{16,0},{1,17},{17,1},{2,18},{18,2},{3,19},{19,3},{4,20},{20... | collective-permute-start | bytes 3932168 | tf_op jit(solution)/shard_map/ppermute | solution.py:24
  160.0 30.6 %collective-permute-start.16 = (bf16[1024,640]{1,0:T(8,128)(2,1)}, bf16[1024,640]{1,0:T(8,128)(2,1)}, u32[]{:S(2)}, u32[]{:S(2)}) collective-permute-start(bf16[1024,640]{1,0:T(8,128)(2,1)} %collective-permute-done.14.refs_19_.refs_3_), channel_id=1, source_target_pairs={{0,96},{32,0},{64,32},{96,64},{1,97},{33,1},{65,33},{97,65},{2,98}... | collective-permute-start | bytes 3932168 | tf_op jit(solution)/shard_map/ppermute | solution.py:24
  161.9 29.6 %collective-permute-start.9 = (bf16[3,16,8192]{2,1,0:T(8,128)(2,1)}, bf16[3,16,8192]{2,1,0:T(8,128)(2,1)}, u32[]{:S(2)}, u32[]{:S(2)}) collective-permute-start(bf16[3,16,8192]{2,1,0:T(8,128)(2,1)} %norm_image.3.refs_10_), channel_id=1, source_target_pairs={{0,12},{4,0},{8,4},{12,8},{1,13},{5,1},{9,5},{13,9},{2,14},{6,2},{... | collective-permute-start | bytes 2359304 | tf_op jit(solution)/shard_map/ppermute | solution.py:24
  169.0 43.9 %collective-permute-start.10 = (bf16[4,16,8192]{2,1,0:T(8,128)(2,1)}, bf16[4,16,8192]{2,1,0:T(8,128)(2,1)}, u32[]{:S(2)}, u32[]{:S(2)}) collective-permute-start(bf16[4,16,8192]{2,1,0:T(8,128)(2,1)} %norm_image.2.refs_9_), channel_id=1, source_target_pairs={{0,4},{4,8},{8,12},{12,0},{1,5},{5,9},{9,13},{13,1},{2,6},{6,10},{... | collective-permute-start | bytes 3145736 | tf_op jit(solution)/shard_map/ppermute | solution.py:24
  169.9 43.2 %collective-permute-start.8 = (bf16[4,16,8192]{2,1,0:T(8,128)(2,1)}, bf16[4,16,8192]{2,1,0:T(8,128)(2,1)}, u32[]{:S(2)}, u32[]{:S(2)}) collective-permute-start(bf16[4,16,8192]{2,1,0:T(8,128)(2,1)} %norm_image.2.refs_9_), channel_id=1, source_target_pairs={{0,12},{4,0},{8,4},{12,8},{1,13},{5,1},{9,5},{13,9},{2,14},{6,2},{... | collective-permute-start | bytes 3145736 | tf_op jit(solution)/shard_map/ppermute | solution.py:24
  172.3 79.9 %copy-start.16 = (s32[1,2048]{1,0:T(1,128)S(1)}, s32[1,2048]{1,0:T(1,128)}, u32[]{:S(2)}) copy-start(s32[1,2048]{1,0:T(1,128)} %param.18) | copy-start | bytes 24580
  172.3 39.2 %collective-permute-start.13 = (bf16[3,16,8192]{2,1,0:T(8,128)(2,1)S(1)}, bf16[3,16,8192]{2,1,0:T(8,128)(2,1)S(1)}, u32[]{:S(2)}, u32[]{:S(2)}) collective-permute-start(bf16[3,16,8192]{2,1,0:T(8,128)(2,1)S(1)} %copy-done.3), channel_id=1, source_target_pairs={{0,4},{4,8},{8,12},{12,0},{1,5},{5,9},{9,13},{13,1},{2,6},{6,10},{... | collective-permute-start | bytes 2359304 | tf_op jit(solution)/shard_map/ppermute | solution.py:24
  190.6 31.5 %collective-permute-start.34 = (bf16[1024,640]{1,0:T(8,128)(2,1)}, bf16[1024,640]{1,0:T(8,128)(2,1)}, u32[]{:S(2)}, u32[]{:S(2)}) collective-permute-start(bf16[1024,640]{1,0:T(8,128)(2,1)} %collective-permute-done.30.refs_36_.refs_12_), channel_id=1, source_target_pairs={{0,16},{16,0},{1,17},{17,1},{2,18},{18,2},{3,19},{19,3},{4,20},{20... | collective-permute-start | bytes 3932168 | tf_op jit(solution)/shard_map/ppermute | solution.py:24
  191.5 29.1 %collective-permute-start.12 = (bf16[3,16,8192]{2,1,0:T(8,128)(2,1)}, bf16[3,16,8192]{2,1,0:T(8,128)(2,1)}, u32[]{:S(2)}, u32[]{:S(2)}) collective-permute-start(bf16[3,16,8192]{2,1,0:T(8,128)(2,1)} %collective-permute-done.9.refs_12_), channel_id=1, source_target_pairs={{0,12},{4,0},{8,4},{12,8},{1,13},{5,1},{9,5},{13,9},{2,14},{6,2},{... | collective-permute-start | bytes 2359304 | tf_op jit(solution)/shard_map/ppermute | solution.py:24
  211.4 13.6 %collective-permute-start.25 = (bf16[1024,640]{1,0:T(8,128)(2,1)}, bf16[1024,640]{1,0:T(8,128)(2,1)S(1)}, u32[]{:S(2)}, u32[]{:S(2)}) collective-permute-start(bf16[1024,640]{1,0:T(8,128)(2,1)} %collective-permute-done.1.refs_26_), channel_id=1, source_target_pairs={{0,16},{16,0},{1,17},{17,1},{2,18},{18,2},{3,19},{19,3},{4,20},{20... | collective-permute-start | bytes 3932168 | tf_op jit(solution)/shard_map/ppermute | solution.py:24
  212.9 31.8 %collective-permute-start.23 = (bf16[1024,640]{1,0:T(8,128)(2,1)}, bf16[1024,640]{1,0:T(8,128)(2,1)}, u32[]{:S(2)}, u32[]{:S(2)}) collective-permute-start(bf16[1024,640]{1,0:T(8,128)(2,1)} %collective-permute-done.1.refs_26_), channel_id=1, source_target_pairs={{0,32},{32,64},{64,96},{96,0},{1,33},{33,65},{65,97},{97,1},{2,34}... | collective-permute-start | bytes 3932168 | tf_op jit(solution)/shard_map/ppermute | solution.py:24
  213.1 11.8 %collective-permute-start.19 = (bf16[1024,640]{1,0:T(8,128)(2,1)}, bf16[1024,640]{1,0:T(8,128)(2,1)S(1)}, u32[]{:S(2)}, u32[]{:S(2)}) collective-permute-start(bf16[1024,640]{1,0:T(8,128)(2,1)} %collective-permute-done.15.refs_20_.refs_4_), channel_id=1, source_target_pairs={{0,16},{16,0},{1,17},{17,1},{2,18},{18,2},{3,19},{19,3},{4,20},{20... | collective-permute-start | bytes 3932168 | tf_op jit(solution)/shard_map/ppermute | solution.py:24
  220.5 29.5 %collective-permute-start.24 = (bf16[1024,640]{1,0:T(8,128)(2,1)}, bf16[1024,640]{1,0:T(8,128)(2,1)}, u32[]{:S(2)}, u32[]{:S(2)}) collective-permute-start(bf16[1024,640]{1,0:T(8,128)(2,1)} %collective-permute-done.22.refs_27_), channel_id=1, source_target_pairs={{0,96},{32,0},{64,32},{96,64},{1,97},{33,1},{65,33},{97,65},{2,98}... | collective-permute-start | bytes 3932168 | tf_op jit(solution)/shard_map/ppermute | solution.py:24
  222.1 29.9 %collective-permute-start.35 = (bf16[1024,640]{1,0:T(8,128)(2,1)}, bf16[1024,640]{1,0:T(8,128)(2,1)S(1)}, u32[]{:S(2)}, u32[]{:S(2)}) collective-permute-start(bf16[1024,640]{1,0:T(8,128)(2,1)} %collective-permute-done.31.refs_37_.refs_13_), channel_id=1, source_target_pairs={{0,16},{16,0},{1,17},{17,1},{2,18},{18,2},{3,19},{19,3},{4,20},{20... | collective-permute-start | bytes 3932168 | tf_op jit(solution)/shard_map/ppermute | solution.py:24
  224.9 30.2 %collective-permute-start.26 = (bf16[1024,640]{1,0:T(8,128)(2,1)}, bf16[1024,640]{1,0:T(8,128)(2,1)S(1)}, u32[]{:S(2)}, u32[]{:S(2)}) collective-permute-start(bf16[1024,640]{1,0:T(8,128)(2,1)} %collective-permute-done.22.refs_27_), channel_id=1, source_target_pairs={{0,16},{16,0},{1,17},{17,1},{2,18},{18,2},{3,19},{19,3},{4,20},{20... | collective-permute-start | bytes 3932168 | tf_op jit(solution)/shard_map/ppermute | solution.py:24
  225.0 30.1 %collective-permute-start.20 = (bf16[1024,640]{1,0:T(8,128)(2,1)}, bf16[1024,640]{1,0:T(8,128)(2,1)S(1)}, u32[]{:S(2)}, u32[]{:S(2)}) collective-permute-start(bf16[1024,640]{1,0:T(8,128)(2,1)} %collective-permute-done.16.refs_21_.refs_5_), channel_id=1, source_target_pairs={{0,16},{16,0},{1,17},{17,1},{2,18},{18,2},{3,19},{19,3},{4,20},{20... | collective-permute-start | bytes 3932168 | tf_op jit(solution)/shard_map/ppermute | solution.py:24
  244.7 33.6 %collective-permute-start.27 = (bf16[1024,640]{1,0:T(8,128)(2,1)}, bf16[1024,640]{1,0:T(8,128)(2,1)S(1)}, u32[]{:S(2)}, u32[]{:S(2)}) collective-permute-start(bf16[1024,640]{1,0:T(8,128)(2,1)} %collective-permute-done.23.refs_28_), channel_id=1, source_target_pairs={{0,16},{16,0},{1,17},{17,1},{2,18},{18,2},{3,19},{19,3},{4,20},{20... | collective-permute-start | bytes 3932168 | tf_op jit(solution)/shard_map/ppermute | solution.py:24
  250.1 28.2 %collective-permute-start.28 = (bf16[1024,640]{1,0:T(8,128)(2,1)}, bf16[1024,640]{1,0:T(8,128)(2,1)S(1)}, u32[]{:S(2)}, u32[]{:S(2)}) collective-permute-start(bf16[1024,640]{1,0:T(8,128)(2,1)} %collective-permute-done.24.refs_29_), channel_id=1, source_target_pairs={{0,16},{16,0},{1,17},{17,1},{2,18},{18,2},{3,19},{19,3},{4,20},{20... | collective-permute-start | bytes 3932168 | tf_op jit(solution)/shard_map/ppermute | solution.py:24
  252.1 26.2 %collective-permute-start.11 = (bf16[4,16,8192]{2,1,0:T(8,128)(2,1)}, bf16[4,16,8192]{2,1,0:T(8,128)(2,1)S(1)}, u32[]{:S(2)}, u32[]{:S(2)}) collective-permute-start(bf16[4,16,8192]{2,1,0:T(8,128)(2,1)} %collective-permute-done.10.refs_15_), channel_id=1, source_target_pairs={{0,4},{4,8},{8,12},{12,0},{1,5},{5,9},{9,13},{13,1},{2,6},{6,10},{... | collective-permute-start | bytes 3145736 | tf_op jit(solution)/shard_map/ppermute | solution.py:24
  303.1 28.1 %collective-permute-start.42 = (bf16[576,256]{1,0:T(8,128)(2,1)}, bf16[576,256]{1,0:T(8,128)(2,1)S(1)}, u32[]{:S(2)}, u32[]{:S(2)}) collective-permute-start(bf16[576,256]{1,0:T(8,128)(2,1)} %get-tuple-element.40), channel_id=1, source_target_pairs={{0,3},{1,0},{2,1},{3,2},{4,7},{5,4},{6,5},{7,6},{8,11},{9,8},{10,9... | collective-permute-start | bytes 884744 | tf_op jit(solution)/shard_map/ppermute | solution.py:24
  325.1 40.9 %collective-permute-start.39 = (bf16[576,512]{1,0:T(8,128)(2,1)}, bf16[576,512]{1,0:T(8,128)(2,1)S(1)}, u32[]{:S(2)}, u32[]{:S(2)}) collective-permute-start(bf16[576,512]{1,0:T(8,128)(2,1)} %get-tuple-element.36), channel_id=1, source_target_pairs={{0,3},{1,0},{2,1},{3,2},{4,7},{5,4},{6,5},{7,6},{8,11},{9,8},{10,9... | collective-permute-start | bytes 1769480 | tf_op jit(solution)/shard_map/ppermute | solution.py:24
  325.1 40.8 %collective-permute-start.41 = (bf16[576,512]{1,0:T(8,128)(2,1)}, bf16[576,512]{1,0:T(8,128)(2,1)S(1)}, u32[]{:S(2)}, u32[]{:S(2)}) collective-permute-start(bf16[576,512]{1,0:T(8,128)(2,1)} %get-tuple-element.38), channel_id=1, source_target_pairs={{0,1},{1,2},{2,3},{3,0},{4,5},{5,6},{6,7},{7,4},{8,9},{9,10},{10,1... | collective-permute-start | bytes 1769480 | tf_op jit(solution)/shard_map/ppermute | solution.py:24
  326.6 39.3 %collective-permute-start.40 = (bf16[576,512]{1,0:T(8,128)(2,1)S(1)}, bf16[576,512]{1,0:T(8,128)(2,1)S(1)}, u32[]{:S(2)}, u32[]{:S(2)}) collective-permute-start(bf16[576,512]{1,0:T(8,128)(2,1)S(1)} %get-tuple-element.37), channel_id=1, source_target_pairs={{0,2},{1,3},{2,0},{3,1},{4,6},{5,7},{6,4},{7,5},{8,10},{9,11},{10,... | collective-permute-start | bytes 1769480 | tf_op jit(solution)/shard_map/ppermute | solution.py:24
  328.2 30.1 %collective-permute-start.43 = (bf16[576,256]{1,0:T(8,128)(2,1)}, bf16[576,256]{1,0:T(8,128)(2,1)S(1)}, u32[]{:S(2)}, u32[]{:S(2)}) collective-permute-start(bf16[576,256]{1,0:T(8,128)(2,1)} %copy-done.1), channel_id=1, source_target_pairs={{0,2},{1,3},{2,0},{3,1},{4,6},{5,7},{6,4},{7,5},{8,10},{9,11},{10,... | collective-permute-start | bytes 884744 | tf_op jit(solution)/shard_map/ppermute | solution.py:24
  331.2 34.7 %collective-permute-start.44 = (bf16[576,256]{1,0:T(8,128)(2,1)}, bf16[576,256]{1,0:T(8,128)(2,1)S(1)}, u32[]{:S(2)}, u32[]{:S(2)}) collective-permute-start(bf16[576,256]{1,0:T(8,128)(2,1)} %copy-done), channel_id=1, source_target_pairs={{0,1},{1,2},{2,3},{3,0},{4,5},{5,6},{6,7},{7,4},{8,9},{9,10},{10,1... | collective-permute-start | bytes 884744 | tf_op jit(solution)/shard_map/ppermute | solution.py:24
  (24 other events, 469.3 us)

commit v5 on v4

--- a/solution.py
+++ b/solution.py
@@ -576,11 +576,16 @@
     y = lax.axis_index("y")
     gain = norm_gain.reshape(1, -1)
 
+    t_low = norm_text(text_rows, gain, 0, 64)
+    t3_low = shifted(t_low, "z", 1)
+    t1_low = shifted(t_low, "z", -1)
+
     quarter = 2 * core + x % 2
+    begin, t_low = lax.optimization_barrier((quarter * 2 * PIECE, t_low))
     own_kv = jnp.concatenate([k_weight, v_weight], axis=1)
 
     def own_part(half):
-        first = quarter * 2 * PIECE + half * PIECE
+        first = begin + half * PIECE
         return jnp.concatenate(
             [
                 lax.dynamic_slice_in_dim(weight, first, PIECE, 0)
@@ -597,33 +602,36 @@
     direct[3, 0] = shifted(low, "y", 1)
 
     low, high, text_rows = lax.optimization_barrier((low, high, text_rows))
-    t_low = norm_text(text_rows, gain, 0, 64)
-    t3_low = shifted(t_low, "z", 1)
-    t1_low = shifted(t_low, "z", -1)
+    t_high = norm_text(text_rows, gain, 64, 64)
+    t3_high = shifted(t_high, "z", 1)
+    t1_high = shifted(t_high, "z", -1)
 
     row_groups = lax.dynamic_slice_in_dim(tile_group, group * 4, 4)
     matches = row_groups[None, :] == jnp.arange(8, dtype=jnp.int32)[:, None]
     chosen = jnp.sum(jnp.where(matches, jnp.arange(4, dtype=jnp.int32)[None, :], 0), axis=1)
-    image_rows, t_low = lax.optimization_barrier((image_rows, t_low))
+    image_rows, t_high = lax.optimization_barrier((image_rows, t_high))
     outgoing = spread(image_rows, chosen.astype(jnp.int32))
     arrived = lax.all_to_all(outgoing, ("x", "c"), split_axis=0, concat_axis=0, tiled=True)
 
-    outgoing, text_rows = lax.optimization_barrier((outgoing, text_rows))
-    t_high = norm_text(text_rows, gain, 64, 64)
-    t3_high = shifted(t_high, "z", 1)
-    t1_high = shifted(t_high, "z", -1)
     t2_low = shifted(t3_low, "z", 1)
     t2_high = shifted(t1_high, "z", -1)
 
     direct[2, 0] = shifted(direct[1, 0], "y", -1)
     direct[2, 1] = shifted(direct[3, 1], "y", 1)
-    across = {key: shifted(value, "x", -1 if key[1] else 1) for key, value in direct.items()}
+    across = {
+        key: shifted(value, "x", -1 if key[1] else 1)
+        for key, value in direct.items()
+        if key[0] != 2
+    }
+    across[2, 0] = shifted(across[1, 0], "y", -1)
+    across[2, 1] = shifted(across[3, 1], "y", 1)
     pieces = {
         delta: [direct[delta, 0], direct[delta, 1], across[delta, 0], across[delta, 1]]
         for delta in (1, 2, 3)
     }
     pieces = {
-        delta: found + [shifted(value, "c", 1) for value in found]
+        delta: found
+        + [shifted(value, "c", 1) for value in found]
         for delta, found in pieces.items()
     }
     quarters = jnp.stack([quarter ^ 0, quarter ^ 1, quarter ^ 2, quarter ^ 3]) * 2 * PIECE
@@ -642,7 +650,7 @@
     i2_high = shifted(i1_high, "z", -1)
 
     bias = jnp.concatenate([q_bias, k_bias, v_bias])
-    bias, i_high = lax.optimization_barrier((bias, i_high))
+    bias, t_high = lax.optimization_barrier((bias, t_high))
     biases = [
         bias, shifted(bias, "y", -1), shifted(bias, "y", 2),
         shifted(bias, "y", 1),
@@ -654,6 +662,7 @@
     cosine = jnp.concatenate([jnp.cos(angles), jnp.cos(angles)], axis=-1)
     sine = jnp.concatenate([-jnp.sin(angles), jnp.sin(angles)], axis=-1)
 
+    place, text_index, info = lax.optimization_barrier((place, text_index, info))
     texts = (t_low, t_high, t1_low, t1_high, t2_low, t2_high, t3_low, t3_high)
     images = (i_low, i_high, i1_low, i1_high, i2_low, i2_high, i3_low, i3_high)
     *pairs, far_query, compact = project_kv(

time: 383 us -> 398 us (1.039)
  waiting for transfers between devices: 194 us -> 206 us
  starting transfers between devices: 73.5 us -> 80.4 us
    all_to_all x1, waiting for transfers between devices: 0.01 us -> 15.7 us  [one_device(): lax.all_to_all(outgoing, ('x', 'c'), split_axis=0, concat_axis=0, tiled=T...]
    ppermute x45, starting transfers between devices: 66.8 us -> 75.8 us  [shifted(): lax.ppermute(block, axis, [(low, (low + step) % count) for low in range(c...]
  transfers between devices with their start and end apart: 46 -> 46, of which waited for: 16 -> 17; matrix products, arithmetic and copies ran while one was open for 4% -> 6% of each run, Pallas kernels for 11% -> 11%
where the time goes in v5:
time: 398 us; the launch traced here: 397 us
  waiting for transfers between devices  206 us (52%)
  Pallas kernels  82.9 us (21%)
  starting transfers between devices  80.4 us (20%)
  other arithmetic  14.2 us (4%)
  local copies, waits for them, and re-layouts  9.9 us (2%)
  between operations  4.13 us (1%)
    ppermute x45, waiting for transfers between devices, shifted(): lax.ppermute(block, axis, [(low, (low + step) % count) for low in range(c...  190 us
    ppermute x45, starting transfers between devices, shifted(): lax.ppermute(block, axis, [(low, (low + step) % count) for low in range(c...  75.8 us
    pallas_call x2, Pallas kernels, project_q(): pl.pallas_call(kernel, grid_spec=pltpu.PrefetchScalarGridSpec(num_scalar_...  28.8 us
    pallas_call x1, Pallas kernels, project_kv(): pl.pallas_call(project_kv_kernel, grid_spec=pltpu.PrefetchScalarGridSpec(...  20.9 us
    pallas_call x1, Pallas kernels, attend(): pl.pallas_call(attend_kernel, grid_spec=pltpu.PrefetchScalarGridSpec(num_...  16.6 us
    all_to_all x1, waiting for transfers between devices, one_device(): lax.all_to_all(outgoing, ('x', 'c'), split_axis=0, concat_axis=0, tiled=T...  15.7 us
    pallas_call x2, Pallas kernels, norm_image(): pl.pallas_call(norm_image_kernel, grid_spec=pltpu.PrefetchScalarGridSpec(...  8.12 us
  transfers between devices with their start and end apart: 46, of which 17 were waited for; matrix products, arithmetic and copies ran while one was open for 6% of the time, Pallas kernels for 11%

profile of v5, /device:TPU:1, one launch (start us, length us, event | category | flops | bytes accessed | tf_op | source)
XLA Modules:
  0.0 397.4 jit_solution(11310177070985317238)
XLA Ops:
  0.0 2.6 shard_map.127.refs_1_
  2.6 2.5 collective-permute-start.4
  5.1 2.1 collective-permute-start.2
  8.3 2.7 copy.19
  12.5 2.0 constant_dynamic-slice_fusion
  15.8 2.6 shard_map.128.refs_2_
  21.1 28.4 %collective-permute-done.38 = f32[640]{0:T(1024)S(1)} collective-permute-done((f32[640]{0:T(1024)S(1)}, f32[640]{0:T(1024)S(1)}, u32[]{:S(2)}, u32[]{:S(2)}) %collective-permute-start.38) | collective-permute-done | bytes 2592 | tf_op jit(solution)/shard_map/ppermute | solution.py:24
  51.1 2.4 collective-permute-done.37
  55.9 2.7 collective-permute-start.3
  58.6 2.3 collective-permute-start
  61.0 2.7 collective-permute-start.14
  63.6 13.8 %collective-permute-done.3.refs_4_ = bf16[64,8192]{1,0:T(8,128)(2,1)} collective-permute-done((bf16[64,8192]{1,0:T(8,128)(2,1)}, bf16[64,8192]{1,0:T(8,128)(2,1)}, u32[]{:S(2)}, u32[]{:S(2)}) %collective-permute-start.3) | collective-permute-done | bytes 1048608 | tf_op jit(solution)/shard_map/ppermute | solution.py:24
  77.4 3.4 collective-permute-start.6
  80.8 4.1 %collective-permute-done.refs_18_.refs_2_ = bf16[1024,640]{1,0:T(8,128)(2,1)} collective-permute-done((bf16[1024,640]{1,0:T(8,128)(2,1)}, bf16[1024,640]{1,0:T(8,128)(2,1)}, u32[]{:S(2)}, u32[]{:S(2)}) %collective-permute-start) | collective-permute-done | bytes 1310752 | tf_op jit(solution)/shard_map/ppermute | solution.py:24
  84.9 10.4 %collective-permute-start.32 = (bf16[1024,640]{1,0:T(8,128)(2,1)}, bf16[1024,640]{1,0:T(8,128)(2,1)}, u32[]{:S(2)}, u32[]{:S(2)}) collective-permute-start(bf16[1024,640]{1,0:T(8,128)(2,1)} %collective-permute-done.30.refs_34_.refs_10_), channel_id=1, source_target_pairs={{0,16},{16,0},{1,17},{17,1},{2,18},{18,2},{3,19},{19,3},{4,20},{20... | collective-permute-start | bytes 3932168 | tf_op jit(solution)/shard_map/ppermute | solution.py:24
  96.6 16.5 %collective-permute-done.14.refs_19_.refs_3_ = bf16[1024,640]{1,0:T(8,128)(2,1)} collective-permute-done((bf16[1024,640]{1,0:T(8,128)(2,1)S(1)}, bf16[1024,640]{1,0:T(8,128)(2,1)}, u32[]{:S(2)}, u32[]{:S(2)}) %collective-permute-start.14) | collective-permute-done | bytes 1310752 | tf_op jit(solution)/shard_map/ppermute | solution.py:24
  113.0 5.2 %collective-permute-start.17 = (bf16[1024,640]{1,0:T(8,128)(2,1)}, bf16[1024,640]{1,0:T(8,128)(2,1)S(1)}, u32[]{:S(2)}, u32[]{:S(2)}) collective-permute-start(bf16[1024,640]{1,0:T(8,128)(2,1)} %collective-permute-done.refs_18_.refs_2_), channel_id=1, source_target_pairs={{0,16},{16,0},{1,17},{17,1},{2,18},{18,2},{3,19},{19,3},{4,20},{20... | collective-permute-start | bytes 3932168 | tf_op jit(solution)/shard_map/ppermute | solution.py:24
  120.2 3.3 spread.1
  123.5 4.6 %all-to-all-start = ((bf16[8,16,8192]{2,1,0:T(8,128)(2,1)}), bf16[8,16,8192]{2,1,0:T(8,128)(2,1)}, u32[]{:S(2)}, u32[]{:S(2)}) async-start(bf16[8,16,8192]{2,1,0:T(8,128)(2,1)} %spread.1), calls=%async_computation | async-start | bytes 4194304 | tf_op jit(solution)/shard_map/all_to_all | solution.py:614
  128.1 3.5 collective-permute-start.1
  135.6 2.9 collective-permute-start.24
  138.5 16.8 %collective-permute-done.15.refs_20_.refs_4_ = bf16[1024,640]{1,0:T(8,128)(2,1)} collective-permute-done((bf16[1024,640]{1,0:T(8,128)(2,1)}, bf16[1024,640]{1,0:T(8,128)(2,1)}, u32[]{:S(2)}, u32[]{:S(2)}) %collective-permute-start.15) | collective-permute-done | bytes 1310752 | tf_op jit(solution)/shard_map/ppermute | solution.py:24
  157.4 2.4 collective-permute-done.1.refs_26_
  159.8 2.4 collective-permute-start.16
  163.1 15.7 %all-to-all-done.rows_ref = bf16[8,16,8192]{2,1,0:T(8,128)(2,1)} async-done(((bf16[8,16,8192]{2,1,0:T(8,128)(2,1)}), bf16[8,16,8192]{2,1,0:T(8,128)(2,1)}, u32[]{:S(2)}, u32[]{:S(2)}) %all-to-all-start) | async-done | bytes 2097184 | tf_op jit(solution)/shard_map/all_to_all | solution.py:614
  178.7 3.5 norm_image.3.refs_10_
  182.9 4.6 %norm_image.2.refs_9_ = bf16[4,16,8192]{2,1,0:T(8,128)(2,1)} custom-call(s32[4]{0:T(128)} %bitcast.37, bf16[8,16,8192]{2,1,0:T(8,128)(2,1)} %all-to-all-done.rows_ref, f32[1,8192]{1,0:T(1,128)} %bitcast.35), custom_call_target="tpu_custom_call" | custom-call | tf_op jit(solution)/shard_map/norm_image/pallas_call | solution.py:59
  190.2 1.7 collective-permute-start.34
  192.0 17.2 %collective-permute-done.16.refs_21_.refs_5_ = bf16[1024,640]{1,0:T(8,128)(2,1)} collective-permute-done((bf16[1024,640]{1,0:T(8,128)(2,1)}, bf16[1024,640]{1,0:T(8,128)(2,1)}, u32[]{:S(2)}, u32[]{:S(2)}) %collective-permute-start.16) | collective-permute-done | bytes 1310752 | tf_op jit(solution)/shard_map/ppermute | solution.py:24
  209.1 2.7 collective-permute-start.12
  212.7 17.3 %collective-permute-done.13.refs_16_ = bf16[3,16,8192]{2,1,0:T(8,128)(2,1)} collective-permute-done((bf16[3,16,8192]{2,1,0:T(8,128)(2,1)S(1)}, bf16[3,16,8192]{2,1,0:T(8,128)(2,1)}, u32[]{:S(2)}, u32[]{:S(2)}) %collective-permute-start.13) | collective-permute-done | bytes 786464 | tf_op jit(solution)/shard_map/ppermute | solution.py:24
  230.0 3.5 collective-permute-start.23
  233.5 1.7 collective-permute-start.19
  235.3 5.1 %collective-permute-done.12.refs_14_ = bf16[3,16,8192]{2,1,0:T(8,128)(2,1)} collective-permute-done((bf16[3,16,8192]{2,1,0:T(8,128)(2,1)}, bf16[3,16,8192]{2,1,0:T(8,128)(2,1)}, u32[]{:S(2)}, u32[]{:S(2)}) %collective-permute-start.12) | collective-permute-done | bytes 786464 | tf_op jit(solution)/shard_map/ppermute | solution.py:24
  244.8 1.8 collective-permute-start.35
  246.6 4.1 %pad_maximum_fusion.refs_17_ = bf16[8192,128]{1,0:T(8,128)(2,1)} fusion(bf16[8192,64]{1,0:T(8,128)(2,1)} %copy.19, bf16[8192,64]{1,0:T(8,128)(2,1)S(1)} %copy.18), kind=kLoop, calls=%fused_computation.3 | loop fusion | flops 4194304 | bytes 4194304 | tf_op jit(solution)/shard_map/concatenate | solution.py:585
  250.7 9.9 %collective-permute-done.23.refs_28_ = bf16[1024,640]{1,0:T(8,128)(2,1)} collective-permute-done((bf16[1024,640]{1,0:T(8,128)(2,1)}, bf16[1024,640]{1,0:T(8,128)(2,1)}, u32[]{:S(2)}, u32[]{:S(2)}) %collective-permute-start.23) | collective-permute-done | bytes 1310752 | tf_op jit(solution)/shard_map/ppermute | solution.py:24
  260.6 2.3 collective-permute-start.27
  263.3 8.2 %collective-permute-done.25.refs_29_ = bf16[1024,640]{1,0:T(8,128)(2,1)} collective-permute-done((bf16[1024,640]{1,0:T(8,128)(2,1)}, bf16[1024,640]{1,0:T(8,128)(2,1)}, u32[]{:S(2)}, u32[]{:S(2)}) %collective-permute-start.25) | collective-permute-done | bytes 1310752 | tf_op jit(solution)/shard_map/ppermute | solution.py:24
  271.5 2.3 collective-permute-start.29
  277.9 22.2 %collective-permute-done.11.refs_13_ = bf16[4,16,8192]{2,1,0:T(8,128)(2,1)} collective-permute-done((bf16[4,16,8192]{2,1,0:T(8,128)(2,1)}, bf16[4,16,8192]{2,1,0:T(8,128)(2,1)}, u32[]{:S(2)}, u32[]{:S(2)}) %collective-permute-start.11) | collective-permute-done | bytes 1048608 | tf_op jit(solution)/shard_map/ppermute | solution.py:24
  300.2 20.9 %project_kv.1 = (bf16[576,256]{1,0:T(8,128)(2,1)S(1)}, bf16[576,256]{1,0:T(8,128)(2,1)S(1)}, bf16[576,256]{1,0:T(8,128)(2,1)S(1)}, bf16[576,256]{1,0:T(8,128)(2,...) custom-call(s32[70]{0:T(128)S(1)} %concatenate.27.refs_0_, bf16[64,8192]{1,0:T(8,128)(2,1)} %shard_map.127.refs_1_, ...), custom_call_target="tpu_custom_call" | custom-call | flops 9663676416 | bytes 26214400 | tf_op jit(solution)/shard_map/project_kv/pallas_call | solution.py:289
  322.8 17.3 %project_q.2 = (bf16[576,512]{1,0:T(8,128)(2,1)S(1)}, bf16[576,512]{1,0:T(8,128)(2,1)S(1)}) custom-call(s32[70]{0:T(128)S(1)} %concatenate.27.refs_0_, bf16[576,8192]{1,0:T(8,128)(2,1)} %get-tuple-element.42.refs_1_, bf16[1024,640]{1,0:T(8,128)(2,1)} %collective-permute-done.refs_18_.refs_2_, bf16[1024,640]{1,0:T(8,128)(2,1)} %collective-permute-done.14.refs_19_.refs_3_, ...), custom_call_target="tpu_custom_call" | custom-call | flops 9663676416 | bytes 26214400 | tf_op jit(solution)/shard_map/project_q/pallas_call | solution.py:358
  341.9 2.8 collective-permute-start.43
  344.7 11.5 %project_q.3.q0 = bf16[576,512]{1,0:T(8,128)(2,1)S(1)} custom-call(s32[70]{0:T(128)S(1)} %concatenate.27.refs_0_, bf16[576,8192]{1,0:T(8,128)(2,1)} %get-tuple-element.42.refs_1_, bf16[8192,512]{1,0:T(8,128)(2,1)} %refs_2_.1, f32[1,512]{1,0:T(1,128)S(1)} %bitcast.28, f32[576,128]{1,0:T(8,128)S(1)} %pad_maximum_fusion.3.refs_44_.refs_20_.refs_4_, ...), custom_call_target="tpu_custom_call" | custom-call | flops 4831838208 | bytes 17825792 | tf_op jit(solution)/shard_map/project_q/pallas_call | solution.py:358
  356.1 17.1 %collective-permute-done.43.kv2 = bf16[576,256]{1,0:T(8,128)(2,1)S(1)} collective-permute-done((bf16[576,256]{1,0:T(8,128)(2,1)S(1)}, bf16[576,256]{1,0:T(8,128)(2,1)S(1)}, u32[]{:S(2)}, u32[]{:S(2)}) %collective-permute-start.43) | collective-permute-done | bytes 294944 | tf_op jit(solution)/shard_map/ppermute | solution.py:24
  373.3 7.5 %collective-permute-done.44.kv3 = bf16[576,256]{1,0:T(8,128)(2,1)S(1)} collective-permute-done((bf16[576,256]{1,0:T(8,128)(2,1)S(1)}, bf16[576,256]{1,0:T(8,128)(2,1)S(1)}, u32[]{:S(2)}, u32[]{:S(2)}) %collective-permute-start.44) | collective-permute-done | bytes 294944 | tf_op jit(solution)/shard_map/ppermute | solution.py:24
  380.8 16.6 %attend.1 = bf16[2048,512]{1,0:T(8,128)(2,1)} custom-call(s32[12]{0:T(128)S(1)} %concatenate.30.info_ref, s32[128]{0:T(128)S(1)} %reshape.320.text_ref, bf16[576,512]{1,0:T(8,128)(2,1)S(1)} %project_q.3.q0, bf16[576,512]{1,0:T(8,128)(2,1)S(1)} %collective-permute-done.39.q1, bf16[576,512]{1,0:T(8,128)(2,1)S(1)} %collective-permute-done.40.q2, ...), custom_call_target="tpu_custom_call" | custom-call | tf_op jit(solution)/shard_map/attend/pallas_call | solution.py:502
  (139 shorter events, 33.5 us)
Async XLA Ops:
  2.6 56.0 %collective-permute-start.4 = (bf16[64,8192]{1,0:T(8,128)(2,1)}, bf16[64,8192]{1,0:T(8,128)(2,1)}, u32[]{:S(2)}, u32[]{:S(2)}) collective-permute-start(bf16[64,8192]{1,0:T(8,128)(2,1)} %shard_map.127.refs_1_), channel_id=1, source_target_pairs={{0,4},{4,8},{8,12},{12,0},{1,5},{5,9},{9,13},{13,1},{2,6},{6,10},{... | collective-permute-start | bytes 3145736 | tf_op jit(solution)/shard_map/ppermute | solution.py:24
  5.1 55.9 %collective-permute-start.2 = (bf16[64,8192]{1,0:T(8,128)(2,1)}, bf16[64,8192]{1,0:T(8,128)(2,1)}, u32[]{:S(2)}, u32[]{:S(2)}) collective-permute-start(bf16[64,8192]{1,0:T(8,128)(2,1)} %shard_map.127.refs_1_), channel_id=1, source_target_pairs={{0,12},{4,0},{8,4},{12,8},{1,13},{5,1},{9,5},{13,9},{2,14},{6,2},{... | collective-permute-start | bytes 3145736 | tf_op jit(solution)/shard_map/ppermute | solution.py:24
  15.8 103.6 %copy-start.12 = (s32[32]{0:T(128)S(1)}, s32[32]{0:T(128)}, u32[]{:S(2)}) copy-start(s32[32]{0:T(128)} %param.15) | copy-start | bytes 388
  18.4 42.6 %collective-permute-start.7 = (bf16[64,8192]{1,0:T(8,128)(2,1)}, bf16[64,8192]{1,0:T(8,128)(2,1)S(1)}, u32[]{:S(2)}, u32[]{:S(2)}) collective-permute-start(bf16[64,8192]{1,0:T(8,128)(2,1)} %shard_map.128.refs_2_), channel_id=1, source_target_pairs={{0,4},{4,8},{8,12},{12,0},{1,5},{5,9},{9,13},{13,1},{2,6},{6,10},{... | collective-permute-start | bytes 3145736 | tf_op jit(solution)/shard_map/ppermute | solution.py:24
  18.4 59.0 %collective-permute-start.30 = (bf16[1024,640]{1,0:T(8,128)(2,1)}, bf16[1024,640]{1,0:T(8,128)(2,1)}, u32[]{:S(2)}, u32[]{:S(2)}) collective-permute-start(bf16[1024,640]{1,0:T(8,128)(2,1)} %pad_maximum_fusion.1), channel_id=1, source_target_pairs={{0,1},{1,2},{2,3},{3,0},{4,5},{5,6},{6,7},{7,4},{8,9},{9,10},{10,1... | collective-permute-start | bytes 3932168 | tf_op jit(solution)/shard_map/ppermute | solution.py:24
  19.8 29.7 %collective-permute-start.38 = (f32[640]{0:T(1024)S(1)}, f32[640]{0:T(1024)S(1)}, u32[]{:S(2)}, u32[]{:S(2)}) collective-permute-start(f32[640]{0:T(1024)S(1)} %pad_maximum_fusion.5), channel_id=1, source_target_pairs={{0,1},{1,2},{2,3},{3,0},{4,5},{5,6},{6,7},{7,4},{8,9},{9,10},{10,1... | collective-permute-start | bytes 7688 | tf_op jit(solution)/shard_map/ppermute | solution.py:24
  49.5 4.0 collective-permute-start.37
  53.5 2.5 collective-permute-start.36
  55.9 21.5 %collective-permute-start.3 = (bf16[64,8192]{1,0:T(8,128)(2,1)}, bf16[64,8192]{1,0:T(8,128)(2,1)}, u32[]{:S(2)}, u32[]{:S(2)}) collective-permute-start(bf16[64,8192]{1,0:T(8,128)(2,1)} %shard_map.128.refs_2_), channel_id=1, source_target_pairs={{0,12},{4,0},{8,4},{12,8},{1,13},{5,1},{9,5},{13,9},{2,14},{6,2},{... | collective-permute-start | bytes 3145736 | tf_op jit(solution)/shard_map/ppermute | solution.py:24
  58.6 26.3 %collective-permute-start = (bf16[1024,640]{1,0:T(8,128)(2,1)}, bf16[1024,640]{1,0:T(8,128)(2,1)}, u32[]{:S(2)}, u32[]{:S(2)}) collective-permute-start(bf16[1024,640]{1,0:T(8,128)(2,1)} %pad_maximum_fusion.1), channel_id=1, source_target_pairs={{0,3},{1,0},{2,1},{3,2},{4,7},{5,4},{6,5},{7,6},{8,11},{9,8},{10,9... | collective-permute-start | bytes 3932168 | tf_op jit(solution)/shard_map/ppermute | solution.py:24
  60.9 34.4 %collective-permute-start.21 = (bf16[1024,640]{1,0:T(8,128)(2,1)S(1)}, bf16[1024,640]{1,0:T(8,128)(2,1)}, u32[]{:S(2)}, u32[]{:S(2)}) collective-permute-start(bf16[1024,640]{1,0:T(8,128)(2,1)S(1)} %pad_maximum_fusion.2), channel_id=1, source_target_pairs={{0,1},{1,2},{2,3},{3,0},{4,5},{5,6},{6,7},{7,4},{8,9},{9,10},{10,1... | collective-permute-start | bytes 3932168 | tf_op jit(solution)/shard_map/ppermute | solution.py:24
  61.0 52.1 %copy-start.5 = (bf16[64,8192]{1,0:T(8,128)(2,1)}, bf16[64,8192]{1,0:T(8,128)(2,1)S(1)}, u32[]{:S(2)}) copy-start(bf16[64,8192]{1,0:T(8,128)(2,1)S(1)} %collective-permute-done.7.refs_8_) | copy-start | bytes 3145732
  61.0 52.1 %collective-permute-start.14 = (bf16[1024,640]{1,0:T(8,128)(2,1)S(1)}, bf16[1024,640]{1,0:T(8,128)(2,1)}, u32[]{:S(2)}, u32[]{:S(2)}) collective-permute-start(bf16[1024,640]{1,0:T(8,128)(2,1)S(1)} %pad_maximum_fusion.2), channel_id=1, source_target_pairs={{0,3},{1,0},{2,1},{3,2},{4,7},{5,4},{6,5},{7,6},{8,11},{9,8},{10,9... | collective-permute-start | bytes 3932168 | tf_op jit(solution)/shard_map/ppermute | solution.py:24
  77.4 40.8 %collective-permute-start.5 = (bf16[64,8192]{1,0:T(8,128)(2,1)}, bf16[64,8192]{1,0:T(8,128)(2,1)}, u32[]{:S(2)}, u32[]{:S(2)}) collective-permute-start(bf16[64,8192]{1,0:T(8,128)(2,1)} %collective-permute-done.4.refs_7_), channel_id=1, source_target_pairs={{0,4},{4,8},{8,12},{12,0},{1,5},{5,9},{9,13},{13,1},{2,6},{6,10},{... | collective-permute-start | bytes 3145736 | tf_op jit(solution)/shard_map/ppermute | solution.py:24
  77.4 50.7 %collective-permute-start.6 = (bf16[64,8192]{1,0:T(8,128)(2,1)}, bf16[64,8192]{1,0:T(8,128)(2,1)}, u32[]{:S(2)}, u32[]{:S(2)}) collective-permute-start(bf16[64,8192]{1,0:T(8,128)(2,1)} %collective-permute-done.3.refs_4_), channel_id=1, source_target_pairs={{0,12},{4,0},{8,4},{12,8},{1,13},{5,1},{9,5},{13,9},{2,14},{6,2},{... | collective-permute-start | bytes 3145736 | tf_op jit(solution)/shard_map/ppermute | solution.py:24
  84.9 46.6 %collective-permute-start.32 = (bf16[1024,640]{1,0:T(8,128)(2,1)}, bf16[1024,640]{1,0:T(8,128)(2,1)}, u32[]{:S(2)}, u32[]{:S(2)}) collective-permute-start(bf16[1024,640]{1,0:T(8,128)(2,1)} %collective-permute-done.30.refs_34_.refs_10_), channel_id=1, source_target_pairs={{0,16},{16,0},{1,17},{17,1},{2,18},{18,2},{3,19},{19,3},{4,20},{20... | collective-permute-start | bytes 3932168 | tf_op jit(solution)/shard_map/ppermute | solution.py:24
  95.3 40.2 %collective-permute-start.31 = (bf16[1024,640]{1,0:T(8,128)(2,1)}, bf16[1024,640]{1,0:T(8,128)(2,1)}, u32[]{:S(2)}, u32[]{:S(2)}) collective-permute-start(bf16[1024,640]{1,0:T(8,128)(2,1)} %collective-permute-done.30.refs_34_.refs_10_), channel_id=1, source_target_pairs={{0,32},{32,64},{64,96},{96,0},{1,33},{33,65},{65,97},{97,1},{2,34}... | collective-permute-start | bytes 3932168 | tf_op jit(solution)/shard_map/ppermute | solution.py:24
  113.0 25.4 %collective-permute-start.17 = (bf16[1024,640]{1,0:T(8,128)(2,1)}, bf16[1024,640]{1,0:T(8,128)(2,1)S(1)}, u32[]{:S(2)}, u32[]{:S(2)}) collective-permute-start(bf16[1024,640]{1,0:T(8,128)(2,1)} %collective-permute-done.refs_18_.refs_2_), channel_id=1, source_target_pairs={{0,16},{16,0},{1,17},{17,1},{2,18},{18,2},{3,19},{19,3},{4,20},{20... | collective-permute-start | bytes 3932168 | tf_op jit(solution)/shard_map/ppermute | solution.py:24
  118.2 37.0 %collective-permute-start.15 = (bf16[1024,640]{1,0:T(8,128)(2,1)}, bf16[1024,640]{1,0:T(8,128)(2,1)}, u32[]{:S(2)}, u32[]{:S(2)}) collective-permute-start(bf16[1024,640]{1,0:T(8,128)(2,1)} %collective-permute-done.refs_18_.refs_2_), channel_id=1, source_target_pairs={{0,32},{32,64},{64,96},{96,0},{1,33},{33,65},{65,97},{97,1},{2,34}... | collective-permute-start | bytes 3932168 | tf_op jit(solution)/shard_map/ppermute | solution.py:24
  123.5 55.3 %all-to-all-start = ((bf16[8,16,8192]{2,1,0:T(8,128)(2,1)}), bf16[8,16,8192]{2,1,0:T(8,128)(2,1)}, u32[]{:S(2)}, u32[]{:S(2)}) async-start(bf16[8,16,8192]{2,1,0:T(8,128)(2,1)} %spread.1), calls=%async_computation | async-start | bytes 4194304 | tf_op jit(solution)/shard_map/all_to_all | solution.py:614
  128.1 31.8 %collective-permute-start.1 = (bf16[1024,640]{1,0:T(8,128)(2,1)}, bf16[1024,640]{1,0:T(8,128)(2,1)}, u32[]{:S(2)}, u32[]{:S(2)}) collective-permute-start(bf16[1024,640]{1,0:T(8,128)(2,1)} %collective-permute-done.refs_18_.refs_2_), channel_id=1, source_target_pairs={{0,3},{1,0},{2,1},{3,2},{4,7},{5,4},{6,5},{7,6},{8,11},{9,8},{10,9... | collective-permute-start | bytes 3932168 | tf_op jit(solution)/shard_map/ppermute | solution.py:24
  131.6 50.7 %collective-permute-start.33 = (bf16[1024,640]{1,0:T(8,128)(2,1)}, bf16[1024,640]{1,0:T(8,128)(2,1)}, u32[]{:S(2)}, u32[]{:S(2)}) collective-permute-start(bf16[1024,640]{1,0:T(8,128)(2,1)} %collective-permute-done.21.refs_35_.refs_11_), channel_id=1, source_target_pairs={{0,16},{16,0},{1,17},{17,1},{2,18},{18,2},{3,19},{19,3},{4,20},{20... | collective-permute-start | bytes 3932168 | tf_op jit(solution)/shard_map/ppermute | solution.py:24
  135.6 51.9 %collective-permute-start.24 = (bf16[1024,640]{1,0:T(8,128)(2,1)}, bf16[1024,640]{1,0:T(8,128)(2,1)}, u32[]{:S(2)}, u32[]{:S(2)}) collective-permute-start(bf16[1024,640]{1,0:T(8,128)(2,1)} %collective-permute-done.21.refs_35_.refs_11_), channel_id=1, source_target_pairs={{0,96},{32,0},{64,32},{96,64},{1,97},{33,1},{65,33},{97,65},{2,98}... | collective-permute-start | bytes 3932168 | tf_op jit(solution)/shard_map/ppermute | solution.py:24
  138.4 50.3 %collective-permute-start.22 = (bf16[1024,640]{1,0:T(8,128)(2,1)}, bf16[1024,640]{1,0:T(8,128)(2,1)}, u32[]{:S(2)}, u32[]{:S(2)}) collective-permute-start(bf16[1024,640]{1,0:T(8,128)(2,1)} %collective-permute-done.21.refs_35_.refs_11_), channel_id=1, source_target_pairs={{0,1},{1,2},{2,3},{3,0},{4,5},{5,6},{6,7},{7,4},{8,9},{9,10},{10,1... | collective-permute-start | bytes 3932168 | tf_op jit(solution)/shard_map/ppermute | solution.py:24
  155.3 34.9 %collective-permute-start.18 = (bf16[1024,640]{1,0:T(8,128)(2,1)}, bf16[1024,640]{1,0:T(8,128)(2,1)}, u32[]{:S(2)}, u32[]{:S(2)}) collective-permute-start(bf16[1024,640]{1,0:T(8,128)(2,1)} %collective-permute-done.14.refs_19_.refs_3_), channel_id=1, source_target_pairs={{0,16},{16,0},{1,17},{17,1},{2,18},{18,2},{3,19},{19,3},{4,20},{20... | collective-permute-start | bytes 3932168 | tf_op jit(solution)/shard_map/ppermute | solution.py:24
  159.8 49.3 %collective-permute-start.16 = (bf16[1024,640]{1,0:T(8,128)(2,1)}, bf16[1024,640]{1,0:T(8,128)(2,1)}, u32[]{:S(2)}, u32[]{:S(2)}) collective-permute-start(bf16[1024,640]{1,0:T(8,128)(2,1)} %collective-permute-done.14.refs_19_.refs_3_), channel_id=1, source_target_pairs={{0,96},{32,0},{64,32},{96,64},{1,97},{33,1},{65,33},{97,65},{2,98}... | collective-permute-start | bytes 3932168 | tf_op jit(solution)/shard_map/ppermute | solution.py:24
  182.3 26.9 %collective-permute-start.9 = (bf16[3,16,8192]{2,1,0:T(8,128)(2,1)}, bf16[3,16,8192]{2,1,0:T(8,128)(2,1)}, u32[]{:S(2)}, u32[]{:S(2)}) collective-permute-start(bf16[3,16,8192]{2,1,0:T(8,128)(2,1)} %norm_image.3.refs_10_), channel_id=1, source_target_pairs={{0,12},{4,0},{8,4},{12,8},{1,13},{5,1},{9,5},{13,9},{2,14},{6,2},{... | collective-permute-start | bytes 2359304 | tf_op jit(solution)/shard_map/ppermute | solution.py:24
  187.5 46.0 %collective-permute-start.10 = (bf16[4,16,8192]{2,1,0:T(8,128)(2,1)}, bf16[4,16,8192]{2,1,0:T(8,128)(2,1)}, u32[]{:S(2)}, u32[]{:S(2)}) collective-permute-start(bf16[4,16,8192]{2,1,0:T(8,128)(2,1)} %norm_image.2.refs_9_), channel_id=1, source_target_pairs={{0,4},{4,8},{8,12},{12,0},{1,5},{5,9},{9,13},{13,1},{2,6},{6,10},{... | collective-permute-start | bytes 3145736 | tf_op jit(solution)/shard_map/ppermute | solution.py:24
  188.8 46.4 %collective-permute-start.8 = (bf16[4,16,8192]{2,1,0:T(8,128)(2,1)}, bf16[4,16,8192]{2,1,0:T(8,128)(2,1)}, u32[]{:S(2)}, u32[]{:S(2)}) collective-permute-start(bf16[4,16,8192]{2,1,0:T(8,128)(2,1)} %norm_image.2.refs_9_), channel_id=1, source_target_pairs={{0,12},{4,0},{8,4},{12,8},{1,13},{5,1},{9,5},{13,9},{2,14},{6,2},{... | collective-permute-start | bytes 3145736 | tf_op jit(solution)/shard_map/ppermute | solution.py:24
  190.2 54.6 %collective-permute-start.34 = (bf16[1024,640]{1,0:T(8,128)(2,1)}, bf16[1024,640]{1,0:T(8,128)(2,1)}, u32[]{:S(2)}, u32[]{:S(2)}) collective-permute-start(bf16[1024,640]{1,0:T(8,128)(2,1)} %collective-permute-done.31.refs_36_.refs_12_), channel_id=1, source_target_pairs={{0,16},{16,0},{1,17},{17,1},{2,18},{18,2},{3,19},{19,3},{4,20},{20... | collective-permute-start | bytes 3932168 | tf_op jit(solution)/shard_map/ppermute | solution.py:24
  209.1 20.9 %collective-permute-start.13 = (bf16[3,16,8192]{2,1,0:T(8,128)(2,1)S(1)}, bf16[3,16,8192]{2,1,0:T(8,128)(2,1)}, u32[]{:S(2)}, u32[]{:S(2)}) collective-permute-start(bf16[3,16,8192]{2,1,0:T(8,128)(2,1)S(1)} %copy-done), channel_id=1, source_target_pairs={{0,4},{4,8},{8,12},{12,0},{1,5},{5,9},{9,13},{13,1},{2,6},{6,10},{... | collective-permute-start | bytes 2359304 | tf_op jit(solution)/shard_map/ppermute | solution.py:24
  209.1 31.3 %collective-permute-start.12 = (bf16[3,16,8192]{2,1,0:T(8,128)(2,1)}, bf16[3,16,8192]{2,1,0:T(8,128)(2,1)}, u32[]{:S(2)}, u32[]{:S(2)}) collective-permute-start(bf16[3,16,8192]{2,1,0:T(8,128)(2,1)} %collective-permute-done.9.refs_12_), channel_id=1, source_target_pairs={{0,12},{4,0},{8,4},{12,8},{1,13},{5,1},{9,5},{13,9},{2,14},{6,2},{... | collective-permute-start | bytes 2359304 | tf_op jit(solution)/shard_map/ppermute | solution.py:24
  230.0 30.6 %collective-permute-start.23 = (bf16[1024,640]{1,0:T(8,128)(2,1)}, bf16[1024,640]{1,0:T(8,128)(2,1)}, u32[]{:S(2)}, u32[]{:S(2)}) collective-permute-start(bf16[1024,640]{1,0:T(8,128)(2,1)} %collective-permute-done.15.refs_20_.refs_4_), channel_id=1, source_target_pairs={{0,3},{1,0},{2,1},{3,2},{4,7},{5,4},{6,5},{7,6},{8,11},{9,8},{10,9... | collective-permute-start | bytes 3932168 | tf_op jit(solution)/shard_map/ppermute | solution.py:24
  233.5 29.3 %collective-permute-start.19 = (bf16[1024,640]{1,0:T(8,128)(2,1)}, bf16[1024,640]{1,0:T(8,128)(2,1)S(1)}, u32[]{:S(2)}, u32[]{:S(2)}) collective-permute-start(bf16[1024,640]{1,0:T(8,128)(2,1)} %collective-permute-done.15.refs_20_.refs_4_), channel_id=1, source_target_pairs={{0,16},{16,0},{1,17},{17,1},{2,18},{18,2},{3,19},{19,3},{4,20},{20... | collective-permute-start | bytes 3932168 | tf_op jit(solution)/shard_map/ppermute | solution.py:24
  235.2 27.7 %collective-permute-start.26 = (bf16[1024,640]{1,0:T(8,128)(2,1)}, bf16[1024,640]{1,0:T(8,128)(2,1)}, u32[]{:S(2)}, u32[]{:S(2)}) collective-permute-start(bf16[1024,640]{1,0:T(8,128)(2,1)} %collective-permute-done.1.refs_26_), channel_id=1, source_target_pairs={{0,16},{16,0},{1,17},{17,1},{2,18},{18,2},{3,19},{19,3},{4,20},{20... | collective-permute-start | bytes 3932168 | tf_op jit(solution)/shard_map/ppermute | solution.py:24
  240.4 31.2 %collective-permute-start.25 = (bf16[1024,640]{1,0:T(8,128)(2,1)}, bf16[1024,640]{1,0:T(8,128)(2,1)}, u32[]{:S(2)}, u32[]{:S(2)}) collective-permute-start(bf16[1024,640]{1,0:T(8,128)(2,1)} %collective-permute-done.24.refs_37_.refs_13_), channel_id=1, source_target_pairs={{0,1},{1,2},{2,3},{3,0},{4,5},{5,6},{6,7},{7,4},{8,9},{9,10},{10,1... | collective-permute-start | bytes 3932168 | tf_op jit(solution)/shard_map/ppermute | solution.py:24
  244.8 29.0 %collective-permute-start.35 = (bf16[1024,640]{1,0:T(8,128)(2,1)}, bf16[1024,640]{1,0:T(8,128)(2,1)S(1)}, u32[]{:S(2)}, u32[]{:S(2)}) collective-permute-start(bf16[1024,640]{1,0:T(8,128)(2,1)} %collective-permute-done.24.refs_37_.refs_13_), channel_id=1, source_target_pairs={{0,16},{16,0},{1,17},{17,1},{2,18},{18,2},{3,19},{19,3},{4,20},{20... | collective-permute-start | bytes 3932168 | tf_op jit(solution)/shard_map/ppermute | solution.py:24
  260.6 17.4 %collective-permute-start.27 = (bf16[1024,640]{1,0:T(8,128)(2,1)}, bf16[1024,640]{1,0:T(8,128)(2,1)}, u32[]{:S(2)}, u32[]{:S(2)}) collective-permute-start(bf16[1024,640]{1,0:T(8,128)(2,1)} %collective-permute-done.22.refs_27_), channel_id=1, source_target_pairs={{0,16},{16,0},{1,17},{17,1},{2,18},{18,2},{3,19},{19,3},{4,20},{20... | collective-permute-start | bytes 3932168 | tf_op jit(solution)/shard_map/ppermute | solution.py:24
  262.8 15.1 %collective-permute-start.20 = (bf16[1024,640]{1,0:T(8,128)(2,1)}, bf16[1024,640]{1,0:T(8,128)(2,1)}, u32[]{:S(2)}, u32[]{:S(2)}) collective-permute-start(bf16[1024,640]{1,0:T(8,128)(2,1)} %collective-permute-done.16.refs_21_.refs_5_), channel_id=1, source_target_pairs={{0,16},{16,0},{1,17},{17,1},{2,18},{18,2},{3,19},{19,3},{4,20},{20... | collective-permute-start | bytes 3932168 | tf_op jit(solution)/shard_map/ppermute | solution.py:24
  262.9 37.3 %collective-permute-start.28 = (bf16[1024,640]{1,0:T(8,128)(2,1)}, bf16[1024,640]{1,0:T(8,128)(2,1)}, u32[]{:S(2)}, u32[]{:S(2)}) collective-permute-start(bf16[1024,640]{1,0:T(8,128)(2,1)} %collective-permute-done.23.refs_28_), channel_id=1, source_target_pairs={{0,16},{16,0},{1,17},{17,1},{2,18},{18,2},{3,19},{19,3},{4,20},{20... | collective-permute-start | bytes 3932168 | tf_op jit(solution)/shard_map/ppermute | solution.py:24
  271.5 28.6 %collective-permute-start.29 = (bf16[1024,640]{1,0:T(8,128)(2,1)}, bf16[1024,640]{1,0:T(8,128)(2,1)}, u32[]{:S(2)}, u32[]{:S(2)}) collective-permute-start(bf16[1024,640]{1,0:T(8,128)(2,1)} %collective-permute-done.25.refs_29_), channel_id=1, source_target_pairs={{0,16},{16,0},{1,17},{17,1},{2,18},{18,2},{3,19},{19,3},{4,20},{20... | collective-permute-start | bytes 3932168 | tf_op jit(solution)/shard_map/ppermute | solution.py:24
  273.9 26.3 %collective-permute-start.11 = (bf16[4,16,8192]{2,1,0:T(8,128)(2,1)}, bf16[4,16,8192]{2,1,0:T(8,128)(2,1)}, u32[]{:S(2)}, u32[]{:S(2)}) collective-permute-start(bf16[4,16,8192]{2,1,0:T(8,128)(2,1)} %collective-permute-done.10.refs_15_), channel_id=1, source_target_pairs={{0,4},{4,8},{8,12},{12,0},{1,5},{5,9},{9,13},{13,1},{2,6},{6,10},{... | collective-permute-start | bytes 3145736 | tf_op jit(solution)/shard_map/ppermute | solution.py:24
  321.1 23.5 %collective-permute-start.42 = (bf16[576,256]{1,0:T(8,128)(2,1)S(1)}, bf16[576,256]{1,0:T(8,128)(2,1)S(1)}, u32[]{:S(2)}, u32[]{:S(2)}) collective-permute-start(bf16[576,256]{1,0:T(8,128)(2,1)S(1)} %get-tuple-element.48), channel_id=1, source_target_pairs={{0,3},{1,0},{2,1},{3,2},{4,7},{5,4},{6,5},{7,6},{8,11},{9,8},{10,9... | collective-permute-start | bytes 884744 | tf_op jit(solution)/shard_map/ppermute | solution.py:24
  340.2 40.7 %collective-permute-start.39 = (bf16[576,512]{1,0:T(8,128)(2,1)S(1)}, bf16[576,512]{1,0:T(8,128)(2,1)S(1)}, u32[]{:S(2)}, u32[]{:S(2)}) collective-permute-start(bf16[576,512]{1,0:T(8,128)(2,1)S(1)} %get-tuple-element.44), channel_id=1, source_target_pairs={{0,3},{1,0},{2,1},{3,2},{4,7},{5,4},{6,5},{7,6},{8,11},{9,8},{10,9... | collective-permute-start | bytes 1769480 | tf_op jit(solution)/shard_map/ppermute | solution.py:24
  340.3 40.6 %collective-permute-start.41 = (bf16[576,512]{1,0:T(8,128)(2,1)S(1)}, bf16[576,512]{1,0:T(8,128)(2,1)S(1)}, u32[]{:S(2)}, u32[]{:S(2)}) collective-permute-start(bf16[576,512]{1,0:T(8,128)(2,1)S(1)} %get-tuple-element.46), channel_id=1, source_target_pairs={{0,1},{1,2},{2,3},{3,0},{4,5},{5,6},{6,7},{7,4},{8,9},{9,10},{10,1... | collective-permute-start | bytes 1769480 | tf_op jit(solution)/shard_map/ppermute | solution.py:24
  341.7 39.1 %collective-permute-start.40 = (bf16[576,512]{1,0:T(8,128)(2,1)S(1)}, bf16[576,512]{1,0:T(8,128)(2,1)S(1)}, u32[]{:S(2)}, u32[]{:S(2)}) collective-permute-start(bf16[576,512]{1,0:T(8,128)(2,1)S(1)} %get-tuple-element.45), channel_id=1, source_target_pairs={{0,2},{1,3},{2,0},{3,1},{4,6},{5,7},{6,4},{7,5},{8,10},{9,11},{10,... | collective-permute-start | bytes 1769480 | tf_op jit(solution)/shard_map/ppermute | solution.py:24
  341.9 31.4 %collective-permute-start.43 = (bf16[576,256]{1,0:T(8,128)(2,1)S(1)}, bf16[576,256]{1,0:T(8,128)(2,1)S(1)}, u32[]{:S(2)}, u32[]{:S(2)}) collective-permute-start(bf16[576,256]{1,0:T(8,128)(2,1)S(1)} %get-tuple-element.49), channel_id=1, source_target_pairs={{0,2},{1,3},{2,0},{3,1},{4,6},{5,7},{6,4},{7,5},{8,10},{9,11},{10,... | collective-permute-start | bytes 884744 | tf_op jit(solution)/shard_map/ppermute | solution.py:24
  344.7 36.1 %collective-permute-start.44 = (bf16[576,256]{1,0:T(8,128)(2,1)S(1)}, bf16[576,256]{1,0:T(8,128)(2,1)S(1)}, u32[]{:S(2)}, u32[]{:S(2)}) collective-permute-start(bf16[576,256]{1,0:T(8,128)(2,1)S(1)} %get-tuple-element.50), channel_id=1, source_target_pairs={{0,1},{1,2},{2,3},{3,0},{4,5},{5,6},{6,7},{7,4},{8,9},{9,10},{10,1... | collective-permute-start | bytes 884744 | tf_op jit(solution)/shard_map/ppermute | solution.py:24
  (11 other events, 190.5 us)

commit v6 on v5

--- a/solution.py
+++ b/solution.py
@@ -424,12 +424,15 @@
             for delta in range(4):
                 number = row * 4 + (mine + delta) % 4
                 begin = number * 128
-                for unit in range(8):
-                    source = pl.multiple_of(text_ref[number * 8 + unit] * UNIT, UNIT)
-                    target = pl.multiple_of(WINDOW + begin + unit * UNIT, UNIT)
-                    query, pair = parts[delta]
-                    merged_ref[pl.ds(target, UNIT), :q_width] = query[pl.ds(source, UNIT), :]
-                    merged_ref[pl.ds(target, UNIT), q_width:] = pair[pl.ds(source, UNIT), :]
+
+                @pl.when((begin < run_start) | (begin + 128 > run_end))
+                def _(delta=delta, number=number, begin=begin):
+                    for unit in range(8):
+                        source = pl.multiple_of(text_ref[number * 8 + unit] * UNIT, UNIT)
+                        target = pl.multiple_of(WINDOW + begin + unit * UNIT, UNIT)
+                        query, pair = parts[delta]
+                        merged_ref[pl.ds(target, UNIT), :q_width] = query[pl.ds(source, UNIT), :]
+                        merged_ref[pl.ds(target, UNIT), q_width:] = pair[pl.ds(source, UNIT), :]
 
                 @pl.when((begin < run_end) & (begin + 128 > run_start))
                 def _():
@@ -636,10 +639,15 @@
     }
     quarters = jnp.stack([quarter ^ 0, quarter ^ 1, quarter ^ 2, quarter ^ 3]) * 2 * PIECE
 
-    doc_ids, direct[2, 0] = lax.optimization_barrier((doc_ids, direct[2, 0]))
+    doc_ids, t1_high = lax.optimization_barrier((doc_ids, t1_high))
     place, slots, text_index, info, in_doc = tables(
         tile_group, tile_offset, seq_len, doc_ids, group, z, y, quarters
     )
+    frequency = THETA ** (-(jnp.arange(HD // 2, dtype=jnp.float32) * 2.0) / HD)
+    angles = in_doc.astype(jnp.float32)[:, None] * frequency[None, :]
+    cosine = jnp.concatenate([jnp.cos(angles), jnp.cos(angles)], axis=-1)
+    sine = jnp.concatenate([-jnp.sin(angles), jnp.sin(angles)], axis=-1)
+    arrived, cosine, sine = lax.optimization_barrier((arrived, cosine, sine))
     i_low = norm_image(arrived, gain, slots[:4])
     i_high = norm_image(arrived, gain, slots[4:])
     i3_low = shifted(i_low, "z", 1)
@@ -657,11 +665,6 @@
     ]
     q_biases = [value[None, :4 * HD] for value in biases]
     kv_bias = jnp.concatenate([value[None, 4 * HD:] for value in biases], axis=1)
-    frequency = THETA ** (-(jnp.arange(HD // 2, dtype=jnp.float32) * 2.0) / HD)
-    angles = in_doc.astype(jnp.float32)[:, None] * frequency[None, :]
-    cosine = jnp.concatenate([jnp.cos(angles), jnp.cos(angles)], axis=-1)
-    sine = jnp.concatenate([-jnp.sin(angles), jnp.sin(angles)], axis=-1)
-
     place, text_index, info = lax.optimization_barrier((place, text_index, info))
     texts = (t_low, t_high, t1_low, t1_high, t2_low, t2_high, t3_low, t3_high)
     images = (i_low, i_high, i1_low, i1_high, i2_low, i2_high, i3_low, i3_high)

time: 398 us -> 398 us (level)
  waiting for transfers between devices: 206 us -> 210 us
    ppermute x45, starting transfers between devices: 75.8 us -> 71.5 us  [shifted(): lax.ppermute(block, axis, [(low, (low + step) % count) for low in range(c...]
where the time goes in v6:
time: 398 us
  waiting for transfers between devices  210 us (53%)
  Pallas kernels  82.6 us (21%)
  starting transfers between devices  76.9 us (19%)
  other arithmetic  13.9 us (3%)
  local copies, waits for them, and re-layouts  10 us (3%)
  between operations  4.29 us (1%)
    ppermute x45, waiting for transfers between devices, shifted(): lax.ppermute(block, axis, [(low, (low + step) % count) for low in range(c...  190 us
    ppermute x45, starting transfers between devices, shifted(): lax.ppermute(block, axis, [(low, (low + step) % count) for low in range(c...  71.5 us
    pallas_call x2, Pallas kernels, project_q(): pl.pallas_call(kernel, grid_spec=pltpu.PrefetchScalarGridSpec(num_scalar_...  28.6 us
    pallas_call x1, Pallas kernels, project_kv(): pl.pallas_call(project_kv_kernel, grid_spec=pltpu.PrefetchScalarGridSpec(...  20.9 us
    all_to_all x1, waiting for transfers between devices, one_device(): lax.all_to_all(outgoing, ('x', 'c'), split_axis=0, concat_axis=0, tiled=T...  19.6 us
    pallas_call x1, Pallas kernels, attend(): pl.pallas_call(attend_kernel, grid_spec=pltpu.PrefetchScalarGridSpec(num_...  16.6 us
    pallas_call x2, Pallas kernels, norm_image(): pl.pallas_call(norm_image_kernel, grid_spec=pltpu.PrefetchScalarGridSpec(...  8.1 us
  transfers between devices with their start and end apart: 46, of which 17 were waited for; matrix products, arithmetic and copies ran while one was open for 6% of the time, Pallas kernels for 11%

profile of v6, /device:TPU:1, one launch (start us, length us, event | category | flops | bytes accessed | tf_op | source)
XLA Modules:
  0.0 397.7 jit_solution(18068848871235744899)
XLA Ops:
  0.0 2.6 shard_map.127.refs_1_
  2.6 2.5 collective-permute-start.2
  5.1 2.1 collective-permute-start.1
  8.3 2.8 copy.19
  11.0 1.5 fusion.1
  12.5 2.0 constant_dynamic-slice_fusion
  15.8 2.6 shard_map.128.refs_2_
  21.1 28.4 %collective-permute-done.38 = f32[640]{0:T(1024)S(1)} collective-permute-done((f32[640]{0:T(1024)S(1)}, f32[640]{0:T(1024)S(1)}, u32[]{:S(2)}, u32[]{:S(2)}) %collective-permute-start.38) | collective-permute-done | bytes 2592 | tf_op jit(solution)/shard_map/ppermute | solution.py:24
  49.5 1.6 collective-permute-start.37
  51.1 2.4 collective-permute-done.37
  55.9 2.7 collective-permute-start
  58.6 2.3 collective-permute-start.12
  61.0 2.7 collective-permute-start.13
  63.6 13.8 %collective-permute-done.refs_4_ = bf16[64,8192]{1,0:T(8,128)(2,1)S(1)} collective-permute-done((bf16[64,8192]{1,0:T(8,128)(2,1)}, bf16[64,8192]{1,0:T(8,128)(2,1)S(1)}, u32[]{:S(2)}, u32[]{:S(2)}) %collective-permute-start) | collective-permute-done | bytes 1048608 | tf_op jit(solution)/shard_map/ppermute | solution.py:24
  77.4 3.5 collective-permute-start.4
  80.9 4.1 %collective-permute-done.12.refs_18_.refs_2_ = bf16[1024,640]{1,0:T(8,128)(2,1)} collective-permute-done((bf16[1024,640]{1,0:T(8,128)(2,1)}, bf16[1024,640]{1,0:T(8,128)(2,1)}, u32[]{:S(2)}, u32[]{:S(2)}) %collective-permute-start.12) | collective-permute-done | bytes 1310752 | tf_op jit(solution)/shard_map/ppermute | solution.py:24
  84.9 10.4 %collective-permute-start.32 = (bf16[1024,640]{1,0:T(8,128)(2,1)}, bf16[1024,640]{1,0:T(8,128)(2,1)}, u32[]{:S(2)}, u32[]{:S(2)}) collective-permute-start(bf16[1024,640]{1,0:T(8,128)(2,1)} %collective-permute-done.30.refs_34_.refs_10_), channel_id=1, source_target_pairs={{0,16},{16,0},{1,17},{17,1},{2,18},{18,2},{3,19},{19,3},{4,20},{20... | collective-permute-start | bytes 3932168 | tf_op jit(solution)/shard_map/ppermute | solution.py:24
  96.5 16.5 %collective-permute-done.13.refs_19_.refs_3_ = bf16[1024,640]{1,0:T(8,128)(2,1)} collective-permute-done((bf16[1024,640]{1,0:T(8,128)(2,1)S(1)}, bf16[1024,640]{1,0:T(8,128)(2,1)}, u32[]{:S(2)}, u32[]{:S(2)}) %collective-permute-start.13) | collective-permute-done | bytes 1310752 | tf_op jit(solution)/shard_map/ppermute | solution.py:24
  113.0 3.2 collective-permute-start.20
  116.3 6.7 %collective-permute-start.16 = (bf16[1024,640]{1,0:T(8,128)(2,1)}, bf16[1024,640]{1,0:T(8,128)(2,1)S(1)}, u32[]{:S(2)}, u32[]{:S(2)}) collective-permute-start(bf16[1024,640]{1,0:T(8,128)(2,1)} %collective-permute-done.12.refs_18_.refs_2_), channel_id=1, source_target_pairs={{0,16},{16,0},{1,17},{17,1},{2,18},{18,2},{3,19},{19,3},{4,20},{20... | collective-permute-start | bytes 3932168 | tf_op jit(solution)/shard_map/ppermute | solution.py:24
  125.9 3.3 spread.1
  129.2 5.4 %all-to-all-start = ((bf16[8,16,8192]{2,1,0:T(8,128)(2,1)}), bf16[8,16,8192]{2,1,0:T(8,128)(2,1)}, u32[]{:S(2)}, u32[]{:S(2)}) async-start(bf16[8,16,8192]{2,1,0:T(8,128)(2,1)} %spread.1), calls=%async_computation | async-start | bytes 4194304 | tf_op jit(solution)/shard_map/all_to_all | solution.py:617
  142.0 2.9 collective-permute-start.24
  146.6 8.4 %collective-permute-done.14.refs_20_.refs_4_ = bf16[1024,640]{1,0:T(8,128)(2,1)} collective-permute-done((bf16[1024,640]{1,0:T(8,128)(2,1)}, bf16[1024,640]{1,0:T(8,128)(2,1)}, u32[]{:S(2)}, u32[]{:S(2)}) %collective-permute-start.14) | collective-permute-done | bytes 1310752 | tf_op jit(solution)/shard_map/ppermute | solution.py:24
  158.8 19.6 %all-to-all-done.rows_ref = bf16[8,16,8192]{2,1,0:T(8,128)(2,1)} async-done(((bf16[8,16,8192]{2,1,0:T(8,128)(2,1)}), bf16[8,16,8192]{2,1,0:T(8,128)(2,1)}, u32[]{:S(2)}, u32[]{:S(2)}) %all-to-all-start) | async-done | bytes 2097184 | tf_op jit(solution)/shard_map/all_to_all | solution.py:617
  178.4 3.5 norm_image.3.refs_10_
  182.2 5.3 %collective-permute-done.24.refs_37_.refs_13_ = bf16[1024,640]{1,0:T(8,128)(2,1)} collective-permute-done((bf16[1024,640]{1,0:T(8,128)(2,1)}, bf16[1024,640]{1,0:T(8,128)(2,1)}, u32[]{:S(2)}, u32[]{:S(2)}) %collective-permute-start.24) | collective-permute-done | bytes 1310752 | tf_op jit(solution)/shard_map/ppermute | solution.py:24
  187.6 1.5 collective-permute-start.34
  189.1 4.6 %norm_image.2.refs_9_ = bf16[4,16,8192]{2,1,0:T(8,128)(2,1)} custom-call(s32[4]{0:T(128)} %bitcast.37, bf16[8,16,8192]{2,1,0:T(8,128)(2,1)} %all-to-all-done.rows_ref, f32[1,8192]{1,0:T(1,128)} %bitcast.35), custom_call_target="tpu_custom_call" | custom-call | tf_op jit(solution)/shard_map/norm_image/pallas_call | solution.py:59
  193.7 2.7 collective-permute-start.6
  196.4 19.3 %collective-permute-done.15.refs_21_.refs_5_ = bf16[1024,640]{1,0:T(8,128)(2,1)} collective-permute-done((bf16[1024,640]{1,0:T(8,128)(2,1)}, bf16[1024,640]{1,0:T(8,128)(2,1)}, u32[]{:S(2)}, u32[]{:S(2)}) %collective-permute-start.15) | collective-permute-done | bytes 1310752 | tf_op jit(solution)/shard_map/ppermute | solution.py:24
  215.7 2.7 collective-permute-start.10
  219.2 17.3 %collective-permute-done.11.refs_16_ = bf16[3,16,8192]{2,1,0:T(8,128)(2,1)} collective-permute-done((bf16[3,16,8192]{2,1,0:T(8,128)(2,1)S(1)}, bf16[3,16,8192]{2,1,0:T(8,128)(2,1)}, u32[]{:S(2)}, u32[]{:S(2)}) %collective-permute-start.11) | collective-permute-done | bytes 786464 | tf_op jit(solution)/shard_map/ppermute | solution.py:24
  239.6 2.1 collective-permute-start.35
  241.8 4.1 %pad_maximum_fusion.refs_17_ = bf16[8192,128]{1,0:T(8,128)(2,1)} fusion(bf16[8192,64]{1,0:T(8,128)(2,1)} %copy.19, bf16[8192,64]{1,0:T(8,128)(2,1)S(1)} %copy.18), kind=kLoop, calls=%fused_computation.3 | loop fusion | flops 4194304 | bytes 4194304 | tf_op jit(solution)/shard_map/concatenate | solution.py:588
  245.9 20.2 %collective-permute-done.23.refs_28_ = bf16[1024,640]{1,0:T(8,128)(2,1)} collective-permute-done((bf16[1024,640]{1,0:T(8,128)(2,1)}, bf16[1024,640]{1,0:T(8,128)(2,1)}, u32[]{:S(2)}, u32[]{:S(2)}) %collective-permute-start.23) | collective-permute-done | bytes 1310752 | tf_op jit(solution)/shard_map/ppermute | solution.py:24
  266.1 2.0 collective-permute-start.19
  268.0 3.3 collective-permute-done.25.refs_29_
  271.4 2.3 collective-permute-start.29
  276.3 24.3 %collective-permute-done.9.refs_13_ = bf16[4,16,8192]{2,1,0:T(8,128)(2,1)} collective-permute-done((bf16[4,16,8192]{2,1,0:T(8,128)(2,1)}, bf16[4,16,8192]{2,1,0:T(8,128)(2,1)}, u32[]{:S(2)}, u32[]{:S(2)}) %collective-permute-start.9) | collective-permute-done | bytes 1048608 | tf_op jit(solution)/shard_map/ppermute | solution.py:24
  300.6 20.9 %project_kv.1 = (bf16[576,256]{1,0:T(8,128)(2,1)S(1)}, bf16[576,256]{1,0:T(8,128)(2,1)S(1)}, bf16[576,256]{1,0:T(8,128)(2,1)S(1)}, bf16[576,256]{1,0:T(8,128)(2,...) custom-call(s32[70]{0:T(128)S(1)} %concatenate.27.refs_0_, bf16[64,8192]{1,0:T(8,128)(2,1)} %shard_map.127.refs_1_, ...), custom_call_target="tpu_custom_call" | custom-call | flops 9663676416 | bytes 26214400 | tf_op jit(solution)/shard_map/project_kv/pallas_call | solution.py:289
  321.5 1.7 collective-permute-start.42
  323.2 17.2 %project_q.2 = (bf16[576,512]{1,0:T(8,128)(2,1)S(1)}, bf16[576,512]{1,0:T(8,128)(2,1)S(1)}) custom-call(s32[70]{0:T(128)S(1)} %concatenate.27.refs_0_, bf16[576,8192]{1,0:T(8,128)(2,1)} %get-tuple-element.50.refs_1_, bf16[1024,640]{1,0:T(8,128)(2,1)} %collective-permute-done.12.refs_18_.refs_2_, bf16[1024,640]{1,0:T(8,128)(2,1)} %collective-permute-done.13.refs_19_.refs_3_, ...), custom_call_target="tpu_custom_call" | custom-call | flops 9663676416 | bytes 26214400 | tf_op jit(solution)/shard_map/project_q/pallas_call | solution.py:358
  342.1 2.8 collective-permute-start.43
  344.9 11.4 %project_q.3.q0 = bf16[576,512]{1,0:T(8,128)(2,1)S(1)} custom-call(s32[70]{0:T(128)S(1)} %concatenate.27.refs_0_, bf16[576,8192]{1,0:T(8,128)(2,1)} %get-tuple-element.50.refs_1_, bf16[8192,512]{1,0:T(8,128)(2,1)} %refs_2_.1, f32[1,512]{1,0:T(1,128)S(1)} %bitcast.28, f32[576,128]{1,0:T(8,128)S(1)} %pad_maximum_fusion.3.refs_44_.refs_20_.refs_4_, ...), custom_call_target="tpu_custom_call" | custom-call | flops 4831838208 | bytes 17825792 | tf_op jit(solution)/shard_map/project_q/pallas_call | solution.py:358
  356.3 17.2 %collective-permute-done.43.kv2 = bf16[576,256]{1,0:T(8,128)(2,1)S(1)} collective-permute-done((bf16[576,256]{1,0:T(8,128)(2,1)S(1)}, bf16[576,256]{1,0:T(8,128)(2,1)S(1)}, u32[]{:S(2)}, u32[]{:S(2)}) %collective-permute-start.43) | collective-permute-done | bytes 294944 | tf_op jit(solution)/shard_map/ppermute | solution.py:24
  373.6 7.5 %collective-permute-done.44.kv3 = bf16[576,256]{1,0:T(8,128)(2,1)S(1)} collective-permute-done((bf16[576,256]{1,0:T(8,128)(2,1)S(1)}, bf16[576,256]{1,0:T(8,128)(2,1)S(1)}, u32[]{:S(2)}, u32[]{:S(2)}) %collective-permute-start.44) | collective-permute-done | bytes 294944 | tf_op jit(solution)/shard_map/ppermute | solution.py:24
  381.1 16.6 %attend.1 = bf16[2048,512]{1,0:T(8,128)(2,1)} custom-call(s32[12]{0:T(128)S(1)} %concatenate.31.info_ref, s32[128]{0:T(128)S(1)} %reshape.320.text_ref, bf16[576,512]{1,0:T(8,128)(2,1)S(1)} %project_q.3.q0, bf16[576,512]{1,0:T(8,128)(2,1)S(1)} %collective-permute-done.39.q1, bf16[576,512]{1,0:T(8,128)(2,1)S(1)} %collective-permute-done.40.q2, ...), custom_call_target="tpu_custom_call" | custom-call | tf_op jit(solution)/shard_map/attend/pallas_call | solution.py:505
  (143 shorter events, 29.2 us)
Async XLA Ops:
  2.6 56.0 %collective-permute-start.2 = (bf16[64,8192]{1,0:T(8,128)(2,1)}, bf16[64,8192]{1,0:T(8,128)(2,1)}, u32[]{:S(2)}, u32[]{:S(2)}) collective-permute-start(bf16[64,8192]{1,0:T(8,128)(2,1)} %shard_map.127.refs_1_), channel_id=1, source_target_pairs={{0,4},{4,8},{8,12},{12,0},{1,5},{5,9},{9,13},{13,1},{2,6},{6,10},{... | collective-permute-start | bytes 3145736 | tf_op jit(solution)/shard_map/ppermute | solution.py:24
  5.1 55.9 %collective-permute-start.1 = (bf16[64,8192]{1,0:T(8,128)(2,1)}, bf16[64,8192]{1,0:T(8,128)(2,1)}, u32[]{:S(2)}, u32[]{:S(2)}) collective-permute-start(bf16[64,8192]{1,0:T(8,128)(2,1)} %shard_map.127.refs_1_), channel_id=1, source_target_pairs={{0,12},{4,0},{8,4},{12,8},{1,13},{5,1},{9,5},{13,9},{2,14},{6,2},{... | collective-permute-start | bytes 3145736 | tf_op jit(solution)/shard_map/ppermute | solution.py:24
  15.8 109.3 %copy-start.14 = (s32[32]{0:T(128)S(1)}, s32[32]{0:T(128)}, u32[]{:S(2)}) copy-start(s32[32]{0:T(128)} %param.15) | copy-start | bytes 388
  18.4 42.6 %collective-permute-start.5 = (bf16[64,8192]{1,0:T(8,128)(2,1)}, bf16[64,8192]{1,0:T(8,128)(2,1)S(1)}, u32[]{:S(2)}, u32[]{:S(2)}) collective-permute-start(bf16[64,8192]{1,0:T(8,128)(2,1)} %shard_map.128.refs_2_), channel_id=1, source_target_pairs={{0,4},{4,8},{8,12},{12,0},{1,5},{5,9},{9,13},{13,1},{2,6},{6,10},{... | collective-permute-start | bytes 3145736 | tf_op jit(solution)/shard_map/ppermute | solution.py:24
  18.4 59.0 %collective-permute-start.30 = (bf16[1024,640]{1,0:T(8,128)(2,1)}, bf16[1024,640]{1,0:T(8,128)(2,1)}, u32[]{:S(2)}, u32[]{:S(2)}) collective-permute-start(bf16[1024,640]{1,0:T(8,128)(2,1)} %pad_maximum_fusion.1), channel_id=1, source_target_pairs={{0,1},{1,2},{2,3},{3,0},{4,5},{5,6},{6,7},{7,4},{8,9},{9,10},{10,1... | collective-permute-start | bytes 3932168 | tf_op jit(solution)/shard_map/ppermute | solution.py:24
  19.8 29.7 %collective-permute-start.38 = (f32[640]{0:T(1024)S(1)}, f32[640]{0:T(1024)S(1)}, u32[]{:S(2)}, u32[]{:S(2)}) collective-permute-start(f32[640]{0:T(1024)S(1)} %pad_maximum_fusion.5), channel_id=1, source_target_pairs={{0,1},{1,2},{2,3},{3,0},{4,5},{5,6},{6,7},{7,4},{8,9},{9,10},{10,1... | collective-permute-start | bytes 7688 | tf_op jit(solution)/shard_map/ppermute | solution.py:24
  49.5 4.0 collective-permute-start.37
  53.5 2.5 collective-permute-start.36
  55.9 21.5 %collective-permute-start = (bf16[64,8192]{1,0:T(8,128)(2,1)}, bf16[64,8192]{1,0:T(8,128)(2,1)S(1)}, u32[]{:S(2)}, u32[]{:S(2)}) collective-permute-start(bf16[64,8192]{1,0:T(8,128)(2,1)} %shard_map.128.refs_2_), channel_id=1, source_target_pairs={{0,12},{4,0},{8,4},{12,8},{1,13},{5,1},{9,5},{13,9},{2,14},{6,2},{... | collective-permute-start | bytes 3145736 | tf_op jit(solution)/shard_map/ppermute | solution.py:24
  58.6 26.3 %collective-permute-start.12 = (bf16[1024,640]{1,0:T(8,128)(2,1)}, bf16[1024,640]{1,0:T(8,128)(2,1)}, u32[]{:S(2)}, u32[]{:S(2)}) collective-permute-start(bf16[1024,640]{1,0:T(8,128)(2,1)} %pad_maximum_fusion.1), channel_id=1, source_target_pairs={{0,3},{1,0},{2,1},{3,2},{4,7},{5,4},{6,5},{7,6},{8,11},{9,8},{10,9... | collective-permute-start | bytes 3932168 | tf_op jit(solution)/shard_map/ppermute | solution.py:24
  60.9 34.4 %collective-permute-start.21 = (bf16[1024,640]{1,0:T(8,128)(2,1)S(1)}, bf16[1024,640]{1,0:T(8,128)(2,1)}, u32[]{:S(2)}, u32[]{:S(2)}) collective-permute-start(bf16[1024,640]{1,0:T(8,128)(2,1)S(1)} %pad_maximum_fusion.2), channel_id=1, source_target_pairs={{0,1},{1,2},{2,3},{3,0},{4,5},{5,6},{6,7},{7,4},{8,9},{9,10},{10,1... | collective-permute-start | bytes 3932168 | tf_op jit(solution)/shard_map/ppermute | solution.py:24
  61.0 55.3 %copy-start.4 = (bf16[64,8192]{1,0:T(8,128)(2,1)}, bf16[64,8192]{1,0:T(8,128)(2,1)S(1)}, u32[]{:S(2)}) copy-start(bf16[64,8192]{1,0:T(8,128)(2,1)S(1)} %collective-permute-done.5.refs_8_) | copy-start | bytes 3145732
  61.0 52.1 %collective-permute-start.13 = (bf16[1024,640]{1,0:T(8,128)(2,1)S(1)}, bf16[1024,640]{1,0:T(8,128)(2,1)}, u32[]{:S(2)}, u32[]{:S(2)}) collective-permute-start(bf16[1024,640]{1,0:T(8,128)(2,1)S(1)} %pad_maximum_fusion.2), channel_id=1, source_target_pairs={{0,3},{1,0},{2,1},{3,2},{4,7},{5,4},{6,5},{7,6},{8,11},{9,8},{10,9... | collective-permute-start | bytes 3932168 | tf_op jit(solution)/shard_map/ppermute | solution.py:24
  77.4 38.9 %collective-permute-start.3 = (bf16[64,8192]{1,0:T(8,128)(2,1)}, bf16[64,8192]{1,0:T(8,128)(2,1)S(1)}, u32[]{:S(2)}, u32[]{:S(2)}) collective-permute-start(bf16[64,8192]{1,0:T(8,128)(2,1)} %collective-permute-done.2.refs_7_), channel_id=1, source_target_pairs={{0,4},{4,8},{8,12},{12,0},{1,5},{5,9},{9,13},{13,1},{2,6},{6,10},{... | collective-permute-start | bytes 3145736 | tf_op jit(solution)/shard_map/ppermute | solution.py:24
  77.4 45.6 %collective-permute-start.4 = (bf16[64,8192]{1,0:T(8,128)(2,1)S(1)}, bf16[64,8192]{1,0:T(8,128)(2,1)S(1)}, u32[]{:S(2)}, u32[]{:S(2)}) collective-permute-start(bf16[64,8192]{1,0:T(8,128)(2,1)S(1)} %collective-permute-done.refs_4_), channel_id=1, source_target_pairs={{0,12},{4,0},{8,4},{12,8},{1,13},{5,1},{9,5},{13,9},{2,14},{6,2},{... | collective-permute-start | bytes 3145736 | tf_op jit(solution)/shard_map/ppermute | solution.py:24
  84.9 50.9 %collective-permute-start.32 = (bf16[1024,640]{1,0:T(8,128)(2,1)}, bf16[1024,640]{1,0:T(8,128)(2,1)}, u32[]{:S(2)}, u32[]{:S(2)}) collective-permute-start(bf16[1024,640]{1,0:T(8,128)(2,1)} %collective-permute-done.30.refs_34_.refs_10_), channel_id=1, source_target_pairs={{0,16},{16,0},{1,17},{17,1},{2,18},{18,2},{3,19},{19,3},{4,20},{20... | collective-permute-start | bytes 3932168 | tf_op jit(solution)/shard_map/ppermute | solution.py:24
  95.3 46.7 %collective-permute-start.31 = (bf16[1024,640]{1,0:T(8,128)(2,1)}, bf16[1024,640]{1,0:T(8,128)(2,1)}, u32[]{:S(2)}, u32[]{:S(2)}) collective-permute-start(bf16[1024,640]{1,0:T(8,128)(2,1)} %collective-permute-done.30.refs_34_.refs_10_), channel_id=1, source_target_pairs={{0,32},{32,64},{64,96},{96,0},{1,33},{33,65},{65,97},{97,1},{2,34}... | collective-permute-start | bytes 3932168 | tf_op jit(solution)/shard_map/ppermute | solution.py:24
  113.0 32.0 %collective-permute-start.20 = (bf16[1024,640]{1,0:T(8,128)(2,1)}, bf16[1024,640]{1,0:T(8,128)(2,1)}, u32[]{:S(2)}, u32[]{:S(2)}) collective-permute-start(bf16[1024,640]{1,0:T(8,128)(2,1)} %collective-permute-done.12.refs_18_.refs_2_), channel_id=1, source_target_pairs={{0,3},{1,0},{2,1},{3,2},{4,7},{5,4},{6,5},{7,6},{8,11},{9,8},{10,9... | collective-permute-start | bytes 3932168 | tf_op jit(solution)/shard_map/ppermute | solution.py:24
  116.3 28.9 %collective-permute-start.16 = (bf16[1024,640]{1,0:T(8,128)(2,1)}, bf16[1024,640]{1,0:T(8,128)(2,1)S(1)}, u32[]{:S(2)}, u32[]{:S(2)}) collective-permute-start(bf16[1024,640]{1,0:T(8,128)(2,1)} %collective-permute-done.12.refs_18_.refs_2_), channel_id=1, source_target_pairs={{0,16},{16,0},{1,17},{17,1},{2,18},{18,2},{3,19},{19,3},{4,20},{20... | collective-permute-start | bytes 3932168 | tf_op jit(solution)/shard_map/ppermute | solution.py:24
  124.0 31.0 %collective-permute-start.14 = (bf16[1024,640]{1,0:T(8,128)(2,1)}, bf16[1024,640]{1,0:T(8,128)(2,1)}, u32[]{:S(2)}, u32[]{:S(2)}) collective-permute-start(bf16[1024,640]{1,0:T(8,128)(2,1)} %collective-permute-done.12.refs_18_.refs_2_), channel_id=1, source_target_pairs={{0,32},{32,64},{64,96},{96,0},{1,33},{33,65},{65,97},{97,1},{2,34}... | collective-permute-start | bytes 3932168 | tf_op jit(solution)/shard_map/ppermute | solution.py:24
  129.2 49.2 %all-to-all-start = ((bf16[8,16,8192]{2,1,0:T(8,128)(2,1)}), bf16[8,16,8192]{2,1,0:T(8,128)(2,1)}, u32[]{:S(2)}, u32[]{:S(2)}) async-start(bf16[8,16,8192]{2,1,0:T(8,128)(2,1)} %spread.1), calls=%async_computation | async-start | bytes 4194304 | tf_op jit(solution)/shard_map/all_to_all | solution.py:617
  135.8 46.1 %collective-permute-start.33 = (bf16[1024,640]{1,0:T(8,128)(2,1)}, bf16[1024,640]{1,0:T(8,128)(2,1)}, u32[]{:S(2)}, u32[]{:S(2)}) collective-permute-start(bf16[1024,640]{1,0:T(8,128)(2,1)} %collective-permute-done.21.refs_35_.refs_11_), channel_id=1, source_target_pairs={{0,16},{16,0},{1,17},{17,1},{2,18},{18,2},{3,19},{19,3},{4,20},{20... | collective-permute-start | bytes 3932168 | tf_op jit(solution)/shard_map/ppermute | solution.py:24
  142.0 45.5 %collective-permute-start.24 = (bf16[1024,640]{1,0:T(8,128)(2,1)}, bf16[1024,640]{1,0:T(8,128)(2,1)}, u32[]{:S(2)}, u32[]{:S(2)}) collective-permute-start(bf16[1024,640]{1,0:T(8,128)(2,1)} %collective-permute-done.21.refs_35_.refs_11_), channel_id=1, source_target_pairs={{0,96},{32,0},{64,32},{96,64},{1,97},{33,1},{65,33},{97,65},{2,98}... | collective-permute-start | bytes 3932168 | tf_op jit(solution)/shard_map/ppermute | solution.py:24
  145.1 48.6 %collective-permute-start.22 = (bf16[1024,640]{1,0:T(8,128)(2,1)}, bf16[1024,640]{1,0:T(8,128)(2,1)}, u32[]{:S(2)}, u32[]{:S(2)}) collective-permute-start(bf16[1024,640]{1,0:T(8,128)(2,1)} %collective-permute-done.21.refs_35_.refs_11_), channel_id=1, source_target_pairs={{0,1},{1,2},{2,3},{3,0},{4,5},{5,6},{6,7},{7,4},{8,9},{9,10},{10,1... | collective-permute-start | bytes 3932168 | tf_op jit(solution)/shard_map/ppermute | solution.py:24
  145.2 48.5 %collective-permute-start.17 = (bf16[1024,640]{1,0:T(8,128)(2,1)}, bf16[1024,640]{1,0:T(8,128)(2,1)}, u32[]{:S(2)}, u32[]{:S(2)}) collective-permute-start(bf16[1024,640]{1,0:T(8,128)(2,1)} %collective-permute-done.13.refs_19_.refs_3_), channel_id=1, source_target_pairs={{0,16},{16,0},{1,17},{17,1},{2,18},{18,2},{3,19},{19,3},{4,20},{20... | collective-permute-start | bytes 3932168 | tf_op jit(solution)/shard_map/ppermute | solution.py:24
  154.9 60.7 %collective-permute-start.15 = (bf16[1024,640]{1,0:T(8,128)(2,1)}, bf16[1024,640]{1,0:T(8,128)(2,1)}, u32[]{:S(2)}, u32[]{:S(2)}) collective-permute-start(bf16[1024,640]{1,0:T(8,128)(2,1)} %collective-permute-done.13.refs_19_.refs_3_), channel_id=1, source_target_pairs={{0,96},{32,0},{64,32},{96,64},{1,97},{33,1},{65,33},{97,65},{2,98}... | collective-permute-start | bytes 3932168 | tf_op jit(solution)/shard_map/ppermute | solution.py:24
  181.9 33.7 %collective-permute-start.7 = (bf16[3,16,8192]{2,1,0:T(8,128)(2,1)}, bf16[3,16,8192]{2,1,0:T(8,128)(2,1)}, u32[]{:S(2)}, u32[]{:S(2)}) collective-permute-start(bf16[3,16,8192]{2,1,0:T(8,128)(2,1)} %norm_image.3.refs_10_), channel_id=1, source_target_pairs={{0,12},{4,0},{8,4},{12,8},{1,13},{5,1},{9,5},{13,9},{2,14},{6,2},{... | collective-permute-start | bytes 2359304 | tf_op jit(solution)/shard_map/ppermute | solution.py:24
  187.6 52.0 %collective-permute-start.34 = (bf16[1024,640]{1,0:T(8,128)(2,1)}, bf16[1024,640]{1,0:T(8,128)(2,1)}, u32[]{:S(2)}, u32[]{:S(2)}) collective-permute-start(bf16[1024,640]{1,0:T(8,128)(2,1)} %collective-permute-done.31.refs_36_.refs_12_), channel_id=1, source_target_pairs={{0,16},{16,0},{1,17},{17,1},{2,18},{18,2},{3,19},{19,3},{4,20},{20... | collective-permute-start | bytes 3932168 | tf_op jit(solution)/shard_map/ppermute | solution.py:24
  193.7 42.8 %collective-permute-start.8 = (bf16[4,16,8192]{2,1,0:T(8,128)(2,1)}, bf16[4,16,8192]{2,1,0:T(8,128)(2,1)}, u32[]{:S(2)}, u32[]{:S(2)}) collective-permute-start(bf16[4,16,8192]{2,1,0:T(8,128)(2,1)} %norm_image.2.refs_9_), channel_id=1, source_target_pairs={{0,4},{4,8},{8,12},{12,0},{1,5},{5,9},{9,13},{13,1},{2,6},{6,10},{... | collective-permute-start | bytes 3145736 | tf_op jit(solution)/shard_map/ppermute | solution.py:24
  193.7 44.0 %collective-permute-start.6 = (bf16[4,16,8192]{2,1,0:T(8,128)(2,1)}, bf16[4,16,8192]{2,1,0:T(8,128)(2,1)}, u32[]{:S(2)}, u32[]{:S(2)}) collective-permute-start(bf16[4,16,8192]{2,1,0:T(8,128)(2,1)} %norm_image.2.refs_9_), channel_id=1, source_target_pairs={{0,12},{4,0},{8,4},{12,8},{1,13},{5,1},{9,5},{13,9},{2,14},{6,2},{... | collective-permute-start | bytes 3145736 | tf_op jit(solution)/shard_map/ppermute | solution.py:24
  215.6 20.9 %collective-permute-start.11 = (bf16[3,16,8192]{2,1,0:T(8,128)(2,1)S(1)}, bf16[3,16,8192]{2,1,0:T(8,128)(2,1)}, u32[]{:S(2)}, u32[]{:S(2)}) collective-permute-start(bf16[3,16,8192]{2,1,0:T(8,128)(2,1)S(1)} %copy-done), channel_id=1, source_target_pairs={{0,4},{4,8},{8,12},{12,0},{1,5},{5,9},{9,13},{13,1},{2,6},{6,10},{... | collective-permute-start | bytes 2359304 | tf_op jit(solution)/shard_map/ppermute | solution.py:24
  215.7 23.3 %collective-permute-start.10 = (bf16[3,16,8192]{2,1,0:T(8,128)(2,1)}, bf16[3,16,8192]{2,1,0:T(8,128)(2,1)}, u32[]{:S(2)}, u32[]{:S(2)}) collective-permute-start(bf16[3,16,8192]{2,1,0:T(8,128)(2,1)} %collective-permute-done.7.refs_12_), channel_id=1, source_target_pairs={{0,12},{4,0},{8,4},{12,8},{1,13},{5,1},{9,5},{13,9},{2,14},{6,2},{... | collective-permute-start | bytes 2359304 | tf_op jit(solution)/shard_map/ppermute | solution.py:24
  236.5 29.5 %collective-permute-start.23 = (bf16[1024,640]{1,0:T(8,128)(2,1)}, bf16[1024,640]{1,0:T(8,128)(2,1)}, u32[]{:S(2)}, u32[]{:S(2)}) collective-permute-start(bf16[1024,640]{1,0:T(8,128)(2,1)} %collective-permute-done.14.refs_20_.refs_4_), channel_id=1, source_target_pairs={{0,3},{1,0},{2,1},{3,2},{4,7},{5,4},{6,5},{7,6},{8,11},{9,8},{10,9... | collective-permute-start | bytes 3932168 | tf_op jit(solution)/shard_map/ppermute | solution.py:24
  236.5 31.5 %collective-permute-start.18 = (bf16[1024,640]{1,0:T(8,128)(2,1)}, bf16[1024,640]{1,0:T(8,128)(2,1)}, u32[]{:S(2)}, u32[]{:S(2)}) collective-permute-start(bf16[1024,640]{1,0:T(8,128)(2,1)} %collective-permute-done.14.refs_20_.refs_4_), channel_id=1, source_target_pairs={{0,16},{16,0},{1,17},{17,1},{2,18},{18,2},{3,19},{19,3},{4,20},{20... | collective-permute-start | bytes 3932168 | tf_op jit(solution)/shard_map/ppermute | solution.py:24
  237.6 8.2 %collective-permute-start.26 = (bf16[1024,640]{1,0:T(8,128)(2,1)}, bf16[1024,640]{1,0:T(8,128)(2,1)}, u32[]{:S(2)}, u32[]{:S(2)}) collective-permute-start(bf16[1024,640]{1,0:T(8,128)(2,1)} %collective-permute-done.20.refs_26_), channel_id=1, source_target_pairs={{0,16},{16,0},{1,17},{17,1},{2,18},{18,2},{3,19},{19,3},{4,20},{20... | collective-permute-start | bytes 3932168 | tf_op jit(solution)/shard_map/ppermute | solution.py:24
  239.0 32.4 %collective-permute-start.25 = (bf16[1024,640]{1,0:T(8,128)(2,1)}, bf16[1024,640]{1,0:T(8,128)(2,1)}, u32[]{:S(2)}, u32[]{:S(2)}) collective-permute-start(bf16[1024,640]{1,0:T(8,128)(2,1)} %collective-permute-done.24.refs_37_.refs_13_), channel_id=1, source_target_pairs={{0,1},{1,2},{2,3},{3,0},{4,5},{5,6},{6,7},{7,4},{8,9},{9,10},{10,1... | collective-permute-start | bytes 3932168 | tf_op jit(solution)/shard_map/ppermute | solution.py:24
  239.6 34.8 %collective-permute-start.35 = (bf16[1024,640]{1,0:T(8,128)(2,1)}, bf16[1024,640]{1,0:T(8,128)(2,1)}, u32[]{:S(2)}, u32[]{:S(2)}) collective-permute-start(bf16[1024,640]{1,0:T(8,128)(2,1)} %collective-permute-done.24.refs_37_.refs_13_), channel_id=1, source_target_pairs={{0,16},{16,0},{1,17},{17,1},{2,18},{18,2},{3,19},{19,3},{4,20},{20... | collective-permute-start | bytes 3932168 | tf_op jit(solution)/shard_map/ppermute | solution.py:24
  245.8 30.4 %collective-permute-start.27 = (bf16[1024,640]{1,0:T(8,128)(2,1)}, bf16[1024,640]{1,0:T(8,128)(2,1)}, u32[]{:S(2)}, u32[]{:S(2)}) collective-permute-start(bf16[1024,640]{1,0:T(8,128)(2,1)} %collective-permute-done.22.refs_27_), channel_id=1, source_target_pairs={{0,16},{16,0},{1,17},{17,1},{2,18},{18,2},{3,19},{19,3},{4,20},{20... | collective-permute-start | bytes 3932168 | tf_op jit(solution)/shard_map/ppermute | solution.py:24
  266.1 10.2 %collective-permute-start.19 = (bf16[1024,640]{1,0:T(8,128)(2,1)}, bf16[1024,640]{1,0:T(8,128)(2,1)S(1)}, u32[]{:S(2)}, u32[]{:S(2)}) collective-permute-start(bf16[1024,640]{1,0:T(8,128)(2,1)} %collective-permute-done.15.refs_21_.refs_5_), channel_id=1, source_target_pairs={{0,16},{16,0},{1,17},{17,1},{2,18},{18,2},{3,19},{19,3},{4,20},{20... | collective-permute-start | bytes 3932168 | tf_op jit(solution)/shard_map/ppermute | solution.py:24
  268.0 32.6 %collective-permute-start.28 = (bf16[1024,640]{1,0:T(8,128)(2,1)}, bf16[1024,640]{1,0:T(8,128)(2,1)}, u32[]{:S(2)}, u32[]{:S(2)}) collective-permute-start(bf16[1024,640]{1,0:T(8,128)(2,1)} %collective-permute-done.23.refs_28_), channel_id=1, source_target_pairs={{0,16},{16,0},{1,17},{17,1},{2,18},{18,2},{3,19},{19,3},{4,20},{20... | collective-permute-start | bytes 3932168 | tf_op jit(solution)/shard_map/ppermute | solution.py:24
  271.4 29.3 %collective-permute-start.29 = (bf16[1024,640]{1,0:T(8,128)(2,1)}, bf16[1024,640]{1,0:T(8,128)(2,1)}, u32[]{:S(2)}, u32[]{:S(2)}) collective-permute-start(bf16[1024,640]{1,0:T(8,128)(2,1)} %collective-permute-done.25.refs_29_), channel_id=1, source_target_pairs={{0,16},{16,0},{1,17},{17,1},{2,18},{18,2},{3,19},{19,3},{4,20},{20... | collective-permute-start | bytes 3932168 | tf_op jit(solution)/shard_map/ppermute | solution.py:24
  274.3 26.3 %collective-permute-start.9 = (bf16[4,16,8192]{2,1,0:T(8,128)(2,1)}, bf16[4,16,8192]{2,1,0:T(8,128)(2,1)}, u32[]{:S(2)}, u32[]{:S(2)}) collective-permute-start(bf16[4,16,8192]{2,1,0:T(8,128)(2,1)} %collective-permute-done.8.refs_15_), channel_id=1, source_target_pairs={{0,4},{4,8},{8,12},{12,0},{1,5},{5,9},{9,13},{13,1},{2,6},{6,10},{... | collective-permute-start | bytes 3145736 | tf_op jit(solution)/shard_map/ppermute | solution.py:24
  321.5 23.4 %collective-permute-start.42 = (bf16[576,256]{1,0:T(8,128)(2,1)S(1)}, bf16[576,256]{1,0:T(8,128)(2,1)S(1)}, u32[]{:S(2)}, u32[]{:S(2)}) collective-permute-start(bf16[576,256]{1,0:T(8,128)(2,1)S(1)} %get-tuple-element.56), channel_id=1, source_target_pairs={{0,3},{1,0},{2,1},{3,2},{4,7},{5,4},{6,5},{7,6},{8,11},{9,8},{10,9... | collective-permute-start | bytes 884744 | tf_op jit(solution)/shard_map/ppermute | solution.py:24
  340.4 40.7 %collective-permute-start.39 = (bf16[576,512]{1,0:T(8,128)(2,1)S(1)}, bf16[576,512]{1,0:T(8,128)(2,1)S(1)}, u32[]{:S(2)}, u32[]{:S(2)}) collective-permute-start(bf16[576,512]{1,0:T(8,128)(2,1)S(1)} %get-tuple-element.52), channel_id=1, source_target_pairs={{0,3},{1,0},{2,1},{3,2},{4,7},{5,4},{6,5},{7,6},{8,11},{9,8},{10,9... | collective-permute-start | bytes 1769480 | tf_op jit(solution)/shard_map/ppermute | solution.py:24
  340.5 40.6 %collective-permute-start.41 = (bf16[576,512]{1,0:T(8,128)(2,1)S(1)}, bf16[576,512]{1,0:T(8,128)(2,1)S(1)}, u32[]{:S(2)}, u32[]{:S(2)}) collective-permute-start(bf16[576,512]{1,0:T(8,128)(2,1)S(1)} %get-tuple-element.54), channel_id=1, source_target_pairs={{0,1},{1,2},{2,3},{3,0},{4,5},{5,6},{6,7},{7,4},{8,9},{9,10},{10,1... | collective-permute-start | bytes 1769480 | tf_op jit(solution)/shard_map/ppermute | solution.py:24
  341.9 39.1 %collective-permute-start.40 = (bf16[576,512]{1,0:T(8,128)(2,1)S(1)}, bf16[576,512]{1,0:T(8,128)(2,1)S(1)}, u32[]{:S(2)}, u32[]{:S(2)}) collective-permute-start(bf16[576,512]{1,0:T(8,128)(2,1)S(1)} %get-tuple-element.53), channel_id=1, source_target_pairs={{0,2},{1,3},{2,0},{3,1},{4,6},{5,7},{6,4},{7,5},{8,10},{9,11},{10,... | collective-permute-start | bytes 1769480 | tf_op jit(solution)/shard_map/ppermute | solution.py:24
  342.1 31.4 %collective-permute-start.43 = (bf16[576,256]{1,0:T(8,128)(2,1)S(1)}, bf16[576,256]{1,0:T(8,128)(2,1)S(1)}, u32[]{:S(2)}, u32[]{:S(2)}) collective-permute-start(bf16[576,256]{1,0:T(8,128)(2,1)S(1)} %get-tuple-element.57), channel_id=1, source_target_pairs={{0,2},{1,3},{2,0},{3,1},{4,6},{5,7},{6,4},{7,5},{8,10},{9,11},{10,... | collective-permute-start | bytes 884744 | tf_op jit(solution)/shard_map/ppermute | solution.py:24
  344.9 36.2 %collective-permute-start.44 = (bf16[576,256]{1,0:T(8,128)(2,1)S(1)}, bf16[576,256]{1,0:T(8,128)(2,1)S(1)}, u32[]{:S(2)}, u32[]{:S(2)}) collective-permute-start(bf16[576,256]{1,0:T(8,128)(2,1)S(1)} %get-tuple-element.58), channel_id=1, source_target_pairs={{0,1},{1,2},{2,3},{3,0},{4,5},{5,6},{6,7},{7,4},{8,9},{9,10},{10,1... | collective-permute-start | bytes 884744 | tf_op jit(solution)/shard_map/ppermute | solution.py:24
  (13 other events, 193.9 us)
